TPU v7x, 32 devices: a 4x4x1 block of a 4x4x8 slice. The times are simulated.
32 devices in a mesh: dp: 1 (over z), tp: 4 (over y), ctx: 8 (over x, core).
Axes of the slice: x: 4, y: 4, z: 1, core: 2. Of those that a mesh axis runs over, the one named last changes fastest.
The devices are a block of a 4x4x8 slice.
Arguments:
- x_tokens: bfloat16 [2048, 7168], P(('dp', 'ctx'))
- positions: int32 [2048], P(('dp', 'ctx'))
- w_dq: bfloat16 [7168, 1536], replicated
- g_q: bfloat16 [1536], replicated
- w_uq: bfloat16 [1536, 16384], P(None, 'tp')
- w_qr: bfloat16 [1536, 8192], P(None, 'tp')
- w_dkv: bfloat16 [7168, 512], replicated
- g_kv: bfloat16 [512], replicated
- w_kr: bfloat16 [7168, 64], replicated
- w_uk: bfloat16 [512, 16384], P(None, 'tp')
- w_uv: bfloat16 [512, 16384], P(None, 'tp')
- w_o: bfloat16 [16384, 7168], P('tp')
Outputs:
- output: bfloat16 [2048, 7168], P(('dp', 'ctx'))
All inputs are finite; a program needn't handle non-finite values.
Results may differ from a plain program's by a relative error of at most 0.00851559.
Values are sent between devices in bfloat16 or wider.
A program may use at most 768 MiB of HBM per device.

v0:
```python
import jax
import jax.numpy as jnp
from jax import lax
from jax.sharding import PartitionSpec as P

ROPE_BASE = 10000.0
NORM_EPS = 1e-6
NEG_BIG = -1e30


def rms_norm(act_in, gain_vec):
    inv_rms = lax.rsqrt(jnp.mean(act_in * act_in, axis=-1, keepdims=True) + NORM_EPS)
    return act_in * inv_rms * gain_vec.astype(jnp.float32)


def rope_tables(pos_vals, rope_dim):
    half_dim = rope_dim // 2
    inv_freq = ROPE_BASE ** (-jnp.arange(half_dim, dtype=jnp.float32) * 2.0 / rope_dim)
    angles = pos_vals.astype(jnp.float32)[..., None] * inv_freq
    return jnp.cos(angles), jnp.sin(angles)


def apply_rope(act_in, cos_t, sin_t):
    half_dim = act_in.shape[-1] // 2
    first_half = act_in[..., :half_dim]
    second_half = act_in[..., half_dim:]
    return jnp.concatenate([first_half * cos_t - second_half * sin_t, second_half * cos_t + first_half * sin_t], axis=-1)


def project_tokens(tok_x, tok_pos, w_dq, g_q, w_uq, w_qr, w_dkv, g_kv, w_kr, heads_loc):
    rope_dim = w_kr.shape[1]
    tok_count = tok_x.shape[0]
    cos_t, sin_t = rope_tables(tok_pos, rope_dim)
    c_q = rms_norm(jnp.dot(tok_x, w_dq, preferred_element_type=jnp.float32), g_q).astype(jnp.bfloat16)
    q_nope = jnp.dot(c_q, w_uq, preferred_element_type=jnp.float32).astype(jnp.bfloat16).reshape(tok_count, heads_loc, -1)
    q_rot = jnp.dot(c_q, w_qr, preferred_element_type=jnp.float32).reshape(tok_count, heads_loc, rope_dim)
    q_pe = apply_rope(q_rot, cos_t[:, None, :], sin_t[:, None, :]).astype(jnp.bfloat16)
    c_kv = rms_norm(jnp.dot(tok_x, w_dkv, preferred_element_type=jnp.float32), g_kv).astype(jnp.bfloat16)
    k_pe = apply_rope(jnp.dot(tok_x, w_kr, preferred_element_type=jnp.float32), cos_t, sin_t).astype(jnp.bfloat16)
    return q_nope, q_pe, c_kv, k_pe


def up_project(lat_rows, w_uk, w_uv, heads_loc):
    row_count = lat_rows.shape[0]
    k_nope = jnp.dot(lat_rows, w_uk, preferred_element_type=jnp.float32).astype(jnp.bfloat16).reshape(row_count, heads_loc, -1)
    v_rows = jnp.dot(lat_rows, w_uv, preferred_element_type=jnp.float32).astype(jnp.bfloat16).reshape(row_count, heads_loc, -1)
    return k_nope, v_rows


def block_scores(q_nope, q_pe, k_nope, k_pe, score_scale):
    nope_part = jnp.einsum('qhn,khn->hqk', q_nope, k_nope, preferred_element_type=jnp.float32)
    rope_part = jnp.einsum('qhr,kr->hqk', q_pe, k_pe, preferred_element_type=jnp.float32)
    return (nope_part + rope_part) * score_scale


def block_stats(scores, v_rows):
    blk_max = jnp.max(scores, axis=-1)
    prob_tile = jnp.exp(scores - blk_max[..., None])
    blk_sum = jnp.sum(prob_tile, axis=-1)
    blk_acc = jnp.einsum('hqk,khv->hqv', prob_tile.astype(jnp.bfloat16), v_rows, preferred_element_type=jnp.float32)
    return blk_max, blk_sum, blk_acc


def merge_stats(run_state, update):
    old_max, old_sum, old_acc = run_state
    new_max, new_sum, new_acc = update
    top_max = jnp.maximum(old_max, new_max)
    old_w = jnp.exp(old_max - top_max)
    new_w = jnp.exp(new_max - top_max)
    return top_max, old_sum * old_w + new_sum * new_w, old_acc * old_w[..., None] + new_acc * new_w[..., None]


def solution(mesh):
    ctx_count = mesh.shape['ctx']
    next_perm = [(src, (src + 1) % ctx_count) for src in range(ctx_count)]
    tok_spec = P(('dp', 'ctx'), None)
    pos_spec = P(('dp', 'ctx'))
    full_mat = P(None, None)
    full_vec = P(None)
    col_spec = P(None, 'tp')
    row_spec = P('tp', None)

    def local_step(tok_x, tok_pos, w_dq, g_q, w_uq, w_qr, w_dkv, g_kv, w_kr, w_uk, w_uv, w_o):
        my_index = lax.axis_index('ctx')
        half_len = tok_x.shape[0] // 2
        rope_dim = w_kr.shape[1]
        heads_loc = w_qr.shape[1] // rope_dim
        nope_dim = w_uq.shape[1] // heads_loc
        value_dim = w_uv.shape[1] // heads_loc
        score_scale = (nope_dim + rope_dim) ** -0.5
        q_nope, q_pe, c_kv, k_pe = project_tokens(tok_x, tok_pos, w_dq, g_q, w_uq, w_qr, w_dkv, g_kv, w_kr, heads_loc)
        k_nope, v_rows = up_project(c_kv, w_uk, w_uv, heads_loc)
        scores = block_scores(q_nope, q_pe, k_nope, k_pe, score_scale)
        visible = tok_pos[None, :] <= tok_pos[:, None]
        run_state = block_stats(jnp.where(visible[None], scores, NEG_BIG), v_rows)

        def attend_lower(lat_blk, rot_blk, run_state):
            k_low, v_low = up_project(lat_blk[:half_len], w_uk, w_uv, heads_loc)
            update = block_stats(block_scores(q_nope, q_pe, k_low, rot_blk[:half_len], score_scale), v_low)
            return merge_stats(run_state, update)

        def attend_upper(lat_blk, rot_blk, run_state):
            k_both, v_both = up_project(lat_blk, w_uk, w_uv, heads_loc)
            update = block_stats(block_scores(q_nope[half_len:], q_pe[half_len:], k_both, rot_blk, score_scale), v_both)
            old_max, old_sum, old_acc = run_state
            top_max, top_sum, top_acc = merge_stats((old_max[:, half_len:], old_sum[:, half_len:], old_acc[:, half_len:]), update)
            return (jnp.concatenate([old_max[:, :half_len], top_max], axis=1),
                    jnp.concatenate([old_sum[:, :half_len], top_sum], axis=1),
                    jnp.concatenate([old_acc[:, :half_len], top_acc], axis=1))

        def ctx_step(hop_idx, loop_carry):
            lat_blk, rot_blk, run_state = loop_carry
            lat_blk = lax.ppermute(lat_blk, 'ctx', next_perm)
            rot_blk = lax.ppermute(rot_blk, 'ctx', next_perm)
            src_index = (my_index - hop_idx) % ctx_count
            run_state = lax.cond(src_index < my_index, attend_lower, attend_upper, lat_blk, rot_blk, run_state)
            return lat_blk, rot_blk, run_state

        loop_carry = lax.fori_loop(1, ctx_count, ctx_step, (c_kv, k_pe, run_state))
        run_max, run_sum, run_acc = loop_carry[2]
        attn_out = (run_acc / run_sum[..., None]).astype(jnp.bfloat16)
        y_part = jnp.einsum('htv,hvd->td', attn_out, w_o.reshape(heads_loc, value_dim, -1), preferred_element_type=jnp.float32)
        return lax.psum(y_part, 'tp').astype(jnp.bfloat16)

    return jax.shard_map(local_step, mesh=mesh,
                         in_specs=(tok_spec, pos_spec, full_mat, full_vec, col_spec, col_spec, full_mat, full_vec, full_mat, col_spec, col_spec, row_spec),
                         out_specs=tok_spec, check_vma=False)
```

profile of v0, /device:TPU:102, one launch (start us, length us, event | category | flops | bytes accessed | tf_op | source)
XLA Modules:
  0.0 357.0 jit_solution(4057560101591086715)
XLA Ops:
  0.0 11.6 %multiply_reduce_fusion = (f32[256]{0:T(256)S(1)}, f32[256,1536]{1,0:T(8,128)S(1)}) fusion(bf16[256,7168]{1,0:T(8,128)(2,1)} %param.16, bf16[7168,1536]{1,0:T(8,128)(2,1)} %param.18), kind=kOutput, calls=%fused_computation.74 | convolution fusion | flops 5637931008 | bytes 27264000 | tf_op jit(solution)/shard_map/dot_general | solution.py:34
  11.6 5.7 %fusion.53 = f32[256,2048]{0,1:T(8,128)S(1)} fusion(bf16[1536,2048]{1,0:T(8,128)(2,1)} %param.21, f32[256,1536]{1,0:T(8,128)S(1)} %get-tuple-element.416, f32[1536]{0:T(1024)S(1)} %convert_element_type.66, f32[256]{0:T(256)S(1)} %add_rsqrt_fusion), kind=kOutput, calls=%fused_computation.90 | convolution fusion | flops 1611792384 | bytes 9968640 | tf_op jit(solution)/shard_map/dot_general | solution.py:36
  19.2 4.1 %fusion.49 = bf16[32,32,8,128]{3,2,1,0:T(8,128)(2,1)S(1)} fusion(bf16[1536,4096]{1,0:T(8,128)(2,1)S(1)} %copy-done.14, f32[256,1536]{1,0:T(8,128)S(1)} %get-tuple-element.416, f32[1536]{0:T(1024)S(1)} %convert_element_type.66, f32[256]{0:T(256)S(1)} %add_rsqrt_fusion), kind=kOutput, calls=%fused_computation.70 | convolution fusion | flops 3223453696 | bytes 16260096 | tf_op jit(solution)/shard_map/dot_general | solution.py:35
  23.4 5.4 %multiply_reduce_fusion.1 = (f32[256]{0:T(256)S(1)}, f32[256,512]{1,0:T(8,128)S(1)}) fusion(bf16[256,7168]{1,0:T(8,128)(2,1)S(1)} %copy-done.9, bf16[7168,512]{1,0:T(8,128)(2,1)} %param.22), kind=kOutput, calls=%fused_computation.79 | convolution fusion | flops 1879310080 | bytes 11535360 | tf_op jit(solution)/shard_map/dot_general | solution.py:38
  35.1 3.8 %fusion.40 = f32[32,256,128]{2,1,0:T(8,128)} fusion(f32[32,256,256]{1,2,0:T(8,128)S(1)} %get-tuple-element.418, f32[32,256]{1,0:T(8,128)S(1)} %get-tuple-element.501, bf16[32,32,8,128]{3,2,1,0:T(8,128)(2,1)S(1)} %fusion.51), kind=kOutput, calls=%fused_computation.60 | convolution fusion | flops 541065216 | bytes 14712832 | tf_op jit(solution)/shard_map/hqk,khv->hqv/dot_general | solution.py:60
  41.2 154.8 %while.23 = (s32[]{:T(128)}, bf16[256,512]{1,0:T(8,128)(2,1)}, bf16[256,64]{0,1:T(8,128)(2,1)S(1)}, f32[32,256]{1,0:T(8,128)S(1)}, f32[32,256]{1,0:T(8,128)S(1)}...) while((s32[]{:T(128)}, bf16[256,512]{1,0:T(8,128)(2,1)}, ...), condition=%wide.region_11.12_spmd, body=%wide.region_4.11_spmd.sunk | while | flops 2830663680 | bytes 97927776 | solution.py:119
  42.3 5.4 %collective-permute-done.1 = bf16[256,64]{0,1:T(8,128)(2,1)S(1)} collective-permute-done((bf16[256,64]{0,1:T(8,128)(2,1)S(1)}, bf16[256,64]{0,1:T(8,128)(2,1)S(1)}, u32[]{:S(2)}, u32[]{:S(2)}) %collective-permute-start.1) | collective-permute-done | bytes 32800 | tf_op jit(solution)/shard_map/while/body/eval_jaxpr/ppermute | solution.py:114
  47.7 14.7 %conditional.2 = (f32[32,256]{1,0:T(8,128)S(1)}, f32[32,256]{1,0:T(8,128)S(1)}, f32[32,256,128]{2,1,0:T(8,128)}) conditional(s32[]{:T(128)} %convert_element_type.110, (f32[32,256]{1,0:T(8,128)S(1)}, bf16[256,512]{1,0:T(8,128)(2,1)S(1)}, bf16[512,4096]{1,0:T(8,128)(2,1)}, bf16[256,32,128]{2,0,1:T(8,128)(2,1)S(1)}, ...), branch_computations={%region_5.7_spmd, %region_8.10_spmd} | conditional | flops 2830663680 | bytes 96157808 | solution.py:116
  47.7 2.9 fusion.25
  55.7 4.6 %multiply_add_fusion.2 = f32[32,256,128]{2,1,0:T(8,128)S(1)} fusion(f32[32,256,128]{2,1,0:T(8,128)S(1)} %copy-done.3, f32[32,256,128]{1,2,0:T(8,128)S(1)} %get-tuple-element.404, f32[32,256]{1,0:T(8,128)S(1)} %get-tuple-element.395, f32[32,256]{1,0:T(8,128)S(1)} %get-tuple-element.394, f32[32,256]{1,0:T(8,128)S(1)} %get-tuple-element.403, ...), kind=kOutput, calls=%fused_computation.31 | convolution fusion | flops 273678336 | bytes 13729792 | tf_op jit(solution)/shard_map/while/body/eval_jaxpr/cond/branch_1_fun/hqk,khv->hqv/dot_general | solution.py:60
  65.2 4.0 %collective-permute-done.1 = bf16[256,64]{0,1:T(8,128)(2,1)S(1)} collective-permute-done((bf16[256,64]{0,1:T(8,128)(2,1)S(1)}, bf16[256,64]{0,1:T(8,128)(2,1)S(1)}, u32[]{:S(2)}, u32[]{:S(2)}) %collective-permute-start.1) | collective-permute-done | bytes 32800 | tf_op jit(solution)/shard_map/while/body/eval_jaxpr/ppermute | solution.py:114
  69.2 14.7 %conditional.2 = (f32[32,256]{1,0:T(8,128)S(1)}, f32[32,256]{1,0:T(8,128)S(1)}, f32[32,256,128]{2,1,0:T(8,128)}) conditional(s32[]{:T(128)} %convert_element_type.110, (f32[32,256]{1,0:T(8,128)S(1)}, bf16[256,512]{1,0:T(8,128)(2,1)S(1)}, bf16[512,4096]{1,0:T(8,128)(2,1)}, bf16[256,32,128]{2,0,1:T(8,128)(2,1)S(1)}, ...), branch_computations={%region_5.7_spmd, %region_8.10_spmd} | conditional | flops 2830663680 | bytes 96157808 | solution.py:116
  77.2 4.6 %multiply_add_fusion.2 = f32[32,256,128]{2,1,0:T(8,128)S(1)} fusion(f32[32,256,128]{2,1,0:T(8,128)S(1)} %copy-done.3, f32[32,256,128]{1,2,0:T(8,128)S(1)} %get-tuple-element.404, f32[32,256]{1,0:T(8,128)S(1)} %get-tuple-element.395, f32[32,256]{1,0:T(8,128)S(1)} %get-tuple-element.394, f32[32,256]{1,0:T(8,128)S(1)} %get-tuple-element.403, ...), kind=kOutput, calls=%fused_computation.31 | convolution fusion | flops 273678336 | bytes 13729792 | tf_op jit(solution)/shard_map/while/body/eval_jaxpr/cond/branch_1_fun/hqk,khv->hqv/dot_general | solution.py:60
  84.6 3.5 collective-permute-start.1
  90.8 14.7 %conditional.2 = (f32[32,256]{1,0:T(8,128)S(1)}, f32[32,256]{1,0:T(8,128)S(1)}, f32[32,256,128]{2,1,0:T(8,128)}) conditional(s32[]{:T(128)} %convert_element_type.110, (f32[32,256]{1,0:T(8,128)S(1)}, bf16[256,512]{1,0:T(8,128)(2,1)S(1)}, bf16[512,4096]{1,0:T(8,128)(2,1)}, bf16[256,32,128]{2,0,1:T(8,128)(2,1)S(1)}, ...), branch_computations={%region_5.7_spmd, %region_8.10_spmd} | conditional | flops 2830663680 | bytes 96157808 | solution.py:116
  98.8 4.6 %multiply_add_fusion.2 = f32[32,256,128]{2,1,0:T(8,128)S(1)} fusion(f32[32,256,128]{2,1,0:T(8,128)S(1)} %copy-done.3, f32[32,256,128]{1,2,0:T(8,128)S(1)} %get-tuple-element.404, f32[32,256]{1,0:T(8,128)S(1)} %get-tuple-element.395, f32[32,256]{1,0:T(8,128)S(1)} %get-tuple-element.394, f32[32,256]{1,0:T(8,128)S(1)} %get-tuple-element.403, ...), kind=kOutput, calls=%fused_computation.31 | convolution fusion | flops 273678336 | bytes 13729792 | tf_op jit(solution)/shard_map/while/body/eval_jaxpr/cond/branch_1_fun/hqk,khv->hqv/dot_general | solution.py:60
  107.1 3.9 %collective-permute-start.1 = (bf16[256,64]{0,1:T(8,128)(2,1)S(1)}, bf16[256,64]{0,1:T(8,128)(2,1)S(1)}, u32[]{:S(2)}, u32[]{:S(2)}) collective-permute-start(bf16[256,64]{0,1:T(8,128)(2,1)S(1)} %get-tuple-element.515), channel_id=1, source_target_pairs={{0,1},{1,2},{2,3},{3,4},{4,5},{5,6},{6,7},{7,0},{8,9},{9,10},{10,1... | collective-permute-start | bytes 98312 | tf_op jit(solution)/shard_map/while/body/eval_jaxpr/ppermute | solution.py:114
  112.3 14.7 %conditional.2 = (f32[32,256]{1,0:T(8,128)S(1)}, f32[32,256]{1,0:T(8,128)S(1)}, f32[32,256,128]{2,1,0:T(8,128)}) conditional(s32[]{:T(128)} %convert_element_type.110, (f32[32,256]{1,0:T(8,128)S(1)}, bf16[256,512]{1,0:T(8,128)(2,1)S(1)}, bf16[512,4096]{1,0:T(8,128)(2,1)}, bf16[256,32,128]{2,0,1:T(8,128)(2,1)S(1)}, ...), branch_computations={%region_5.7_spmd, %region_8.10_spmd} | conditional | flops 2830663680 | bytes 96157808 | solution.py:116
  120.3 4.6 %multiply_add_fusion.2 = f32[32,256,128]{2,1,0:T(8,128)S(1)} fusion(f32[32,256,128]{2,1,0:T(8,128)S(1)} %copy-done.3, f32[32,256,128]{1,2,0:T(8,128)S(1)} %get-tuple-element.404, f32[32,256]{1,0:T(8,128)S(1)} %get-tuple-element.395, f32[32,256]{1,0:T(8,128)S(1)} %get-tuple-element.394, f32[32,256]{1,0:T(8,128)S(1)} %get-tuple-element.403, ...), kind=kOutput, calls=%fused_computation.31 | convolution fusion | flops 273678336 | bytes 13729792 | tf_op jit(solution)/shard_map/while/body/eval_jaxpr/cond/branch_1_fun/hqk,khv->hqv/dot_general | solution.py:60
  130.0 3.9 %collective-permute-start.1 = (bf16[256,64]{0,1:T(8,128)(2,1)S(1)}, bf16[256,64]{0,1:T(8,128)(2,1)S(1)}, u32[]{:S(2)}, u32[]{:S(2)}) collective-permute-start(bf16[256,64]{0,1:T(8,128)(2,1)S(1)} %get-tuple-element.515), channel_id=1, source_target_pairs={{0,1},{1,2},{2,3},{3,4},{4,5},{5,6},{6,7},{7,0},{8,9},{9,10},{10,1... | collective-permute-start | bytes 98312 | tf_op jit(solution)/shard_map/while/body/eval_jaxpr/ppermute | solution.py:114
  134.7 14.7 %conditional.2 = (f32[32,256]{1,0:T(8,128)S(1)}, f32[32,256]{1,0:T(8,128)S(1)}, f32[32,256,128]{2,1,0:T(8,128)}) conditional(s32[]{:T(128)} %convert_element_type.110, (f32[32,256]{1,0:T(8,128)S(1)}, bf16[256,512]{1,0:T(8,128)(2,1)S(1)}, bf16[512,4096]{1,0:T(8,128)(2,1)}, bf16[256,32,128]{2,0,1:T(8,128)(2,1)S(1)}, ...), branch_computations={%region_5.7_spmd, %region_8.10_spmd} | conditional | flops 2830663680 | bytes 96157808 | solution.py:116
  134.7 2.9 fusion.25
  142.7 4.6 %multiply_add_fusion.2 = f32[32,256,128]{2,1,0:T(8,128)S(1)} fusion(f32[32,256,128]{2,1,0:T(8,128)S(1)} %copy-done.3, f32[32,256,128]{1,2,0:T(8,128)S(1)} %get-tuple-element.404, f32[32,256]{1,0:T(8,128)S(1)} %get-tuple-element.395, f32[32,256]{1,0:T(8,128)S(1)} %get-tuple-element.394, f32[32,256]{1,0:T(8,128)S(1)} %get-tuple-element.403, ...), kind=kOutput, calls=%fused_computation.31 | convolution fusion | flops 273678336 | bytes 13729792 | tf_op jit(solution)/shard_map/while/body/eval_jaxpr/cond/branch_1_fun/hqk,khv->hqv/dot_general | solution.py:60
  152.9 3.9 %collective-permute-start.1 = (bf16[256,64]{0,1:T(8,128)(2,1)S(1)}, bf16[256,64]{0,1:T(8,128)(2,1)S(1)}, u32[]{:S(2)}, u32[]{:S(2)}) collective-permute-start(bf16[256,64]{0,1:T(8,128)(2,1)S(1)} %get-tuple-element.515), channel_id=1, source_target_pairs={{0,1},{1,2},{2,3},{3,4},{4,5},{5,6},{6,7},{7,0},{8,9},{9,10},{10,1... | collective-permute-start | bytes 98312 | tf_op jit(solution)/shard_map/while/body/eval_jaxpr/ppermute | solution.py:114
  157.6 14.7 %conditional.2 = (f32[32,256]{1,0:T(8,128)S(1)}, f32[32,256]{1,0:T(8,128)S(1)}, f32[32,256,128]{2,1,0:T(8,128)}) conditional(s32[]{:T(128)} %convert_element_type.110, (f32[32,256]{1,0:T(8,128)S(1)}, bf16[256,512]{1,0:T(8,128)(2,1)S(1)}, bf16[512,4096]{1,0:T(8,128)(2,1)}, bf16[256,32,128]{2,0,1:T(8,128)(2,1)S(1)}, ...), branch_computations={%region_5.7_spmd, %region_8.10_spmd} | conditional | flops 2830663680 | bytes 96157808 | solution.py:116
  157.6 2.9 fusion.25
  165.6 4.6 %multiply_add_fusion.2 = f32[32,256,128]{2,1,0:T(8,128)S(1)} fusion(f32[32,256,128]{2,1,0:T(8,128)S(1)} %copy-done.3, f32[32,256,128]{1,2,0:T(8,128)S(1)} %get-tuple-element.404, f32[32,256]{1,0:T(8,128)S(1)} %get-tuple-element.395, f32[32,256]{1,0:T(8,128)S(1)} %get-tuple-element.394, f32[32,256]{1,0:T(8,128)S(1)} %get-tuple-element.403, ...), kind=kOutput, calls=%fused_computation.31 | convolution fusion | flops 273678336 | bytes 13729792 | tf_op jit(solution)/shard_map/while/body/eval_jaxpr/cond/branch_1_fun/hqk,khv->hqv/dot_general | solution.py:60
  175.8 3.9 %collective-permute-start.1 = (bf16[256,64]{0,1:T(8,128)(2,1)S(1)}, bf16[256,64]{0,1:T(8,128)(2,1)S(1)}, u32[]{:S(2)}, u32[]{:S(2)}) collective-permute-start(bf16[256,64]{0,1:T(8,128)(2,1)S(1)} %get-tuple-element.515), channel_id=1, source_target_pairs={{0,1},{1,2},{2,3},{3,4},{4,5},{5,6},{6,7},{7,0},{8,9},{9,10},{10,1... | collective-permute-start | bytes 98312 | tf_op jit(solution)/shard_map/while/body/eval_jaxpr/ppermute | solution.py:114
  180.5 14.8 %conditional.2 = (f32[32,256]{1,0:T(8,128)S(1)}, f32[32,256]{1,0:T(8,128)S(1)}, f32[32,256,128]{2,1,0:T(8,128)}) conditional(s32[]{:T(128)} %convert_element_type.110, (f32[32,256]{1,0:T(8,128)S(1)}, bf16[256,512]{1,0:T(8,128)(2,1)S(1)}, bf16[512,4096]{1,0:T(8,128)(2,1)}, bf16[256,32,128]{2,0,1:T(8,128)(2,1)S(1)}, ...), branch_computations={%region_5.7_spmd, %region_8.10_spmd} | conditional | flops 2830663680 | bytes 96157808 | solution.py:116
  180.5 3.5 fusion.10
  196.0 27.8 %convolution_bitcast_fusion = f32[256,7168]{1,0:T(8,128)} fusion(bf16[32,128,7168]{2,1,0:T(8,128)(2,1)} %bitcast.98, f32[32,256,128]{2,1,0:T(8,128)} %get-tuple-element.343, f32[32,256]{1,0:T(8,128)S(1)} %get-tuple-element.344), kind=kOutput, calls=%fused_computation.50 | convolution fusion | flops 15034482688 | bytes 70287360 | tf_op jit(solution)/shard_map/htv,hvd->td/dot_general | solution.py:122
  223.8 133.1 %all-reduce.1 = bf16[256,7168]{1,0:T(8,128)(2,1)} all-reduce(f32[256,7168]{1,0:T(8,128)} %convolution_bitcast_fusion), channel_id=1, replica_groups=mesh['dp'=1,'tp'=4,'ctx'=8] {'tp'}, use_global_device_ids=true, to_apply=%region_12.13 | all-reduce | flops 1835008 | bytes 11010048 | tf_op jit(solution)/shard_map/psum | solution.py:123
  (156 shorter events, 96.7 us)
Async XLA Ops:
  0.0 17.4 %copy-start = (bf16[7168,64]{0,1:T(8,128)(2,1)S(1)}, bf16[7168,64]{0,1:T(8,128)(2,1)}, u32[]{:S(2)}) copy-start(bf16[7168,64]{0,1:T(8,128)(2,1)} %param.24) | copy-start | bytes 2752516
  0.0 11.6 %copy-start.12 = (bf16[1536]{0:T(1024)(128)(2,1)S(1)}, bf16[1536]{0:T(1024)(128)(2,1)}, u32[]{:S(2)}) copy-start(bf16[1536]{0:T(1024)(128)(2,1)} %param.19) | copy-start | bytes 9220
  0.0 19.2 %copy-start.14 = (bf16[1536,4096]{1,0:T(8,128)(2,1)S(1)}, bf16[1536,4096]{1,0:T(8,128)(2,1)}, u32[]{:S(2)}) copy-start(bf16[1536,4096]{1,0:T(8,128)(2,1)} %param.20) | copy-start | bytes 37748740
  11.6 5.8 %copy-start.9 = (bf16[256,7168]{1,0:T(8,128)(2,1)S(1)}, bf16[256,7168]{1,0:T(8,128)(2,1)}, u32[]{:S(2)}) copy-start(bf16[256,7168]{1,0:T(8,128)(2,1)} %param.16) | copy-start | bytes 11010052
  23.3 5.4 %copy-start.13 = (bf16[512]{0:T(512)(128)(2,1)S(1)}, bf16[512]{0:T(512)(128)(2,1)}, u32[]{:S(2)}) copy-start(bf16[512]{0:T(512)(128)(2,1)} %param.23) | copy-start | bytes 3076
  23.4 5.5 %copy-start.5 = (bf16[512,4096]{1,0:T(8,128)(2,1)S(1)}, bf16[512,4096]{1,0:T(8,128)(2,1)}, u32[]{:S(2)}) copy-start(bf16[512,4096]{1,0:T(8,128)(2,1)} %param.25) | copy-start | bytes 12582916
  28.9 4.7 %copy-start.10 = (bf16[256,512]{1,0:T(8,128)(2,1)}, bf16[256,512]{1,0:T(8,128)(2,1)S(1)}, u32[]{:S(2)}) copy-start(bf16[256,512]{1,0:T(8,128)(2,1)S(1)} %multiply_convert_fusion.1) | copy-start | bytes 786436
  31.6 2.2 copy-start.6
  41.5 6.2 %collective-permute-start = (bf16[256,512]{1,0:T(8,128)(2,1)}, bf16[256,512]{1,0:T(8,128)(2,1)S(1)}, u32[]{:S(2)}, u32[]{:S(2)}) collective-permute-start(bf16[256,512]{1,0:T(8,128)(2,1)} %get-tuple-element.514), channel_id=1, source_target_pairs={{0,1},{1,2},{2,3},{3,4},{4,5},{5,6},{6,7},{7,0},{8,9},{9,10},{10,1... | collective-permute-start | bytes 786440 | tf_op jit(solution)/shard_map/while/body/eval_jaxpr/ppermute | solution.py:113
  41.5 6.1 %collective-permute-start.1 = (bf16[256,64]{0,1:T(8,128)(2,1)S(1)}, bf16[256,64]{0,1:T(8,128)(2,1)S(1)}, u32[]{:S(2)}, u32[]{:S(2)}) collective-permute-start(bf16[256,64]{0,1:T(8,128)(2,1)S(1)} %get-tuple-element.515), channel_id=1, source_target_pairs={{0,1},{1,2},{2,3},{3,4},{4,5},{5,6},{6,7},{7,0},{8,9},{9,10},{10,1... | collective-permute-start | bytes 98312 | tf_op jit(solution)/shard_map/while/body/eval_jaxpr/ppermute | solution.py:114
  52.2 2.2 copy-start.8
  52.2 3.5 copy-start.3
  63.1 6.2 %collective-permute-start = (bf16[256,512]{1,0:T(8,128)(2,1)}, bf16[256,512]{1,0:T(8,128)(2,1)S(1)}, u32[]{:S(2)}, u32[]{:S(2)}) collective-permute-start(bf16[256,512]{1,0:T(8,128)(2,1)} %get-tuple-element.514), channel_id=1, source_target_pairs={{0,1},{1,2},{2,3},{3,4},{4,5},{5,6},{6,7},{7,0},{8,9},{9,10},{10,1... | collective-permute-start | bytes 786440 | tf_op jit(solution)/shard_map/while/body/eval_jaxpr/ppermute | solution.py:113
  63.1 6.1 %collective-permute-start.1 = (bf16[256,64]{0,1:T(8,128)(2,1)S(1)}, bf16[256,64]{0,1:T(8,128)(2,1)S(1)}, u32[]{:S(2)}, u32[]{:S(2)}) collective-permute-start(bf16[256,64]{0,1:T(8,128)(2,1)S(1)} %get-tuple-element.515), channel_id=1, source_target_pairs={{0,1},{1,2},{2,3},{3,4},{4,5},{5,6},{6,7},{7,0},{8,9},{9,10},{10,1... | collective-permute-start | bytes 98312 | tf_op jit(solution)/shard_map/while/body/eval_jaxpr/ppermute | solution.py:114
  73.8 2.2 copy-start.8
  73.8 3.5 copy-start.3
  84.6 6.2 %collective-permute-start = (bf16[256,512]{1,0:T(8,128)(2,1)}, bf16[256,512]{1,0:T(8,128)(2,1)S(1)}, u32[]{:S(2)}, u32[]{:S(2)}) collective-permute-start(bf16[256,512]{1,0:T(8,128)(2,1)} %get-tuple-element.514), channel_id=1, source_target_pairs={{0,1},{1,2},{2,3},{3,4},{4,5},{5,6},{6,7},{7,0},{8,9},{9,10},{10,1... | collective-permute-start | bytes 786440 | tf_op jit(solution)/shard_map/while/body/eval_jaxpr/ppermute | solution.py:113
  84.6 6.1 %collective-permute-start.1 = (bf16[256,64]{0,1:T(8,128)(2,1)S(1)}, bf16[256,64]{0,1:T(8,128)(2,1)S(1)}, u32[]{:S(2)}, u32[]{:S(2)}) collective-permute-start(bf16[256,64]{0,1:T(8,128)(2,1)S(1)} %get-tuple-element.515), channel_id=1, source_target_pairs={{0,1},{1,2},{2,3},{3,4},{4,5},{5,6},{6,7},{7,0},{8,9},{9,10},{10,1... | collective-permute-start | bytes 98312 | tf_op jit(solution)/shard_map/while/body/eval_jaxpr/ppermute | solution.py:114
  95.3 2.2 copy-start.8
  95.3 3.5 copy-start.3
  106.1 6.2 %collective-permute-start = (bf16[256,512]{1,0:T(8,128)(2,1)}, bf16[256,512]{1,0:T(8,128)(2,1)S(1)}, u32[]{:S(2)}, u32[]{:S(2)}) collective-permute-start(bf16[256,512]{1,0:T(8,128)(2,1)} %get-tuple-element.514), channel_id=1, source_target_pairs={{0,1},{1,2},{2,3},{3,4},{4,5},{5,6},{6,7},{7,0},{8,9},{9,10},{10,1... | collective-permute-start | bytes 786440 | tf_op jit(solution)/shard_map/while/body/eval_jaxpr/ppermute | solution.py:113
  107.1 5.2 %collective-permute-start.1 = (bf16[256,64]{0,1:T(8,128)(2,1)S(1)}, bf16[256,64]{0,1:T(8,128)(2,1)S(1)}, u32[]{:S(2)}, u32[]{:S(2)}) collective-permute-start(bf16[256,64]{0,1:T(8,128)(2,1)S(1)} %get-tuple-element.515), channel_id=1, source_target_pairs={{0,1},{1,2},{2,3},{3,4},{4,5},{5,6},{6,7},{7,0},{8,9},{9,10},{10,1... | collective-permute-start | bytes 98312 | tf_op jit(solution)/shard_map/while/body/eval_jaxpr/ppermute | solution.py:114
  116.9 3.5 copy-start.3
  127.7 7.0 %collective-permute-start = (bf16[256,512]{1,0:T(8,128)(2,1)}, bf16[256,512]{1,0:T(8,128)(2,1)S(1)}, u32[]{:S(2)}, u32[]{:S(2)}) collective-permute-start(bf16[256,512]{1,0:T(8,128)(2,1)} %get-tuple-element.514), channel_id=1, source_target_pairs={{0,1},{1,2},{2,3},{3,4},{4,5},{5,6},{6,7},{7,0},{8,9},{9,10},{10,1... | collective-permute-start | bytes 786440 | tf_op jit(solution)/shard_map/while/body/eval_jaxpr/ppermute | solution.py:113
  130.0 4.7 %collective-permute-start.1 = (bf16[256,64]{0,1:T(8,128)(2,1)S(1)}, bf16[256,64]{0,1:T(8,128)(2,1)S(1)}, u32[]{:S(2)}, u32[]{:S(2)}) collective-permute-start(bf16[256,64]{0,1:T(8,128)(2,1)S(1)} %get-tuple-element.515), channel_id=1, source_target_pairs={{0,1},{1,2},{2,3},{3,4},{4,5},{5,6},{6,7},{7,0},{8,9},{9,10},{10,1... | collective-permute-start | bytes 98312 | tf_op jit(solution)/shard_map/while/body/eval_jaxpr/ppermute | solution.py:114
  139.3 3.5 copy-start.3
  150.1 7.5 %collective-permute-start = (bf16[256,512]{1,0:T(8,128)(2,1)}, bf16[256,512]{1,0:T(8,128)(2,1)S(1)}, u32[]{:S(2)}, u32[]{:S(2)}) collective-permute-start(bf16[256,512]{1,0:T(8,128)(2,1)} %get-tuple-element.514), channel_id=1, source_target_pairs={{0,1},{1,2},{2,3},{3,4},{4,5},{5,6},{6,7},{7,0},{8,9},{9,10},{10,1... | collective-permute-start | bytes 786440 | tf_op jit(solution)/shard_map/while/body/eval_jaxpr/ppermute | solution.py:113
  152.9 4.7 %collective-permute-start.1 = (bf16[256,64]{0,1:T(8,128)(2,1)S(1)}, bf16[256,64]{0,1:T(8,128)(2,1)S(1)}, u32[]{:S(2)}, u32[]{:S(2)}) collective-permute-start(bf16[256,64]{0,1:T(8,128)(2,1)S(1)} %get-tuple-element.515), channel_id=1, source_target_pairs={{0,1},{1,2},{2,3},{3,4},{4,5},{5,6},{6,7},{7,0},{8,9},{9,10},{10,1... | collective-permute-start | bytes 98312 | tf_op jit(solution)/shard_map/while/body/eval_jaxpr/ppermute | solution.py:114
  162.2 3.5 copy-start.3
  173.0 7.5 %collective-permute-start = (bf16[256,512]{1,0:T(8,128)(2,1)}, bf16[256,512]{1,0:T(8,128)(2,1)S(1)}, u32[]{:S(2)}, u32[]{:S(2)}) collective-permute-start(bf16[256,512]{1,0:T(8,128)(2,1)} %get-tuple-element.514), channel_id=1, source_target_pairs={{0,1},{1,2},{2,3},{3,4},{4,5},{5,6},{6,7},{7,0},{8,9},{9,10},{10,1... | collective-permute-start | bytes 786440 | tf_op jit(solution)/shard_map/while/body/eval_jaxpr/ppermute | solution.py:113
  175.8 4.7 %collective-permute-start.1 = (bf16[256,64]{0,1:T(8,128)(2,1)S(1)}, bf16[256,64]{0,1:T(8,128)(2,1)S(1)}, u32[]{:S(2)}, u32[]{:S(2)}) collective-permute-start(bf16[256,64]{0,1:T(8,128)(2,1)S(1)} %get-tuple-element.515), channel_id=1, source_target_pairs={{0,1},{1,2},{2,3},{3,4},{4,5},{5,6},{6,7},{7,0},{8,9},{9,10},{10,1... | collective-permute-start | bytes 98312 | tf_op jit(solution)/shard_map/while/body/eval_jaxpr/ppermute | solution.py:114
  196.0 160.9 %copy-start.1 = (bf16[7168,64]{0,1:T(8,128)(2,1)S(1)}, bf16[7168,64]{0,1:T(8,128)(2,1)}, u32[]{:S(2)}) copy-start(bf16[7168,64]{0,1:T(8,128)(2,1)} %param.24) | copy-start | bytes 2752516
  (12 other events, 24.7 us)
where the time goes:
time: 359 us; the launch traced here: 357 us
  matrix products  134 us (37%)
  blocking collectives  133 us (37%)
  local copies, waits for them, and re-layouts  31.4 us (9%)
  starting transfers between devices  30.7 us (9%)
  waiting for transfers between devices  16 us (4%)
  other arithmetic  11.1 us (3%)
    psum x1, blocking collectives, local_step(): return lax.psum(y_part, 'tp').astype(jnp.bfloat16)  133 us
    dot_general x8, matrix products, block_stats(): jnp.einsum('hqk,khv->hqv', prob_tile.astype(jnp.bfloat16), v_rows, prefer...  33.9 us
    dot_general x1, matrix products, local_step(): jnp.einsum('htv,hvd->td', attn_out, w_o.reshape(heads_loc, value_dim, -1)...  27.8 us
    cond x40, local copies, waits for them, and re-layouts  25.5 us
    dot_general x8, matrix products, up_project(): jnp.dot(lat_rows, w_uk, preferred_element_type=jnp.float32)  22.3 us
    ppermute x7, starting transfers between devices, ctx_step(): rot_blk = lax.ppermute(rot_blk, 'ctx', next_perm)  21.7 us
    ppermute x7, waiting for transfers between devices, ctx_step(): rot_blk = lax.ppermute(rot_blk, 'ctx', next_perm)  16 us
    dot_general x1, matrix products, project_tokens(): jnp.dot(tok_x, w_dq, preferred_element_type=jnp.float32)  11.6 us
  transfers between devices with their start and end apart: 14, of which 7 were waited for; matrix products, arithmetic and copies ran while one was open for 0% of the time, Pallas kernels for 0%

commit v1 on v0

--- a/solution.py
+++ b/solution.py
@@ -1,6 +1,10 @@
+import functools
+
 import jax
 import jax.numpy as jnp
 from jax import lax
+from jax.experimental import pallas as pl
+from jax.experimental.pallas import tpu as pltpu
 from jax.sharding import PartitionSpec as P
 
 ROPE_BASE = 10000.0
@@ -68,6 +72,154 @@
     old_w = jnp.exp(old_max - top_max)
     new_w = jnp.exp(new_max - top_max)
     return top_max, old_sum * old_w + new_sum * new_w, old_acc * old_w[..., None] + new_acc * new_w[..., None]
+
+
+MESH = pl.DeviceIdType.MESH
+OUT_BLOCK = 512
+W_SLOTS = 3
+
+
+def out_kernel(n_tp, n_blk, o_ref, w_hbm, out_hbm, wbuf, part, recv, ybuf, w_sem, rs_send, rs_recv, ag_send, ag_recv, out_sem):
+    me = lax.axis_index('tp')
+    right = lax.rem(me + 1, n_tp)
+    left = lax.rem(me + n_tp - 1, n_tp)
+    peer = (right, left)
+    step_of = (n_tp - 1, 1)
+    blk = wbuf.shape[2]
+    rows = part.shape[2]
+    n_pair = n_blk // 2
+
+    def w_copy(b):
+        return pltpu.make_async_copy(w_hbm.at[:, pl.ds(pl.multiple_of(b * blk, blk), blk)], wbuf.at[lax.rem(b, W_SLOTS)], w_sem.at[lax.rem(b, W_SLOTS)])
+
+    def chunk_at(way, hop):
+        return lax.rem(me + (hop + 1) * step_of[way], n_tp)
+
+    def rs_copy(b, way, hop):
+        src = part.at[b, chunk_at(way, 0)] if hop == 0 else recv.at[b, hop - 1]
+        return pltpu.make_async_remote_copy(src_ref=src, dst_ref=recv.at[b, hop], send_sem=rs_send.at[b, hop], recv_sem=rs_recv.at[b, hop],
+                                            device_id={'tp': peer[way]}, device_id_type=MESH)
+
+    def ag_copy(b, slot, way, chunk):
+        return pltpu.make_async_remote_copy(src_ref=ybuf.at[chunk, b], dst_ref=ybuf.at[chunk, b], send_sem=ag_send.at[b, slot], recv_sem=ag_recv.at[b, slot],
+                                            device_id={'tp': peer[way]}, device_id_type=MESH)
+
+    def out_copy(b, chunk):
+        return pltpu.make_async_copy(ybuf.at[chunk, b], out_hbm.at[pl.ds(pl.multiple_of(chunk * rows, rows), rows), pl.ds(pl.multiple_of(b * blk, blk), blk)],
+                                     out_sem.at[chunk, b])
+
+    for b in range(W_SLOTS):
+        w_copy(b).start()
+    barrier = pltpu.get_barrier_semaphore()
+    for neighbour in peer:
+        pl.semaphore_signal(barrier, inc=1, device_id={'tp': neighbour}, device_id_type=MESH)
+    pl.semaphore_wait(barrier, 2)
+
+    def product(p, _):
+        for way in range(2):
+            b = 2 * p + way
+            w_copy(b).wait()
+            res = jnp.dot(o_ref[...], wbuf[lax.rem(b, W_SLOTS)], preferred_element_type=jnp.float32)
+            part[b] = res.reshape(n_tp, rows, blk)
+
+            @pl.when(b + W_SLOTS < n_blk)
+            def _():
+                w_copy(b + W_SLOTS).start()
+
+            rs_copy(b, way, 0).start()
+        return 0
+
+    lax.fori_loop(0, n_pair, product, 0)
+
+    for hop in range(1, n_tp - 1):
+        def forward(p, _):
+            for way in range(2):
+                b = 2 * p + way
+                rs_copy(b, way, hop - 1).wait_recv()
+                recv[b, hop - 1] = recv[b, hop - 1] + part[b, chunk_at(way, hop)]
+            for way in range(2):
+                rs_copy(2 * p + way, way, hop).start()
+            return 0
+
+        lax.fori_loop(0, n_pair, forward, 0)
+
+    def relay(p):
+        ag_copy(2 * p, 0, 0, left).wait_recv()
+        ag_copy(2 * p, 2, 0, left).start()
+        ag_copy(2 * p + 1, 1, 1, right).wait_recv()
+        ag_copy(2 * p + 1, 2, 1, right).start()
+        out_copy(2 * p, left).start()
+        out_copy(2 * p + 1, right).start()
+
+    def finish(p, _):
+        for way in range(2):
+            b = 2 * p + way
+            rs_copy(b, way, n_tp - 2).wait_recv()
+            ybuf[me, b] = (recv[b, n_tp - 2] + part[b, me]).astype(ybuf.dtype)
+        for way in range(2):
+            b = 2 * p + way
+            ag_copy(b, 0, 0, me).start()
+            ag_copy(b, 1, 1, me).start()
+            out_copy(b, me).start()
+
+        @pl.when(p > 0)
+        def _():
+            relay(p - 1)
+        return 0
+
+    lax.fori_loop(0, n_pair, finish, 0)
+    relay(n_pair - 1)
+
+    def drain(p, _):
+        ag_copy(2 * p, 1, 1, right).wait_recv()
+        out_copy(2 * p, right).start()
+        ag_copy(2 * p + 1, 0, 0, left).wait_recv()
+        out_copy(2 * p + 1, left).start()
+        for way in range(2):
+            b = 2 * p + way
+            ag_copy(b, 2, way, lax.rem(me + 2, n_tp)).wait_recv()
+            out_copy(b, lax.rem(me + 2, n_tp)).start()
+        return 0
+
+    lax.fori_loop(0, n_pair, drain, 0)
+
+    def settle(p, _):
+        for way in range(2):
+            b = 2 * p + way
+            for hop in range(n_tp - 1):
+                rs_copy(b, way, hop).wait_send()
+            ag_copy(b, 0, 0, me).wait_send()
+            ag_copy(b, 1, 1, me).wait_send()
+            ag_copy(b, 2, way, left if way == 0 else right).wait_send()
+            for chunk in range(n_tp):
+                out_copy(b, chunk).wait()
+        return 0
+
+    lax.fori_loop(0, n_pair, settle, 0)
+
+
+def project_out(attn_out, w_o, n_tp):
+    tok_count, depth = attn_out.shape
+    width = w_o.shape[1]
+    n_blk = width // OUT_BLOCK
+    assert n_tp == 4 and n_blk % 2 == 0 and width % OUT_BLOCK == 0
+    rows = tok_count // n_tp
+    dma = pltpu.SemaphoreType.DMA
+    return pl.pallas_call(
+        functools.partial(out_kernel, n_tp, n_blk),
+        out_shape=jax.ShapeDtypeStruct((tok_count, width), jnp.bfloat16),
+        in_specs=[pl.BlockSpec(memory_space=pltpu.VMEM), pl.BlockSpec(memory_space=pl.ANY)],
+        out_specs=pl.BlockSpec(memory_space=pl.ANY),
+        scratch_shapes=[
+            pltpu.VMEM((W_SLOTS, depth, OUT_BLOCK), jnp.bfloat16),
+            pltpu.VMEM((n_blk, n_tp, rows, OUT_BLOCK), jnp.float32),
+            pltpu.VMEM((n_blk, n_tp - 1, rows, OUT_BLOCK), jnp.float32),
+            pltpu.VMEM((n_tp, n_blk, rows, OUT_BLOCK), jnp.bfloat16),
+            dma((W_SLOTS,)), dma((n_blk, n_tp - 1)), dma((n_blk, n_tp - 1)), dma((n_blk, 3)), dma((n_blk, 3)), dma((n_tp, n_blk)),
+        ],
+        compiler_params=pltpu.CompilerParams(collective_id=1, has_side_effects=True, vmem_limit_bytes=60 * 1024 * 1024),
+        name='out_proj',
+    )(attn_out, w_o)
 
 
 def solution(mesh):
@@ -119,8 +271,8 @@
         loop_carry = lax.fori_loop(1, ctx_count, ctx_step, (c_kv, k_pe, run_state))
         run_max, run_sum, run_acc = loop_carry[2]
         attn_out = (run_acc / run_sum[..., None]).astype(jnp.bfloat16)
-        y_part = jnp.einsum('htv,hvd->td', attn_out, w_o.reshape(heads_loc, value_dim, -1), preferred_element_type=jnp.float32)
-        return lax.psum(y_part, 'tp').astype(jnp.bfloat16)
+        attn_out = jnp.transpose(attn_out, (1, 0, 2)).reshape(tok_x.shape[0], -1)
+        return project_out(attn_out, w_o, mesh.shape['tp'])
 
     return jax.shard_map(local_step, mesh=mesh,
                          in_specs=(tok_spec, pos_spec, full_mat, full_vec, col_spec, col_spec, full_mat, full_vec, full_mat, col_spec, col_spec, row_spec),

time: 359 us -> 306 us (0.85)
  blocking collectives: 133 us -> 0 us
  Pallas kernels: 0 us -> 102 us
  matrix products: 134 us -> 103 us
  other arithmetic: 11.1 us -> 14.8 us
    psum x1 -> x0, blocking collectives: 133 us -> none  [local_step(): return lax.psum(y_part, 'tp').astype(jnp.bfloat16)]
    pallas_call x0 -> x1, Pallas kernels: none -> 102 us  [project_out(): pl.pallas_call(functools.partial(out_kernel, n_tp, n_blk), out_shape=jax....]
    dot_general x1 -> x0, matrix products: 27.8 us -> none  [local_step(): jnp.einsum('htv,hvd->td', attn_out, w_o.reshape(heads_loc, value_dim, -1)...]
    unnamed x20 -> x23, local copies, waits for them, and re-layouts: 0.23 us -> 4.33 us
    reshape x0 -> x1, other arithmetic: none -> 3.81 us  [local_step(): attn_out = jnp.transpose(attn_out, (1, 0, 2)).reshape(tok_x.shape[0], -1)]
where the time goes in v1:
time: 306 us; the launch traced here: 301 us
  matrix products  103 us (34%)
  Pallas kernels  102 us (33%)
  local copies, waits for them, and re-layouts  34.6 us (11%)
  starting transfers between devices  30.6 us (10%)
  waiting for transfers between devices  16 us (5%)
  other arithmetic  14.8 us (5%)
    pallas_call x1, Pallas kernels, project_out(): pl.pallas_call(functools.partial(out_kernel, n_tp, n_blk), out_shape=jax....  102 us
    dot_general x8, matrix products, block_stats(): jnp.einsum('hqk,khv->hqv', prob_tile.astype(jnp.bfloat16), v_rows, prefer...  33.8 us
    cond x40, local copies, waits for them, and re-layouts  24.6 us
    dot_general x8, matrix products, up_project(): jnp.dot(lat_rows, w_uk, preferred_element_type=jnp.float32)  22.3 us
    ppermute x7, starting transfers between devices, ctx_step(): rot_blk = lax.ppermute(rot_blk, 'ctx', next_perm)  21.7 us
    ppermute x7, waiting for transfers between devices, ctx_step(): rot_blk = lax.ppermute(rot_blk, 'ctx', next_perm)  16 us
    dot_general x1, matrix products, project_tokens(): jnp.dot(tok_x, w_dq, preferred_element_type=jnp.float32)  11.6 us
    ppermute x7, starting transfers between devices, ctx_step(): lat_blk = lax.ppermute(lat_blk, 'ctx', next_perm)  8.89 us
  transfers between devices with their start and end apart: 14, of which 7 were waited for; matrix products, arithmetic and copies ran while one was open for 0% of the time, Pallas kernels for 0%

profile of v1, /device:TPU:102, one launch (start us, length us, event | category | flops | bytes accessed | tf_op | source)
XLA Modules:
  0.0 301.4 jit_solution(7192853930990099676)
XLA Ops:
  0.0 11.6 %multiply_reduce_fusion = (f32[256]{0:T(256)S(1)}, f32[256,1536]{1,0:T(8,128)S(1)}) fusion(bf16[256,7168]{1,0:T(8,128)(2,1)} %param.16, bf16[7168,1536]{1,0:T(8,128)(2,1)} %param.18), kind=kOutput, calls=%fused_computation.74 | convolution fusion | flops 5637931008 | bytes 27264000 | tf_op jit(solution)/shard_map/dot_general | solution.py:38
  16.3 3.9 %fusion.49 = bf16[32,32,8,128]{3,2,1,0:T(8,128)(2,1)S(1)} fusion(bf16[1536,4096]{1,0:T(8,128)(2,1)S(1)} %copy-done.14, f32[256,1536]{1,0:T(8,128)S(1)} %get-tuple-element.416, f32[1536]{0:T(1024)S(1)} %convert_element_type.63, f32[256]{0:T(256)S(1)} %add_rsqrt_fusion), kind=kOutput, calls=%fused_computation.70 | convolution fusion | flops 3223453696 | bytes 16260096 | tf_op jit(solution)/shard_map/dot_general | solution.py:39
  20.3 5.4 %multiply_reduce_fusion.1 = (f32[256]{0:T(256)S(1)}, f32[256,512]{1,0:T(8,128)S(1)}) fusion(bf16[256,7168]{1,0:T(8,128)(2,1)S(1)} %copy-done.9, bf16[7168,512]{1,0:T(8,128)(2,1)} %param.22), kind=kOutput, calls=%fused_computation.79 | convolution fusion | flops 1879310080 | bytes 11535360 | tf_op jit(solution)/shard_map/dot_general | solution.py:42
  32.0 3.6 %fusion.40 = f32[32,256,128]{2,1,0:T(8,128)} fusion(f32[32,256,256]{1,2,0:T(8,128)S(1)} %get-tuple-element.418, f32[32,256]{1,0:T(8,128)S(1)} %get-tuple-element.501, bf16[32,32,8,128]{3,2,1,0:T(8,128)(2,1)S(1)} %fusion.51), kind=kOutput, calls=%fused_computation.59 | convolution fusion | flops 541065216 | bytes 14712832 | tf_op jit(solution)/shard_map/hqk,khv->hqv/dot_general | solution.py:64
  38.0 153.7 %while.23 = (s32[]{:T(128)}, bf16[256,512]{1,0:T(8,128)(2,1)}, bf16[256,64]{0,1:T(8,128)(2,1)S(1)}, f32[32,256]{1,0:T(8,128)S(1)}, f32[32,256]{1,0:T(8,128)S(1)}...) while((s32[]{:T(128)}, bf16[256,512]{1,0:T(8,128)(2,1)}, ...), condition=%wide.region_11.12_spmd, body=%wide.region_4.11_spmd.sunk | while | flops 2830663680 | bytes 97927776 | solution.py:271
  39.1 5.4 %collective-permute-done.1 = bf16[256,64]{0,1:T(8,128)(2,1)S(1)} collective-permute-done((bf16[256,64]{0,1:T(8,128)(2,1)S(1)}, bf16[256,64]{0,1:T(8,128)(2,1)S(1)}, u32[]{:S(2)}, u32[]{:S(2)}) %collective-permute-start.1) | collective-permute-done | bytes 32800 | tf_op jit(solution)/shard_map/while/body/eval_jaxpr/ppermute | solution.py:266
  44.5 14.5 %conditional.2 = (f32[32,256]{1,0:T(8,128)S(1)}, f32[32,256]{1,0:T(8,128)S(1)}, f32[32,256,128]{2,1,0:T(8,128)}) conditional(s32[]{:T(128)} %convert_element_type.108, (f32[32,256]{1,0:T(8,128)S(1)}, bf16[256,512]{1,0:T(8,128)(2,1)S(1)}, bf16[512,4096]{1,0:T(8,128)(2,1)}, bf16[256,32,128]{2,0,1:T(8,128)(2,1)S(1)}, ...), branch_computations={%region_5.7_spmd, %region_8.10_spmd} | conditional | flops 2830663680 | bytes 96157808 | solution.py:268
  52.5 4.6 %multiply_add_fusion.2 = f32[32,256,128]{2,1,0:T(8,128)S(1)} fusion(f32[32,256,128]{2,1,0:T(8,128)S(1)} %copy-done.3, f32[32,256,128]{1,2,0:T(8,128)S(1)} %get-tuple-element.404, f32[32,256]{1,0:T(8,128)S(1)} %get-tuple-element.395, f32[32,256]{1,0:T(8,128)S(1)} %get-tuple-element.394, f32[32,256]{1,0:T(8,128)S(1)} %get-tuple-element.403, ...), kind=kOutput, calls=%fused_computation.31 | convolution fusion | flops 273678336 | bytes 13729792 | tf_op jit(solution)/shard_map/while/body/eval_jaxpr/cond/branch_1_fun/hqk,khv->hqv/dot_general | solution.py:64
  61.8 4.0 %collective-permute-done.1 = bf16[256,64]{0,1:T(8,128)(2,1)S(1)} collective-permute-done((bf16[256,64]{0,1:T(8,128)(2,1)S(1)}, bf16[256,64]{0,1:T(8,128)(2,1)S(1)}, u32[]{:S(2)}, u32[]{:S(2)}) %collective-permute-start.1) | collective-permute-done | bytes 32800 | tf_op jit(solution)/shard_map/while/body/eval_jaxpr/ppermute | solution.py:266
  65.8 14.5 %conditional.2 = (f32[32,256]{1,0:T(8,128)S(1)}, f32[32,256]{1,0:T(8,128)S(1)}, f32[32,256,128]{2,1,0:T(8,128)}) conditional(s32[]{:T(128)} %convert_element_type.108, (f32[32,256]{1,0:T(8,128)S(1)}, bf16[256,512]{1,0:T(8,128)(2,1)S(1)}, bf16[512,4096]{1,0:T(8,128)(2,1)}, bf16[256,32,128]{2,0,1:T(8,128)(2,1)S(1)}, ...), branch_computations={%region_5.7_spmd, %region_8.10_spmd} | conditional | flops 2830663680 | bytes 96157808 | solution.py:268
  65.8 2.9 fusion.25
  73.9 4.6 %multiply_add_fusion.2 = f32[32,256,128]{2,1,0:T(8,128)S(1)} fusion(f32[32,256,128]{2,1,0:T(8,128)S(1)} %copy-done.3, f32[32,256,128]{1,2,0:T(8,128)S(1)} %get-tuple-element.404, f32[32,256]{1,0:T(8,128)S(1)} %get-tuple-element.395, f32[32,256]{1,0:T(8,128)S(1)} %get-tuple-element.394, f32[32,256]{1,0:T(8,128)S(1)} %get-tuple-element.403, ...), kind=kOutput, calls=%fused_computation.31 | convolution fusion | flops 273678336 | bytes 13729792 | tf_op jit(solution)/shard_map/while/body/eval_jaxpr/cond/branch_1_fun/hqk,khv->hqv/dot_general | solution.py:64
  81.1 3.5 %collective-permute-start.1 = (bf16[256,64]{0,1:T(8,128)(2,1)S(1)}, bf16[256,64]{0,1:T(8,128)(2,1)S(1)}, u32[]{:S(2)}, u32[]{:S(2)}) collective-permute-start(bf16[256,64]{0,1:T(8,128)(2,1)S(1)} %get-tuple-element.515), channel_id=1, source_target_pairs={{0,1},{1,2},{2,3},{3,4},{4,5},{5,6},{6,7},{7,0},{8,9},{9,10},{10,1... | collective-permute-start | bytes 98312 | tf_op jit(solution)/shard_map/while/body/eval_jaxpr/ppermute | solution.py:266
  87.2 14.5 %conditional.2 = (f32[32,256]{1,0:T(8,128)S(1)}, f32[32,256]{1,0:T(8,128)S(1)}, f32[32,256,128]{2,1,0:T(8,128)}) conditional(s32[]{:T(128)} %convert_element_type.108, (f32[32,256]{1,0:T(8,128)S(1)}, bf16[256,512]{1,0:T(8,128)(2,1)S(1)}, bf16[512,4096]{1,0:T(8,128)(2,1)}, bf16[256,32,128]{2,0,1:T(8,128)(2,1)S(1)}, ...), branch_computations={%region_5.7_spmd, %region_8.10_spmd} | conditional | flops 2830663680 | bytes 96157808 | solution.py:268
  87.2 2.9 fusion.25
  95.3 4.6 %multiply_add_fusion.2 = f32[32,256,128]{2,1,0:T(8,128)S(1)} fusion(f32[32,256,128]{2,1,0:T(8,128)S(1)} %copy-done.3, f32[32,256,128]{1,2,0:T(8,128)S(1)} %get-tuple-element.404, f32[32,256]{1,0:T(8,128)S(1)} %get-tuple-element.395, f32[32,256]{1,0:T(8,128)S(1)} %get-tuple-element.394, f32[32,256]{1,0:T(8,128)S(1)} %get-tuple-element.403, ...), kind=kOutput, calls=%fused_computation.31 | convolution fusion | flops 273678336 | bytes 13729792 | tf_op jit(solution)/shard_map/while/body/eval_jaxpr/cond/branch_1_fun/hqk,khv->hqv/dot_general | solution.py:64
  103.5 3.8 %collective-permute-start.1 = (bf16[256,64]{0,1:T(8,128)(2,1)S(1)}, bf16[256,64]{0,1:T(8,128)(2,1)S(1)}, u32[]{:S(2)}, u32[]{:S(2)}) collective-permute-start(bf16[256,64]{0,1:T(8,128)(2,1)S(1)} %get-tuple-element.515), channel_id=1, source_target_pairs={{0,1},{1,2},{2,3},{3,4},{4,5},{5,6},{6,7},{7,0},{8,9},{9,10},{10,1... | collective-permute-start | bytes 98312 | tf_op jit(solution)/shard_map/while/body/eval_jaxpr/ppermute | solution.py:266
  108.6 14.5 %conditional.2 = (f32[32,256]{1,0:T(8,128)S(1)}, f32[32,256]{1,0:T(8,128)S(1)}, f32[32,256,128]{2,1,0:T(8,128)}) conditional(s32[]{:T(128)} %convert_element_type.108, (f32[32,256]{1,0:T(8,128)S(1)}, bf16[256,512]{1,0:T(8,128)(2,1)S(1)}, bf16[512,4096]{1,0:T(8,128)(2,1)}, bf16[256,32,128]{2,0,1:T(8,128)(2,1)S(1)}, ...), branch_computations={%region_5.7_spmd, %region_8.10_spmd} | conditional | flops 2830663680 | bytes 96157808 | solution.py:268
  108.6 2.9 fusion.25
  116.7 4.6 %multiply_add_fusion.2 = f32[32,256,128]{2,1,0:T(8,128)S(1)} fusion(f32[32,256,128]{2,1,0:T(8,128)S(1)} %copy-done.3, f32[32,256,128]{1,2,0:T(8,128)S(1)} %get-tuple-element.404, f32[32,256]{1,0:T(8,128)S(1)} %get-tuple-element.395, f32[32,256]{1,0:T(8,128)S(1)} %get-tuple-element.394, f32[32,256]{1,0:T(8,128)S(1)} %get-tuple-element.403, ...), kind=kOutput, calls=%fused_computation.31 | convolution fusion | flops 273678336 | bytes 13729792 | tf_op jit(solution)/shard_map/while/body/eval_jaxpr/cond/branch_1_fun/hqk,khv->hqv/dot_general | solution.py:64
  126.2 3.8 %collective-permute-start.1 = (bf16[256,64]{0,1:T(8,128)(2,1)S(1)}, bf16[256,64]{0,1:T(8,128)(2,1)S(1)}, u32[]{:S(2)}, u32[]{:S(2)}) collective-permute-start(bf16[256,64]{0,1:T(8,128)(2,1)S(1)} %get-tuple-element.515), channel_id=1, source_target_pairs={{0,1},{1,2},{2,3},{3,4},{4,5},{5,6},{6,7},{7,0},{8,9},{9,10},{10,1... | collective-permute-start | bytes 98312 | tf_op jit(solution)/shard_map/while/body/eval_jaxpr/ppermute | solution.py:266
  130.9 14.5 %conditional.2 = (f32[32,256]{1,0:T(8,128)S(1)}, f32[32,256]{1,0:T(8,128)S(1)}, f32[32,256,128]{2,1,0:T(8,128)}) conditional(s32[]{:T(128)} %convert_element_type.108, (f32[32,256]{1,0:T(8,128)S(1)}, bf16[256,512]{1,0:T(8,128)(2,1)S(1)}, bf16[512,4096]{1,0:T(8,128)(2,1)}, bf16[256,32,128]{2,0,1:T(8,128)(2,1)S(1)}, ...), branch_computations={%region_5.7_spmd, %region_8.10_spmd} | conditional | flops 2830663680 | bytes 96157808 | solution.py:268
  138.9 4.6 %multiply_add_fusion.2 = f32[32,256,128]{2,1,0:T(8,128)S(1)} fusion(f32[32,256,128]{2,1,0:T(8,128)S(1)} %copy-done.3, f32[32,256,128]{1,2,0:T(8,128)S(1)} %get-tuple-element.404, f32[32,256]{1,0:T(8,128)S(1)} %get-tuple-element.395, f32[32,256]{1,0:T(8,128)S(1)} %get-tuple-element.394, f32[32,256]{1,0:T(8,128)S(1)} %get-tuple-element.403, ...), kind=kOutput, calls=%fused_computation.31 | convolution fusion | flops 273678336 | bytes 13729792 | tf_op jit(solution)/shard_map/while/body/eval_jaxpr/cond/branch_1_fun/hqk,khv->hqv/dot_general | solution.py:64
  148.9 3.8 %collective-permute-start.1 = (bf16[256,64]{0,1:T(8,128)(2,1)S(1)}, bf16[256,64]{0,1:T(8,128)(2,1)S(1)}, u32[]{:S(2)}, u32[]{:S(2)}) collective-permute-start(bf16[256,64]{0,1:T(8,128)(2,1)S(1)} %get-tuple-element.515), channel_id=1, source_target_pairs={{0,1},{1,2},{2,3},{3,4},{4,5},{5,6},{6,7},{7,0},{8,9},{9,10},{10,1... | collective-permute-start | bytes 98312 | tf_op jit(solution)/shard_map/while/body/eval_jaxpr/ppermute | solution.py:266
  153.6 14.5 %conditional.2 = (f32[32,256]{1,0:T(8,128)S(1)}, f32[32,256]{1,0:T(8,128)S(1)}, f32[32,256,128]{2,1,0:T(8,128)}) conditional(s32[]{:T(128)} %convert_element_type.108, (f32[32,256]{1,0:T(8,128)S(1)}, bf16[256,512]{1,0:T(8,128)(2,1)S(1)}, bf16[512,4096]{1,0:T(8,128)(2,1)}, bf16[256,32,128]{2,0,1:T(8,128)(2,1)S(1)}, ...), branch_computations={%region_5.7_spmd, %region_8.10_spmd} | conditional | flops 2830663680 | bytes 96157808 | solution.py:268
  161.7 4.6 %multiply_add_fusion.2 = f32[32,256,128]{2,1,0:T(8,128)S(1)} fusion(f32[32,256,128]{2,1,0:T(8,128)S(1)} %copy-done.3, f32[32,256,128]{1,2,0:T(8,128)S(1)} %get-tuple-element.404, f32[32,256]{1,0:T(8,128)S(1)} %get-tuple-element.395, f32[32,256]{1,0:T(8,128)S(1)} %get-tuple-element.394, f32[32,256]{1,0:T(8,128)S(1)} %get-tuple-element.403, ...), kind=kOutput, calls=%fused_computation.31 | convolution fusion | flops 273678336 | bytes 13729792 | tf_op jit(solution)/shard_map/while/body/eval_jaxpr/cond/branch_1_fun/hqk,khv->hqv/dot_general | solution.py:64
  171.7 3.8 %collective-permute-start.1 = (bf16[256,64]{0,1:T(8,128)(2,1)S(1)}, bf16[256,64]{0,1:T(8,128)(2,1)S(1)}, u32[]{:S(2)}, u32[]{:S(2)}) collective-permute-start(bf16[256,64]{0,1:T(8,128)(2,1)S(1)} %get-tuple-element.515), channel_id=1, source_target_pairs={{0,1},{1,2},{2,3},{3,4},{4,5},{5,6},{6,7},{7,0},{8,9},{9,10},{10,1... | collective-permute-start | bytes 98312 | tf_op jit(solution)/shard_map/while/body/eval_jaxpr/ppermute | solution.py:266
  176.4 14.7 %conditional.2 = (f32[32,256]{1,0:T(8,128)S(1)}, f32[32,256]{1,0:T(8,128)S(1)}, f32[32,256,128]{2,1,0:T(8,128)}) conditional(s32[]{:T(128)} %convert_element_type.108, (f32[32,256]{1,0:T(8,128)S(1)}, bf16[256,512]{1,0:T(8,128)(2,1)S(1)}, bf16[512,4096]{1,0:T(8,128)(2,1)}, bf16[256,32,128]{2,0,1:T(8,128)(2,1)S(1)}, ...), branch_computations={%region_5.7_spmd, %region_8.10_spmd} | conditional | flops 2830663680 | bytes 96157808 | solution.py:268
  176.4 3.5 %fusion.10 = bf16[32,32,8,128]{3,2,1,0:T(8,128)(2,1)S(1)} fusion(bf16[256,512]{1,0:T(8,128)(2,1)S(1)} %get-tuple-element.309, bf16[512,4096]{1,0:T(8,128)(2,1)} %get-tuple-element.310), kind=kOutput, calls=%fused_computation.15 | convolution fusion | flops 1074790400 | bytes 6553600 | tf_op jit(solution)/shard_map/while/body/eval_jaxpr/cond/branch_0_fun/dot_general | solution.py:49
  191.7 3.8 %copy_bitcast_fusion.o_ref = bf16[256,4096]{1,0:T(8,128)(2,1)} fusion(f32[32,256,128]{2,1,0:T(8,128)} %get-tuple-element.343, f32[32,256]{1,0:T(8,128)S(1)} %get-tuple-element.344), kind=kLoop, calls=%fused_computation.62 | loop fusion | flops 2097152 | bytes 6324224 | tf_op jit(solution)/shard_map/reshape | solution.py:274
  195.6 101.7 %out_proj.1 = bf16[256,7168]{1,0:T(8,128)(2,1)} custom-call(bf16[256,4096]{1,0:T(8,128)(2,1)} %copy_bitcast_fusion.o_ref, bf16[4096,7168]{1,0:T(8,128)(2,1)} %w_hbm.1), custom_call_target="tpu_custom_call" | custom-call | tf_op jit(solution)/shard_map/out_proj/pallas_call | solution.py:208
  297.3 4.1 %copy.111 = bf16[256,7168]{1,0:T(8,128)(2,1)} copy(bf16[256,7168]{1,0:T(8,128)(2,1)} %out_proj.1) | data formatting | bytes 7340032
  (159 shorter events, 98.4 us)
Async XLA Ops:
  0.0 14.4 %copy-start = (bf16[7168,64]{0,1:T(8,128)(2,1)S(1)}, bf16[7168,64]{0,1:T(8,128)(2,1)}, u32[]{:S(2)}) copy-start(bf16[7168,64]{0,1:T(8,128)(2,1)} %param.24) | copy-start | bytes 2752516
  0.0 11.6 %copy-start.12 = (bf16[1536]{0:T(1024)(128)(2,1)S(1)}, bf16[1536]{0:T(1024)(128)(2,1)}, u32[]{:S(2)}) copy-start(bf16[1536]{0:T(1024)(128)(2,1)} %param.19) | copy-start | bytes 9220
  0.0 11.6 %copy-start.15 = (bf16[1536,2048]{1,0:T(8,128)(2,1)S(1)}, bf16[1536,2048]{1,0:T(8,128)(2,1)}, u32[]{:S(2)}) copy-start(bf16[1536,2048]{1,0:T(8,128)(2,1)} %param.21) | copy-start | bytes 18874372
  0.0 16.3 %copy-start.14 = (bf16[1536,4096]{1,0:T(8,128)(2,1)S(1)}, bf16[1536,4096]{1,0:T(8,128)(2,1)}, u32[]{:S(2)}) copy-start(bf16[1536,4096]{1,0:T(8,128)(2,1)} %param.20) | copy-start | bytes 37748740
  11.6 2.8 copy-start.9
  20.3 5.4 %copy-start.13 = (bf16[512]{0:T(512)(128)(2,1)S(1)}, bf16[512]{0:T(512)(128)(2,1)}, u32[]{:S(2)}) copy-start(bf16[512]{0:T(512)(128)(2,1)} %param.23) | copy-start | bytes 3076
  20.3 5.5 %copy-start.5 = (bf16[512,4096]{1,0:T(8,128)(2,1)S(1)}, bf16[512,4096]{1,0:T(8,128)(2,1)}, u32[]{:S(2)}) copy-start(bf16[512,4096]{1,0:T(8,128)(2,1)} %param.25) | copy-start | bytes 12582916
  25.8 4.7 %copy-start.10 = (bf16[256,512]{1,0:T(8,128)(2,1)}, bf16[256,512]{1,0:T(8,128)(2,1)S(1)}, u32[]{:S(2)}) copy-start(bf16[256,512]{1,0:T(8,128)(2,1)S(1)} %multiply_convert_fusion.1) | copy-start | bytes 786436
  28.5 2.2 copy-start.6
  38.3 6.2 %collective-permute-start = (bf16[256,512]{1,0:T(8,128)(2,1)}, bf16[256,512]{1,0:T(8,128)(2,1)S(1)}, u32[]{:S(2)}, u32[]{:S(2)}) collective-permute-start(bf16[256,512]{1,0:T(8,128)(2,1)} %get-tuple-element.514), channel_id=1, source_target_pairs={{0,1},{1,2},{2,3},{3,4},{4,5},{5,6},{6,7},{7,0},{8,9},{9,10},{10,1... | collective-permute-start | bytes 786440 | tf_op jit(solution)/shard_map/while/body/eval_jaxpr/ppermute | solution.py:265
  38.3 6.1 %collective-permute-start.1 = (bf16[256,64]{0,1:T(8,128)(2,1)S(1)}, bf16[256,64]{0,1:T(8,128)(2,1)S(1)}, u32[]{:S(2)}, u32[]{:S(2)}) collective-permute-start(bf16[256,64]{0,1:T(8,128)(2,1)S(1)} %get-tuple-element.515), channel_id=1, source_target_pairs={{0,1},{1,2},{2,3},{3,4},{4,5},{5,6},{6,7},{7,0},{8,9},{9,10},{10,1... | collective-permute-start | bytes 98312 | tf_op jit(solution)/shard_map/while/body/eval_jaxpr/ppermute | solution.py:266
  49.0 2.2 copy-start.8
  49.0 3.5 %copy-start.3 = (f32[32,256,128]{2,1,0:T(8,128)S(1)}, f32[32,256,128]{2,1,0:T(8,128)}, u32[]{:S(2)}) copy-start(f32[32,256,128]{2,1,0:T(8,128)} %get-tuple-element.324) | copy-start | bytes 12582916 | tf_op jit(solution)/shard_map/while/body/eval_jaxpr/cond
  59.7 6.2 %collective-permute-start = (bf16[256,512]{1,0:T(8,128)(2,1)}, bf16[256,512]{1,0:T(8,128)(2,1)S(1)}, u32[]{:S(2)}, u32[]{:S(2)}) collective-permute-start(bf16[256,512]{1,0:T(8,128)(2,1)} %get-tuple-element.514), channel_id=1, source_target_pairs={{0,1},{1,2},{2,3},{3,4},{4,5},{5,6},{6,7},{7,0},{8,9},{9,10},{10,1... | collective-permute-start | bytes 786440 | tf_op jit(solution)/shard_map/while/body/eval_jaxpr/ppermute | solution.py:265
  59.7 6.1 %collective-permute-start.1 = (bf16[256,64]{0,1:T(8,128)(2,1)S(1)}, bf16[256,64]{0,1:T(8,128)(2,1)S(1)}, u32[]{:S(2)}, u32[]{:S(2)}) collective-permute-start(bf16[256,64]{0,1:T(8,128)(2,1)S(1)} %get-tuple-element.515), channel_id=1, source_target_pairs={{0,1},{1,2},{2,3},{3,4},{4,5},{5,6},{6,7},{7,0},{8,9},{9,10},{10,1... | collective-permute-start | bytes 98312 | tf_op jit(solution)/shard_map/while/body/eval_jaxpr/ppermute | solution.py:266
  70.4 2.2 copy-start.8
  70.4 3.5 %copy-start.3 = (f32[32,256,128]{2,1,0:T(8,128)S(1)}, f32[32,256,128]{2,1,0:T(8,128)}, u32[]{:S(2)}) copy-start(f32[32,256,128]{2,1,0:T(8,128)} %get-tuple-element.324) | copy-start | bytes 12582916 | tf_op jit(solution)/shard_map/while/body/eval_jaxpr/cond
  81.1 6.2 %collective-permute-start = (bf16[256,512]{1,0:T(8,128)(2,1)}, bf16[256,512]{1,0:T(8,128)(2,1)S(1)}, u32[]{:S(2)}, u32[]{:S(2)}) collective-permute-start(bf16[256,512]{1,0:T(8,128)(2,1)} %get-tuple-element.514), channel_id=1, source_target_pairs={{0,1},{1,2},{2,3},{3,4},{4,5},{5,6},{6,7},{7,0},{8,9},{9,10},{10,1... | collective-permute-start | bytes 786440 | tf_op jit(solution)/shard_map/while/body/eval_jaxpr/ppermute | solution.py:265
  81.1 6.1 %collective-permute-start.1 = (bf16[256,64]{0,1:T(8,128)(2,1)S(1)}, bf16[256,64]{0,1:T(8,128)(2,1)S(1)}, u32[]{:S(2)}, u32[]{:S(2)}) collective-permute-start(bf16[256,64]{0,1:T(8,128)(2,1)S(1)} %get-tuple-element.515), channel_id=1, source_target_pairs={{0,1},{1,2},{2,3},{3,4},{4,5},{5,6},{6,7},{7,0},{8,9},{9,10},{10,1... | collective-permute-start | bytes 98312 | tf_op jit(solution)/shard_map/while/body/eval_jaxpr/ppermute | solution.py:266
  91.8 3.5 %copy-start.3 = (f32[32,256,128]{2,1,0:T(8,128)S(1)}, f32[32,256,128]{2,1,0:T(8,128)}, u32[]{:S(2)}) copy-start(f32[32,256,128]{2,1,0:T(8,128)} %get-tuple-element.324) | copy-start | bytes 12582916 | tf_op jit(solution)/shard_map/while/body/eval_jaxpr/cond
  102.5 6.2 %collective-permute-start = (bf16[256,512]{1,0:T(8,128)(2,1)}, bf16[256,512]{1,0:T(8,128)(2,1)S(1)}, u32[]{:S(2)}, u32[]{:S(2)}) collective-permute-start(bf16[256,512]{1,0:T(8,128)(2,1)} %get-tuple-element.514), channel_id=1, source_target_pairs={{0,1},{1,2},{2,3},{3,4},{4,5},{5,6},{6,7},{7,0},{8,9},{9,10},{10,1... | collective-permute-start | bytes 786440 | tf_op jit(solution)/shard_map/while/body/eval_jaxpr/ppermute | solution.py:265
  103.5 5.2 %collective-permute-start.1 = (bf16[256,64]{0,1:T(8,128)(2,1)S(1)}, bf16[256,64]{0,1:T(8,128)(2,1)S(1)}, u32[]{:S(2)}, u32[]{:S(2)}) collective-permute-start(bf16[256,64]{0,1:T(8,128)(2,1)S(1)} %get-tuple-element.515), channel_id=1, source_target_pairs={{0,1},{1,2},{2,3},{3,4},{4,5},{5,6},{6,7},{7,0},{8,9},{9,10},{10,1... | collective-permute-start | bytes 98312 | tf_op jit(solution)/shard_map/while/body/eval_jaxpr/ppermute | solution.py:266
  113.2 3.5 %copy-start.3 = (f32[32,256,128]{2,1,0:T(8,128)S(1)}, f32[32,256,128]{2,1,0:T(8,128)}, u32[]{:S(2)}) copy-start(f32[32,256,128]{2,1,0:T(8,128)} %get-tuple-element.324) | copy-start | bytes 12582916 | tf_op jit(solution)/shard_map/while/body/eval_jaxpr/cond
  123.9 7.0 %collective-permute-start = (bf16[256,512]{1,0:T(8,128)(2,1)}, bf16[256,512]{1,0:T(8,128)(2,1)S(1)}, u32[]{:S(2)}, u32[]{:S(2)}) collective-permute-start(bf16[256,512]{1,0:T(8,128)(2,1)} %get-tuple-element.514), channel_id=1, source_target_pairs={{0,1},{1,2},{2,3},{3,4},{4,5},{5,6},{6,7},{7,0},{8,9},{9,10},{10,1... | collective-permute-start | bytes 786440 | tf_op jit(solution)/shard_map/while/body/eval_jaxpr/ppermute | solution.py:265
  126.2 4.7 %collective-permute-start.1 = (bf16[256,64]{0,1:T(8,128)(2,1)S(1)}, bf16[256,64]{0,1:T(8,128)(2,1)S(1)}, u32[]{:S(2)}, u32[]{:S(2)}) collective-permute-start(bf16[256,64]{0,1:T(8,128)(2,1)S(1)} %get-tuple-element.515), channel_id=1, source_target_pairs={{0,1},{1,2},{2,3},{3,4},{4,5},{5,6},{6,7},{7,0},{8,9},{9,10},{10,1... | collective-permute-start | bytes 98312 | tf_op jit(solution)/shard_map/while/body/eval_jaxpr/ppermute | solution.py:266
  135.5 3.5 %copy-start.3 = (f32[32,256,128]{2,1,0:T(8,128)S(1)}, f32[32,256,128]{2,1,0:T(8,128)}, u32[]{:S(2)}) copy-start(f32[32,256,128]{2,1,0:T(8,128)} %get-tuple-element.324) | copy-start | bytes 12582916 | tf_op jit(solution)/shard_map/while/body/eval_jaxpr/cond
  146.1 7.5 %collective-permute-start = (bf16[256,512]{1,0:T(8,128)(2,1)}, bf16[256,512]{1,0:T(8,128)(2,1)S(1)}, u32[]{:S(2)}, u32[]{:S(2)}) collective-permute-start(bf16[256,512]{1,0:T(8,128)(2,1)} %get-tuple-element.514), channel_id=1, source_target_pairs={{0,1},{1,2},{2,3},{3,4},{4,5},{5,6},{6,7},{7,0},{8,9},{9,10},{10,1... | collective-permute-start | bytes 786440 | tf_op jit(solution)/shard_map/while/body/eval_jaxpr/ppermute | solution.py:265
  148.9 4.7 %collective-permute-start.1 = (bf16[256,64]{0,1:T(8,128)(2,1)S(1)}, bf16[256,64]{0,1:T(8,128)(2,1)S(1)}, u32[]{:S(2)}, u32[]{:S(2)}) collective-permute-start(bf16[256,64]{0,1:T(8,128)(2,1)S(1)} %get-tuple-element.515), channel_id=1, source_target_pairs={{0,1},{1,2},{2,3},{3,4},{4,5},{5,6},{6,7},{7,0},{8,9},{9,10},{10,1... | collective-permute-start | bytes 98312 | tf_op jit(solution)/shard_map/while/body/eval_jaxpr/ppermute | solution.py:266
  158.2 3.5 %copy-start.3 = (f32[32,256,128]{2,1,0:T(8,128)S(1)}, f32[32,256,128]{2,1,0:T(8,128)}, u32[]{:S(2)}) copy-start(f32[32,256,128]{2,1,0:T(8,128)} %get-tuple-element.324) | copy-start | bytes 12582916 | tf_op jit(solution)/shard_map/while/body/eval_jaxpr/cond
  168.9 7.5 %collective-permute-start = (bf16[256,512]{1,0:T(8,128)(2,1)}, bf16[256,512]{1,0:T(8,128)(2,1)S(1)}, u32[]{:S(2)}, u32[]{:S(2)}) collective-permute-start(bf16[256,512]{1,0:T(8,128)(2,1)} %get-tuple-element.514), channel_id=1, source_target_pairs={{0,1},{1,2},{2,3},{3,4},{4,5},{5,6},{6,7},{7,0},{8,9},{9,10},{10,1... | collective-permute-start | bytes 786440 | tf_op jit(solution)/shard_map/while/body/eval_jaxpr/ppermute | solution.py:265
  171.7 4.7 %collective-permute-start.1 = (bf16[256,64]{0,1:T(8,128)(2,1)S(1)}, bf16[256,64]{0,1:T(8,128)(2,1)S(1)}, u32[]{:S(2)}, u32[]{:S(2)}) collective-permute-start(bf16[256,64]{0,1:T(8,128)(2,1)S(1)} %get-tuple-element.515), channel_id=1, source_target_pairs={{0,1},{1,2},{2,3},{3,4},{4,5},{5,6},{6,7},{7,0},{8,9},{9,10},{10,1... | collective-permute-start | bytes 98312 | tf_op jit(solution)/shard_map/while/body/eval_jaxpr/ppermute | solution.py:266
  195.6 105.9 %copy-start.1 = (bf16[7168,64]{0,1:T(8,128)(2,1)S(1)}, bf16[7168,64]{0,1:T(8,128)(2,1)}, u32[]{:S(2)}) copy-start(bf16[7168,64]{0,1:T(8,128)(2,1)} %param.24) | copy-start | bytes 2752516
  (13 other events, 26.0 us)

commit v2 on v1

--- a/solution.py
+++ b/solution.py
@@ -9,7 +9,6 @@
 
 ROPE_BASE = 10000.0
 NORM_EPS = 1e-6
-NEG_BIG = -1e30
 
 
 def rms_norm(act_in, gain_vec):
@@ -29,49 +28,6 @@
     first_half = act_in[..., :half_dim]
     second_half = act_in[..., half_dim:]
     return jnp.concatenate([first_half * cos_t - second_half * sin_t, second_half * cos_t + first_half * sin_t], axis=-1)
-
-
-def project_tokens(tok_x, tok_pos, w_dq, g_q, w_uq, w_qr, w_dkv, g_kv, w_kr, heads_loc):
-    rope_dim = w_kr.shape[1]
-    tok_count = tok_x.shape[0]
-    cos_t, sin_t = rope_tables(tok_pos, rope_dim)
-    c_q = rms_norm(jnp.dot(tok_x, w_dq, preferred_element_type=jnp.float32), g_q).astype(jnp.bfloat16)
-    q_nope = jnp.dot(c_q, w_uq, preferred_element_type=jnp.float32).astype(jnp.bfloat16).reshape(tok_count, heads_loc, -1)
-    q_rot = jnp.dot(c_q, w_qr, preferred_element_type=jnp.float32).reshape(tok_count, heads_loc, rope_dim)
-    q_pe = apply_rope(q_rot, cos_t[:, None, :], sin_t[:, None, :]).astype(jnp.bfloat16)
-    c_kv = rms_norm(jnp.dot(tok_x, w_dkv, preferred_element_type=jnp.float32), g_kv).astype(jnp.bfloat16)
-    k_pe = apply_rope(jnp.dot(tok_x, w_kr, preferred_element_type=jnp.float32), cos_t, sin_t).astype(jnp.bfloat16)
-    return q_nope, q_pe, c_kv, k_pe
-
-
-def up_project(lat_rows, w_uk, w_uv, heads_loc):
-    row_count = lat_rows.shape[0]
-    k_nope = jnp.dot(lat_rows, w_uk, preferred_element_type=jnp.float32).astype(jnp.bfloat16).reshape(row_count, heads_loc, -1)
-    v_rows = jnp.dot(lat_rows, w_uv, preferred_element_type=jnp.float32).astype(jnp.bfloat16).reshape(row_count, heads_loc, -1)
-    return k_nope, v_rows
-
-
-def block_scores(q_nope, q_pe, k_nope, k_pe, score_scale):
-    nope_part = jnp.einsum('qhn,khn->hqk', q_nope, k_nope, preferred_element_type=jnp.float32)
-    rope_part = jnp.einsum('qhr,kr->hqk', q_pe, k_pe, preferred_element_type=jnp.float32)
-    return (nope_part + rope_part) * score_scale
-
-
-def block_stats(scores, v_rows):
-    blk_max = jnp.max(scores, axis=-1)
-    prob_tile = jnp.exp(scores - blk_max[..., None])
-    blk_sum = jnp.sum(prob_tile, axis=-1)
-    blk_acc = jnp.einsum('hqk,khv->hqv', prob_tile.astype(jnp.bfloat16), v_rows, preferred_element_type=jnp.float32)
-    return blk_max, blk_sum, blk_acc
-
-
-def merge_stats(run_state, update):
-    old_max, old_sum, old_acc = run_state
-    new_max, new_sum, new_acc = update
-    top_max = jnp.maximum(old_max, new_max)
-    old_w = jnp.exp(old_max - top_max)
-    new_w = jnp.exp(new_max - top_max)
-    return top_max, old_sum * old_w + new_sum * new_w, old_acc * old_w[..., None] + new_acc * new_w[..., None]
 
 
 MESH = pl.DeviceIdType.MESH
@@ -222,9 +178,113 @@
     )(attn_out, w_o)
 
 
+KEY_BLOCK = 256
+
+
+def attend_kernel(n_ctx, scale, q_ref, lat_ref, kpe_ref, wuk_hbm, wuv_hbm, o_ref, wuk, wuv, wuv_t, lat_t, kcat, v_t, s_buf, p_buf, w_sem):
+    me = lax.axis_index('ctx')
+    col = me // 2
+    part = lax.rem(me, 2)
+    n_col = n_ctx // 2
+    heads = q_ref.shape[0]
+    n_pair = heads // 2
+    rank = lat_ref.shape[1]
+    v_dim = v_t.shape[0] // 2
+    nope = wuk.shape[2] // 2
+    rope = kpe_ref.shape[1]
+    exp_scale = scale * 1.4426950408889634
+
+    def w_copy(src, dst, which, hp):
+        cols = dst.shape[2]
+        return pltpu.make_async_copy(src.at[:, pl.ds(pl.multiple_of((part * n_pair + hp) * cols, cols), cols)], dst.at[hp], w_sem.at[which, hp])
+
+    for hp in range(n_pair):
+        w_copy(wuk_hbm, wuk, 0, hp).start()
+        w_copy(wuv_hbm, wuv, 1, hp).start()
+    for blk in range(lat_ref.shape[0] // KEY_BLOCK):
+        lat_t[:, blk * KEY_BLOCK:(blk + 1) * KEY_BLOCK] = lat_ref[blk * KEY_BLOCK:(blk + 1) * KEY_BLOCK].T
+        for g in range(2):
+            kcat[g, blk * KEY_BLOCK:(blk + 1) * KEY_BLOCK, nope:nope + rope] = kpe_ref[blk * KEY_BLOCK:(blk + 1) * KEY_BLOCK]
+    for hp in range(n_pair):
+        w_copy(wuk_hbm, wuk, 0, hp).wait()
+        w_copy(wuv_hbm, wuv, 1, hp).wait()
+        wuv_t[hp] = wuv[hp].T
+
+    def phase(sel, n_blk):
+        q_cols = slice(sel * KEY_BLOCK, (sel + 1) * KEY_BLOCK)
+        key_i = lax.broadcasted_iota(jnp.int32, (KEY_BLOCK, KEY_BLOCK), 0)
+        q_i = lax.broadcasted_iota(jnp.int32, (KEY_BLOCK, KEY_BLOCK), 1)
+        visible = key_i <= q_i
+
+        def pair_step(hp, _):
+            for blk in range(n_blk):
+                rows = slice(blk * KEY_BLOCK, (blk + 1) * KEY_BLOCK)
+                k2 = jnp.dot(lat_ref[rows], wuk[hp], preferred_element_type=jnp.float32).astype(jnp.bfloat16)
+                kcat[0, rows, 0:nope] = k2[:, :nope]
+                kcat[1, rows, 0:nope] = k2[:, nope:]
+                v_t[:, rows] = jnp.dot(wuv_t[hp], lat_t[:, rows], preferred_element_type=jnp.float32).astype(jnp.bfloat16)
+            top = []
+            for g in range(2):
+                q_t = q_ref[2 * hp + g, :, q_cols]
+                top8 = None
+                for blk in range(n_blk):
+                    rows = slice(blk * KEY_BLOCK, (blk + 1) * KEY_BLOCK)
+                    s = jnp.dot(kcat[g, rows, 0:nope + rope], q_t, preferred_element_type=jnp.float32)
+                    if blk == n_blk - 1:
+                        s = jnp.where(visible, s, -1e30)
+                    s_buf[g, rows] = s
+                    blk8 = jnp.max(s.reshape(KEY_BLOCK // 8, 8, KEY_BLOCK), axis=0)
+                    top8 = blk8 if top8 is None else jnp.maximum(top8, blk8)
+                top.append(jnp.max(top8, axis=0, keepdims=True) * exp_scale)
+            for g in range(2):
+                sum8 = None
+                for blk in range(n_blk):
+                    rows = slice(blk * KEY_BLOCK, (blk + 1) * KEY_BLOCK)
+                    p = jnp.exp2(s_buf[g, rows] * exp_scale - top[g])
+                    blk8 = jnp.sum(p.reshape(KEY_BLOCK // 8, 8, KEY_BLOCK), axis=0)
+                    sum8 = blk8 if sum8 is None else sum8 + blk8
+                    p_buf[g, rows] = p.astype(jnp.bfloat16)
+                total = jnp.sum(sum8, axis=0, keepdims=True)
+                o_t = jnp.dot(v_t[g * v_dim:(g + 1) * v_dim, 0:n_blk * KEY_BLOCK], p_buf[g, 0:n_blk * KEY_BLOCK], preferred_element_type=jnp.float32)
+                o_ref[q_cols, pl.ds(pl.multiple_of((2 * hp + g) * v_dim, v_dim), v_dim)] = (o_t / total).T.astype(o_ref.dtype)
+            return 0
+
+        lax.fori_loop(0, n_pair, pair_step, 0)
+
+    for v in range(n_col):
+        pl.when(col == v)(functools.partial(phase, 0, v + 1))
+    for v in range(n_col):
+        pl.when(col == v)(functools.partial(phase, 1, 2 * n_col - v))
+
+
+def attend(q_t, lat, kpe, w_uk, w_uv, n_ctx, scale):
+    heads, q_dim, q_count = q_t.shape
+    keys, rank = lat.shape
+    rope = kpe.shape[1]
+    nope = q_dim - rope
+    v_dim = w_uv.shape[1] // (2 * heads)
+    n_pair = heads // 2
+    bf16, f32 = jnp.bfloat16, jnp.float32
+    vmem = pl.BlockSpec(memory_space=pltpu.VMEM)
+    hbm = pl.BlockSpec(memory_space=pl.ANY)
+    assert q_count == 2 * KEY_BLOCK and keys == n_ctx * KEY_BLOCK
+    return pl.pallas_call(
+        functools.partial(attend_kernel, n_ctx, scale),
+        out_shape=jax.ShapeDtypeStruct((q_count, heads * v_dim), bf16),
+        in_specs=[vmem, vmem, vmem, hbm, hbm],
+        out_specs=vmem,
+        scratch_shapes=[
+            pltpu.VMEM((n_pair, rank, 2 * nope), bf16), pltpu.VMEM((n_pair, rank, 2 * v_dim), bf16), pltpu.VMEM((n_pair, 2 * v_dim, rank), bf16),
+            pltpu.VMEM((rank, keys), bf16), pltpu.VMEM((2, keys, nope + rope), bf16), pltpu.VMEM((2 * v_dim, keys), bf16),
+            pltpu.VMEM((2, keys, KEY_BLOCK), f32), pltpu.VMEM((2, keys, KEY_BLOCK), bf16),
+            pltpu.SemaphoreType.DMA((2, n_pair)),
+        ],
+        compiler_params=pltpu.CompilerParams(vmem_limit_bytes=60 * 1024 * 1024),
+        name='attend',
+    )(q_t, lat, kpe, w_uk, w_uv)
+
+
 def solution(mesh):
-    ctx_count = mesh.shape['ctx']
-    next_perm = [(src, (src + 1) % ctx_count) for src in range(ctx_count)]
     tok_spec = P(('dp', 'ctx'), None)
     pos_spec = P(('dp', 'ctx'))
     full_mat = P(None, None)
@@ -240,38 +300,43 @@
         nope_dim = w_uq.shape[1] // heads_loc
         value_dim = w_uv.shape[1] // heads_loc
         score_scale = (nope_dim + rope_dim) ** -0.5
-        q_nope, q_pe, c_kv, k_pe = project_tokens(tok_x, tok_pos, w_dq, g_q, w_uq, w_qr, w_dkv, g_kv, w_kr, heads_loc)
-        k_nope, v_rows = up_project(c_kv, w_uk, w_uv, heads_loc)
-        scores = block_scores(q_nope, q_pe, k_nope, k_pe, score_scale)
-        visible = tok_pos[None, :] <= tok_pos[:, None]
-        run_state = block_stats(jnp.where(visible[None], scores, NEG_BIG), v_rows)
-
-        def attend_lower(lat_blk, rot_blk, run_state):
-            k_low, v_low = up_project(lat_blk[:half_len], w_uk, w_uv, heads_loc)
-            update = block_stats(block_scores(q_nope, q_pe, k_low, rot_blk[:half_len], score_scale), v_low)
-            return merge_stats(run_state, update)
-
-        def attend_upper(lat_blk, rot_blk, run_state):
-            k_both, v_both = up_project(lat_blk, w_uk, w_uv, heads_loc)
-            update = block_stats(block_scores(q_nope[half_len:], q_pe[half_len:], k_both, rot_blk, score_scale), v_both)
-            old_max, old_sum, old_acc = run_state
-            top_max, top_sum, top_acc = merge_stats((old_max[:, half_len:], old_sum[:, half_len:], old_acc[:, half_len:]), update)
-            return (jnp.concatenate([old_max[:, :half_len], top_max], axis=1),
-                    jnp.concatenate([old_sum[:, :half_len], top_sum], axis=1),
-                    jnp.concatenate([old_acc[:, :half_len], top_acc], axis=1))
-
-        def ctx_step(hop_idx, loop_carry):
-            lat_blk, rot_blk, run_state = loop_carry
-            lat_blk = lax.ppermute(lat_blk, 'ctx', next_perm)
-            rot_blk = lax.ppermute(rot_blk, 'ctx', next_perm)
-            src_index = (my_index - hop_idx) % ctx_count
-            run_state = lax.cond(src_index < my_index, attend_lower, attend_upper, lat_blk, rot_blk, run_state)
-            return lat_blk, rot_blk, run_state
-
-        loop_carry = lax.fori_loop(1, ctx_count, ctx_step, (c_kv, k_pe, run_state))
-        run_max, run_sum, run_acc = loop_carry[2]
-        attn_out = (run_acc / run_sum[..., None]).astype(jnp.bfloat16)
-        attn_out = jnp.transpose(attn_out, (1, 0, 2)).reshape(tok_x.shape[0], -1)
+        n_ctx = mesh.shape['ctx']
+        heads_half = heads_loc // 2
+        part = my_index % 2
+        swap = [(i, i ^ 1) for i in range(n_ctx)]
+        cos_t, sin_t = rope_tables(tok_pos, rope_dim)
+        c_kv = rms_norm(jnp.dot(tok_x, w_dkv, preferred_element_type=jnp.float32), g_kv).astype(jnp.bfloat16)
+        k_pe = apply_rope(jnp.dot(tok_x, w_kr, preferred_element_type=jnp.float32), cos_t, sin_t).astype(jnp.bfloat16)
+        c_q = rms_norm(jnp.dot(tok_x, w_dq, preferred_element_type=jnp.float32), g_q).astype(jnp.bfloat16)
+
+        def in_order(rows):
+            rows = lax.all_gather(rows, 'ctx')
+            halves = rows.reshape((n_ctx, 2, half_len) + rows.shape[2:])
+            return jnp.concatenate([halves[:, 0], halves[::-1, 1]], axis=0).reshape((-1,) + rows.shape[2:])
+
+        def pair_rows(own):
+            other = lax.ppermute(own, 'ctx', swap)
+            even = jnp.where(part == 0, own, other)
+            odd = jnp.where(part == 0, other, own)
+            return jnp.concatenate([even[:half_len], odd[:half_len], odd[half_len:], even[half_len:]], axis=0)
+
+        lat_all = in_order(c_kv)
+        kpe_all = in_order(k_pe)
+        c_q2 = pair_rows(c_q)
+        cos_2, sin_2 = rope_tables(pair_rows(tok_pos[:, None])[:, 0], rope_dim)
+        w_uq_half = lax.dynamic_slice_in_dim(w_uq, part * heads_half * nope_dim, heads_half * nope_dim, axis=1)
+        w_qr_half = lax.dynamic_slice_in_dim(w_qr, part * heads_half * rope_dim, heads_half * rope_dim, axis=1)
+        q_nope = jnp.dot(c_q2, w_uq_half, preferred_element_type=jnp.float32).astype(jnp.bfloat16).reshape(-1, heads_half, nope_dim)
+        q_rot = jnp.dot(c_q2, w_qr_half, preferred_element_type=jnp.float32).reshape(-1, heads_half, rope_dim)
+        q_pe = apply_rope(q_rot, cos_2[:, None, :], sin_2[:, None, :]).astype(jnp.bfloat16)
+        q_t = jnp.transpose(jnp.concatenate([q_nope, q_pe], axis=-1), (1, 2, 0))
+        o_half = attend(q_t, lat_all, kpe_all, w_uk, w_uv, n_ctx, score_scale)
+        quarter = [o_half[i * half_len:(i + 1) * half_len] for i in range(4)]
+        o_even = jnp.concatenate([quarter[0], quarter[3]], axis=0)
+        o_odd = jnp.concatenate([quarter[1], quarter[2]], axis=0)
+        mine = jnp.where(part == 0, o_even, o_odd)
+        theirs = lax.ppermute(jnp.where(part == 0, o_odd, o_even), 'ctx', swap)
+        attn_out = jnp.concatenate([jnp.where(part == 0, mine, theirs), jnp.where(part == 0, theirs, mine)], axis=1)
         return project_out(attn_out, w_o, mesh.shape['tp'])
 
     return jax.shard_map(local_step, mesh=mesh,

time: 306 us -> 237 us (0.77)
  matrix products: 103 us -> 31.9 us
  Pallas kernels: 102 us -> 139 us
  starting transfers between devices: 30.6 us -> 0.63 us
  local copies, waits for them, and re-layouts: 34.6 us -> 12.2 us
  blocking collectives: 0 us -> 22.2 us
  between operations: 0.29 us -> 13.7 us
  waiting for transfers between devices: 16 us -> 2.69 us
    dot_general x45 -> x5, matrix products: 103 us -> 31.9 us  [the longest x1 14.5 us: local_step(): jnp.dot(tok_x, w_dq, preferred_element_type=jnp.float32)]
    pallas_call x0 -> x1, Pallas kernels: none -> 36.3 us  [attend(): pl.pallas_call(functools.partial(attend_kernel, n_ctx, scale), out_shape=...]
    ppermute x14 -> x3, starting transfers between devices: 30.6 us -> 0.63 us  [the longest x2 0.51 us: pair_rows(): other = lax.ppermute(own, 'ctx', swap)]
    cond x40 -> x0, local copies, waits for them, and re-layouts: 24.6 us -> none
    all_gather x0 -> x1, blocking collectives: none -> 22.2 us  [in_order(): rows = lax.all_gather(rows, 'ctx')]
    ppermute x14 -> x3, waiting for transfers between devices: 16 us -> 2.64 us  [the longest x1 2.63 us: local_step(): theirs = lax.ppermute(jnp.where(part == 0, o_odd, o_even), 'ctx', swap)]
    reduce_sum x8 -> x0, other arithmetic: 7.49 us -> none  [block_stats(): blk_sum = jnp.sum(prob_tile, axis=-1)]
    while x14 -> x0, local copies, waits for them, and re-layouts: 4.94 us -> none
  transfers between devices with their start and end apart: 14 -> 4, of which waited for: 7 -> 1; matrix products, arithmetic and copies ran while one was open for 0% -> 11% of each run, Pallas kernels for 0% -> 0%
where the time goes in v2:
time: 237 us; the launch traced here: 235 us
  Pallas kernels  139 us (59%)
  matrix products  31.9 us (13%)
  blocking collectives  22.2 us (9%)
  between operations  13.7 us (6%)
  local copies, waits for them, and re-layouts  12.2 us (5%)
  other arithmetic  11.9 us (5%)
  waiting for transfers between devices  2.69 us (1%)
    pallas_call x1, Pallas kernels, project_out(): pl.pallas_call(functools.partial(out_kernel, n_tp, n_blk), out_shape=jax....  103 us
    pallas_call x1, Pallas kernels, attend(): pl.pallas_call(functools.partial(attend_kernel, n_ctx, scale), out_shape=...  36.3 us
    all_gather x1, blocking collectives, in_order(): rows = lax.all_gather(rows, 'ctx')  22.2 us
    dot_general x1, matrix products, local_step(): jnp.dot(tok_x, w_dq, preferred_element_type=jnp.float32)  14.5 us
    dot_general x1, matrix products, local_step(): jnp.dot(c_q2, w_uq_half, preferred_element_type=jnp.float32)  8.13 us
    unnamed x23, local copies, waits for them, and re-layouts  5.48 us
  transfers between devices with their start and end apart: 4, of which 1 were waited for; matrix products, arithmetic and copies ran while one was open for 11% of the time, Pallas kernels for 0%

profile of v2, /device:TPU:102, one launch (start us, length us, event | category | flops | bytes accessed | tf_op | source)
XLA Modules:
  0.0 234.5 jit_solution(13114345068597804393)
XLA Ops:
  6.6 0.8 convert_element_type.34
  7.3 14.5 %multiply_reduce_fusion = (f32[256]{0:T(256)S(1)}, f32[256,1536]{1,0:T(8,128)S(1)}) fusion(bf16[256,7168]{1,0:T(8,128)(2,1)} %param.12, bf16[7168,1536]{1,0:T(8,128)(2,1)} %param.14), kind=kOutput, calls=%fused_computation.10 | convolution fusion | flops 5637931008 | bytes 27264000 | tf_op jit(solution)/shard_map/dot_general | solution.py:310
  21.9 1.1 multiply_convert_fusion
  23.0 0.5 collective-permute-start.1
  23.5 2.1 multiply_reduce_fusion.1
  25.6 0.8 multiply_convert_fusion.1
  26.6 3.3 %fusion.24 = f32[256,64]{0,1:T(8,128)S(1)} fusion(bf16[256,7168]{1,0:T(8,128)(2,1)} %param.12, bf16[7168,64]{0,1:T(8,128)(2,1)S(1)} %copy-done), kind=kOutput, calls=%fused_computation.57 | convolution fusion | flops 234881024 | bytes 4653056 | tf_op jit(solution)/shard_map/dot_general | solution.py:309
  29.8 0.2 fusion.16
  30.1 22.2 %all_gather.12 = bf16[8,256,64]{1,2,0:T(8,128)(2,1)S(1)} all-gather(bf16[1,256,64]{1,2,0:T(8,128)(2,1)S(1)} %pad_maximum_fusion.7), channel_id=1, replica_groups=mesh['dp'=1,'tp'=4,'ctx'=8] {'ctx'}, dimensions={0}, use_global_device_ids=true | all-gather | bytes 294912 | tf_op jit(solution)/shard_map/all_gather | solution.py:313
  52.3 0.5 fusion.23
  52.8 0.2 copy.29
  53.0 0.2 copy.28
  53.2 0.9 pad_maximum_fusion.6
  54.2 0.3 multiply_cosine_fusion
  54.5 0.4 broadcast_select_fusion.4
  55.0 0.8 copy-done.4
  55.8 0.1 copy-done.6
  55.9 8.1 %fusion.4 = bf16[512,2048]{1,0:T(8,128)(2,1)} fusion(bf16[1536,4096]{1,0:T(8,128)(2,1)} %param.16, s32[]{:T(128)S(6)} %select_n.62, bf16[128,1536]{1,0:T(8,128)(2,1)S(1)} %get-tuple-element.16, bf16[256,1536]{1,0:T(8,128)(2,1)S(1)} %get-tuple-element.13, bf16[128,1536]{1,0:T(8,128)(2,1)S(1)} %get-tuple-element.15), kind=kOutput, calls=%fused_computation.5 | convolution fusion | flops 3226992640 | bytes 9961476 | tf_op jit(solution)/shard_map/dot_general | solution.py:329
  64.1 2.9 %copy.19 = bf16[512,2048]{0,1:T(8,128)(2,1)S(1)} copy(bf16[512,2048]{1,0:T(8,128)(2,1)} %fusion.4) | data formatting | bytes 4194304 | tf_op jit(solution)/shard_map/convert_element_type | solution.py:329
  67.0 3.9 %fusion.2 = f32[512,1024]{0,1:T(8,128)S(1)} fusion(bf16[1536,2048]{1,0:T(8,128)(2,1)} %param.17, s32[]{:T(128)S(6)} %select_n.63, bf16[128,1536]{1,0:T(8,128)(2,1)} %copy-done.6, bf16[256,1536]{1,0:T(8,128)(2,1)S(1)} %copy-done.5, bf16[128,1536]{1,0:T(8,128)(2,1)S(1)} %get-tuple-element.15), kind=kOutput, calls=%fused_computation.3 | convolution fusion | flops 1615331328 | bytes 6815748 | tf_op jit(solution)/shard_map/dot_general | solution.py:330
  70.9 0.3 subtract_convert_fusion
  71.2 1.8 maximum_bitcast_fusion.q_ref
  73.0 1.7 slice_bitcast_fusion.1
  74.8 1.5 pad_maximum_fusion
  76.3 36.3 %attend.1 = bf16[512,2048]{1,0:T(8,128)(2,1)} custom-call(bf16[16,192,512]{2,1,0:T(8,128)(2,1)} %maximum_bitcast_fusion.q_ref, bf16[2048,512]{1,0:T(8,128)(2,1)} %bitcast.37, bf16[2048,64]{1,0:T(8,128)(2,1)} %bitcast.38, bf16[512,4096]{1,0:T(8,128)(2,1)} %wuk_hbm.1, bf16[512,4096]{1,0:T(8,128)(2,1)} %wuv_hbm.1), custom_call_target="tpu_custom_call" | custom-call | tf_op jit(solution)/shard_map/attend/pallas_call | solution.py:271
  112.7 1.4 fusion.21
  114.1 1.6 broadcast_select_fusion.2
  115.8 2.6 %collective-permute-done.2 = bf16[256,2048]{1,0:T(8,128)(2,1)S(1)} collective-permute-done((bf16[256,2048]{1,0:T(8,128)(2,1)S(1)}, bf16[256,2048]{1,0:T(8,128)(2,1)S(1)}, u32[]{:S(2)}, u32[]{:S(2)}) %collective-permute-start.2) | collective-permute-done | bytes 1048608 | tf_op jit(solution)/shard_map/ppermute | solution.py:338
  118.5 0.6 broadcast_select_fusion.1
  119.1 1.5 pad_maximum_fusion.1.o_ref
  120.6 102.9 %out_proj.1 = bf16[256,7168]{1,0:T(8,128)(2,1)} custom-call(bf16[256,4096]{1,0:T(8,128)(2,1)} %pad_maximum_fusion.1.o_ref, bf16[4096,7168]{1,0:T(8,128)(2,1)} %w_hbm.1), custom_call_target="tpu_custom_call" | custom-call | tf_op jit(solution)/shard_map/out_proj/pallas_call | solution.py:164
  223.6 4.1 %copy.31 = bf16[256,7168]{1,0:T(8,128)(2,1)} copy(bf16[256,7168]{1,0:T(8,128)(2,1)} %out_proj.1) | data formatting | bytes 7340032
  (38 shorter events, 0.5 us)
Async XLA Ops:
  6.5 20.0 %copy-start = (bf16[7168,64]{0,1:T(8,128)(2,1)S(1)}, bf16[7168,64]{0,1:T(8,128)(2,1)}, u32[]{:S(2)}) copy-start(bf16[7168,64]{0,1:T(8,128)(2,1)} %param.20) | copy-start | bytes 2752516
  6.6 66.5 %all-gather.3.cloned.1.call-start = ((), (), s32[]{:S(2)}) async-start(), calls=%async_computation | async-start | bytes 2359296 | tf_op jit(solution)/shard_map/all_gather | solution.py:313
  7.3 15.6 %copy-start.7 = (s32[256]{0:T(256)S(1)}, s32[256]{0:T(256)}, u32[]{:S(2)}) copy-start(s32[256]{0:T(256)} %param.13) | copy-start | bytes 3076
  7.3 16.2 %copy-start.3 = (bf16[256,7168]{1,0:T(8,128)(2,1)S(1)}, bf16[256,7168]{1,0:T(8,128)(2,1)}, u32[]{:S(2)}) copy-start(bf16[256,7168]{1,0:T(8,128)(2,1)} %param.12) | copy-start | bytes 11010052
  7.3 16.2 %copy-start.9 = (bf16[7168,512]{1,0:T(8,128)(2,1)S(1)}, bf16[7168,512]{1,0:T(8,128)(2,1)}, u32[]{:S(2)}) copy-start(bf16[7168,512]{1,0:T(8,128)(2,1)} %param.18) | copy-start | bytes 22020100
  23.0 31.5 %collective-permute-start = (bf16[256,1536]{1,0:T(8,128)(2,1)}, bf16[256,1536]{1,0:T(8,128)(2,1)S(1)}, u32[]{:S(2)}, u32[]{:S(2)}) collective-permute-start(bf16[256,1536]{1,0:T(8,128)(2,1)} %multiply_convert_fusion), channel_id=1, source_target_pairs={{0,1},{1,0},{2,3},{3,2},{4,5},{5,4},{6,7},{7,6},{8,9},{9,8},{10,11... | collective-permute-start | bytes 2359304 | tf_op jit(solution)/shard_map/ppermute | solution.py:318
  23.0 2.6 %copy-start.8 = (bf16[512]{0:T(512)(128)(2,1)S(1)}, bf16[512]{0:T(512)(128)(2,1)}, u32[]{:S(2)}) copy-start(bf16[512]{0:T(512)(128)(2,1)} %param.19) | copy-start | bytes 3076
  23.0 31.2 %collective-permute-start.1 = (s32[256,1]{0,1:T(1,128)S(1)}, s32[256,1]{0,1:T(1,128)S(1)}, u32[]{:S(2)}, u32[]{:S(2)}) collective-permute-start(s32[256,1]{0,1:T(1,128)S(1)} %bitcast.42), channel_id=1, source_target_pairs={{0,1},{1,0},{2,3},{3,2},{4,5},{5,4},{6,7},{7,6},{8,9},{9,8},{10,11... | collective-permute-start | bytes 3080 | tf_op jit(solution)/shard_map/ppermute | solution.py:318
  54.9 0.9 copy-start.4
  55.0 1.0 copy-start.6
  64.1 2.9 %copy-start.5 = (bf16[256,1536]{1,0:T(8,128)(2,1)S(1)}, bf16[256,1536]{1,0:T(8,128)(2,1)}, u32[]{:S(2)}) copy-start(bf16[256,1536]{1,0:T(8,128)(2,1)} %copy-done.4) | copy-start | bytes 2359300
  112.7 5.8 %copy-start.2 = (bf16[512,2048]{1,0:T(8,128)(2,1)S(1)}, bf16[512,2048]{1,0:T(8,128)(2,1)}, u32[]{:S(2)}) copy-start(bf16[512,2048]{1,0:T(8,128)(2,1)} %attend.1) | copy-start | bytes 6291460
  115.7 2.8 %collective-permute-start.2 = (bf16[256,2048]{1,0:T(8,128)(2,1)S(1)}, bf16[256,2048]{1,0:T(8,128)(2,1)S(1)}, u32[]{:S(2)}, u32[]{:S(2)}) collective-permute-start(bf16[256,2048]{1,0:T(8,128)(2,1)S(1)} %broadcast_select_fusion.2), channel_id=1, source_target_pairs={{0,1},{1,0},{2,3},{3,2},{4,5},{5,4},{6,7},{7,6},{8,9},{9,8},{10,11... | collective-permute-start | bytes 3145736 | tf_op jit(solution)/shard_map/ppermute | solution.py:338
  120.6 107.0 %copy-start.1 = (bf16[7168,64]{0,1:T(8,128)(2,1)S(1)}, bf16[7168,64]{0,1:T(8,128)(2,1)}, u32[]{:S(2)}) copy-start(bf16[7168,64]{0,1:T(8,128)(2,1)} %param.20) | copy-start | bytes 2752516
Sparse Core Ops, SparseCore 0:
  26.6 24.6 all-gather.2

commit v3 on v2

--- a/solution.py
+++ b/solution.py
@@ -11,11 +11,6 @@
 NORM_EPS = 1e-6
 
 
-def rms_norm(act_in, gain_vec):
-    inv_rms = lax.rsqrt(jnp.mean(act_in * act_in, axis=-1, keepdims=True) + NORM_EPS)
-    return act_in * inv_rms * gain_vec.astype(jnp.float32)
-
-
 def rope_tables(pos_vals, rope_dim):
     half_dim = rope_dim // 2
     inv_freq = ROPE_BASE ** (-jnp.arange(half_dim, dtype=jnp.float32) * 2.0 / rope_dim)
@@ -23,19 +18,12 @@
     return jnp.cos(angles), jnp.sin(angles)
 
 
-def apply_rope(act_in, cos_t, sin_t):
-    half_dim = act_in.shape[-1] // 2
-    first_half = act_in[..., :half_dim]
-    second_half = act_in[..., half_dim:]
-    return jnp.concatenate([first_half * cos_t - second_half * sin_t, second_half * cos_t + first_half * sin_t], axis=-1)
-
-
 MESH = pl.DeviceIdType.MESH
 OUT_BLOCK = 512
 W_SLOTS = 3
 
 
-def out_kernel(n_tp, n_blk, o_ref, w_hbm, out_hbm, wbuf, part, recv, ybuf, w_sem, rs_send, rs_recv, ag_send, ag_recv, out_sem):
+def out_kernel(n_tp, n_blk, o_ref, w_hbm, out_hbm, o_all, wbuf, part, recv, ybuf, w_sem, rs_send, rs_recv, ag_send, ag_recv, out_sem, o_send, o_recv):
     me = lax.axis_index('tp')
     right = lax.rem(me + 1, n_tp)
     left = lax.rem(me + n_tp - 1, n_tp)
@@ -66,16 +54,33 @@
 
     for b in range(W_SLOTS):
         w_copy(b).start()
+    ctx = lax.axis_index('ctx')
+    half_id = lax.rem(ctx, 2)
+    mate = ctx + 1 - 2 * half_id
+    half = o_all.shape[1] // 2
     barrier = pltpu.get_barrier_semaphore()
     for neighbour in peer:
         pl.semaphore_signal(barrier, inc=1, device_id={'tp': neighbour}, device_id_type=MESH)
-    pl.semaphore_wait(barrier, 2)
+    pl.semaphore_signal(barrier, inc=1, device_id={'ctx': mate}, device_id_type=MESH)
+    pl.semaphore_wait(barrier, 3)
+    own_at = (half_id, 3 - half_id)
+    mate_at = (1 - half_id, 2 + half_id)
+    o_share = [pltpu.make_async_remote_copy(src_ref=o_ref.at[pl.ds(pl.multiple_of(mate_at[s] * half, half), half)], dst_ref=o_all.at[half_id, pl.ds(s * half, half)],
+                                            send_sem=o_send.at[s], recv_sem=o_recv.at[s], device_id={'ctx': mate}, device_id_type=MESH) for s in range(2)]
+    for s in range(2):
+        o_share[s].start()
+    for s in range(2):
+        o_all[half_id, s * half:(s + 1) * half] = o_ref[pl.ds(pl.multiple_of(own_at[s] * half, half), half), :]
+    for s in range(2):
+        o_share[s].wait()
 
     def product(p, _):
         for way in range(2):
             b = 2 * p + way
             w_copy(b).wait()
-            res = jnp.dot(o_ref[...], wbuf[lax.rem(b, W_SLOTS)], preferred_element_type=jnp.float32)
+            slot = lax.rem(b, W_SLOTS)
+            depth = o_all.shape[2]
+            res = jnp.dot(o_all[0], wbuf[slot, 0:depth], preferred_element_type=jnp.float32) + jnp.dot(o_all[1], wbuf[slot, depth:], preferred_element_type=jnp.float32)
             part[b] = res.reshape(n_tp, rows, blk)
 
             @pl.when(b + W_SLOTS < n_blk)
@@ -155,8 +160,8 @@
 
 
 def project_out(attn_out, w_o, n_tp):
-    tok_count, depth = attn_out.shape
-    width = w_o.shape[1]
+    tok_count = attn_out.shape[0] // 2
+    depth, width = w_o.shape
     n_blk = width // OUT_BLOCK
     assert n_tp == 4 and n_blk % 2 == 0 and width % OUT_BLOCK == 0
     rows = tok_count // n_tp
@@ -167,31 +172,233 @@
         in_specs=[pl.BlockSpec(memory_space=pltpu.VMEM), pl.BlockSpec(memory_space=pl.ANY)],
         out_specs=pl.BlockSpec(memory_space=pl.ANY),
         scratch_shapes=[
+            pltpu.VMEM((2, tok_count, depth // 2), jnp.bfloat16),
             pltpu.VMEM((W_SLOTS, depth, OUT_BLOCK), jnp.bfloat16),
             pltpu.VMEM((n_blk, n_tp, rows, OUT_BLOCK), jnp.float32),
             pltpu.VMEM((n_blk, n_tp - 1, rows, OUT_BLOCK), jnp.float32),
             pltpu.VMEM((n_tp, n_blk, rows, OUT_BLOCK), jnp.bfloat16),
-            dma((W_SLOTS,)), dma((n_blk, n_tp - 1)), dma((n_blk, n_tp - 1)), dma((n_blk, 3)), dma((n_blk, 3)), dma((n_tp, n_blk)),
+            dma((W_SLOTS,)), dma((n_blk, n_tp - 1)), dma((n_blk, n_tp - 1)), dma((n_blk, 3)), dma((n_blk, 3)), dma((n_tp, n_blk)), dma((2,)), dma((2,)),
         ],
         compiler_params=pltpu.CompilerParams(collective_id=1, has_side_effects=True, vmem_limit_bytes=60 * 1024 * 1024),
         name='out_proj',
     )(attn_out, w_o)
 
 
+K_CHUNKS = 4
+Q_BLOCK = 256
+Q_SLOTS = 4
+
+
+def latent_kernel(n_ctx, x_hbm, wdkv_hbm, wkr_hbm, wdq_hbm, wuq_hbm, wqr_hbm, gq_ref, gkv_ref, tab_ref, tabk_ref, lat_hbm, q_ref,
+                  x_v, wdkv, wkr, wdq, wuq, wqr, kv_acc, kr_acc, cq_acc, cq_all, tab_all, lat,
+                  x_sem, dkv_sem, kr_sem, dq_sem, uq_sem, qr_sem, ring_send, ring_recv, mate_send, mate_recv, cq_send, cq_recv, tab_send, tab_recv, lat_sem):
+    me = lax.axis_index('ctx')
+    part = lax.rem(me, 2)
+    mate = me + 1 - 2 * part
+    right = lax.rem(me + 2, n_ctx)
+    left = lax.rem(me + n_ctx - 2, n_ctx)
+    far = lax.rem(me + 4, n_ctx)
+    f32 = jnp.float32
+    rows, width = x_v.shape
+    half = rows // 2
+    rank = kv_acc.shape[1]
+    rope = kr_acc.shape[1]
+    rot = rope // 2
+    kc = width // K_CHUNKS
+    n_dq = cq_acc.shape[1] // Q_BLOCK
+    n_uq, n_qr = wuq.shape[0], wqr.shape[0]
+    nope = q_ref.shape[1] - rope
+
+    def kcols(k):
+        return pl.ds(k * kc, kc)
+
+    x_copy = [pltpu.make_async_copy(x_hbm.at[:, kcols(k)], x_v.at[:, kcols(k)], x_sem.at[k]) for k in range(K_CHUNKS)]
+    dkv_copy = [pltpu.make_async_copy(wdkv_hbm.at[kcols(k)], wdkv.at[kcols(k)], dkv_sem.at[k]) for k in range(K_CHUNKS)]
+    kr_copy = [pltpu.make_async_copy(wkr_hbm.at[kcols(k)], wkr.at[kcols(k)], kr_sem.at[k]) for k in range(K_CHUNKS)]
+    dq_copy = [pltpu.make_async_copy(wdq_hbm.at[:, pl.ds(b * Q_BLOCK, Q_BLOCK)], wdq.at[b % Q_SLOTS], dq_sem.at[b % Q_SLOTS]) for b in range(n_dq)]
+    uq_copy = [pltpu.make_async_copy(wuq_hbm.at[:, pl.ds(pl.multiple_of((part * n_uq + b) * Q_BLOCK, Q_BLOCK), Q_BLOCK)], wuq.at[b], uq_sem.at[b]) for b in range(n_uq)]
+    qr_copy = [pltpu.make_async_copy(wqr_hbm.at[:, pl.ds(pl.multiple_of((part * n_qr + b) * Q_BLOCK, Q_BLOCK), Q_BLOCK)], wqr.at[b], qr_sem.at[b]) for b in range(n_qr)]
+
+    def piece(dev, sub):
+        return dev if sub == 0 else 2 * n_ctx - 1 - dev
+
+    def send(src, dst, send_sem, recv_sem, dev):
+        return pltpu.make_async_remote_copy(src_ref=src, dst_ref=dst, send_sem=send_sem, recv_sem=recv_sem, device_id={'ctx': dev}, device_id_type=MESH)
+
+    def ring(slot, src_dev, sub, dev):
+        return send(lat.at[piece(src_dev, sub)], lat.at[piece(src_dev, sub)], ring_send.at[slot], ring_recv.at[slot], dev)
+
+    def share(slot, src_dev, sub):
+        return send(lat.at[piece(src_dev, sub)], lat.at[piece(src_dev, sub)], mate_send.at[slot], mate_recv.at[slot], mate)
+
+    to_right = [ring(0, me, 0, right), ring(1, me, 1, right)]
+    to_left = [ring(2, me, 0, left), ring(3, me, 1, left)]
+    on_right = ring(4, left, 0, right)
+    on_left = ring(5, right, 1, left)
+    order = [(me, 0), (me, 1), (left, 0), (right, 1), (left, 1), (right, 0), (far, 0), (far, 1)]
+    shares = [share(i, d, s) for i, (d, s) in enumerate(order)]
+    slot_of = (part, 3 - part)
+    cq_share = [send(cq_all.at[slot_of[s]], cq_all.at[slot_of[s]], cq_send.at[s], cq_recv.at[s], mate) for s in range(2)]
+
+    def lanes(s):
+        return pl.ds(pl.multiple_of(slot_of[s] * half, half), half)
+
+    tab_share = [send(tab_all.at[:, lanes(s)], tab_all.at[:, lanes(s)], tab_send.at[s], tab_recv.at[s], mate) for s in range(2)]
+
+    for k in range(K_CHUNKS):
+        x_copy[k].start()
+        dkv_copy[k].start()
+        kr_copy[k].start()
+    for b in range(Q_SLOTS):
+        dq_copy[b].start()
+    barrier = pltpu.get_barrier_semaphore()
+    for dev in (mate, right, left):
+        pl.semaphore_signal(barrier, inc=1, device_id={'ctx': dev}, device_id_type=MESH)
+    for s in range(2):
+        tab_all[:, lanes(s)] = tab_ref[:, s * half:(s + 1) * half]
+
+    for k in range(K_CHUNKS):
+        cols = slice(k * kc, (k + 1) * kc)
+        x_copy[k].wait()
+        dkv_copy[k].wait()
+        kr_copy[k].wait()
+        kv_new = jnp.dot(x_v[:, cols], wdkv[cols], preferred_element_type=f32)
+        kr_new = jnp.dot(x_v[:, cols], wkr[cols], preferred_element_type=f32)
+        if k == 0:
+            kv_acc[...] = kv_new
+            kr_acc[...] = kr_new
+        else:
+            kv_acc[...] += kv_new
+            kr_acc[...] += kr_new
+    kv = kv_acc[...]
+    c_kv = (kv * lax.rsqrt(jnp.mean(kv * kv, axis=-1, keepdims=True) + NORM_EPS) * gkv_ref[...]).astype(jnp.bfloat16)
+    kr = kr_acc[...]
+    cos_k, sin_k = tabk_ref[:, :rot], tabk_ref[:, rot:]
+    k_lo = (kr[:, :rot] * cos_k - kr[:, rot:] * sin_k).astype(jnp.bfloat16)
+    k_hi = (kr[:, rot:] * cos_k + kr[:, :rot] * sin_k).astype(jnp.bfloat16)
+    pad = jnp.zeros((half, lat.shape[2] - rank - rope), jnp.bfloat16)
+    for s in range(2):
+        own = slice(s * half, (s + 1) * half)
+        lat[piece(me, s), :, 0:rank] = c_kv[own]
+        lat[piece(me, s), :, rank:] = jnp.concatenate([k_lo[own], k_hi[own], pad], axis=1)
+
+    pl.semaphore_wait(barrier, 3)
+    for s in range(2):
+        to_right[s].start()
+        to_left[1 - s].start()
+    for s in range(2):
+        tab_share[s].start()
+        shares[s].start()
+
+    for b in range(n_dq):
+        dq_copy[b].wait()
+        cq_acc[:, b * Q_BLOCK:(b + 1) * Q_BLOCK] = jnp.dot(x_v[...], wdq[b % Q_SLOTS], preferred_element_type=f32)
+        if b + Q_SLOTS < n_dq:
+            dq_copy[b + Q_SLOTS].start()
+        if b == 1:
+            for c in qr_copy + uq_copy:
+                c.start()
+    for s in range(2):
+        own = slice(s * half, (s + 1) * half)
+        cq = cq_acc[own]
+        cq_all[slot_of[s]] = (cq * lax.rsqrt(jnp.mean(cq * cq, axis=-1, keepdims=True) + NORM_EPS) * gq_ref[...]).astype(jnp.bfloat16)
+        cq_share[s].start()
+
+    to_right[0].wait_recv()
+    on_right.start()
+    to_left[1].wait_recv()
+    on_left.start()
+    shares[2].start()
+    shares[3].start()
+    for s in range(2):
+        cq_share[s].wait_recv()
+        tab_share[s].wait_recv()
+
+    def rotary(b, _):
+        pltpu.make_async_copy(wqr_hbm.at[:, pl.ds(0, Q_BLOCK)], wqr.at[b], qr_sem.at[b]).wait()
+        res = jnp.dot(cq_all[...].reshape(2 * rows, cq_all.shape[2]), wqr[b], preferred_element_type=f32).T
+        cos_q, sin_q = tab_all[0:rot], tab_all[rot:rope]
+        for i in range(Q_BLOCK // rope):
+            lo = res[i * rope:i * rope + rot]
+            hi = res[i * rope + rot:(i + 1) * rope]
+            h = b * (Q_BLOCK // rope) + i
+            q_ref[h, nope:nope + rot, :] = (lo * cos_q - hi * sin_q).astype(jnp.bfloat16)
+            q_ref[h, nope + rot:nope + rope, :] = (hi * cos_q + lo * sin_q).astype(jnp.bfloat16)
+        return 0
+
+    lax.fori_loop(0, n_qr, rotary, 0)
+    to_right[1].wait_recv()
+    to_left[0].wait_recv()
+    shares[4].start()
+    shares[5].start()
+
+    def plain(b, _):
+        pltpu.make_async_copy(wuq_hbm.at[:, pl.ds(0, Q_BLOCK)], wuq.at[b], uq_sem.at[b]).wait()
+        res = jnp.dot(cq_all[...].reshape(2 * rows, cq_all.shape[2]), wuq[b], preferred_element_type=f32).astype(jnp.bfloat16).T
+        for i in range(Q_BLOCK // nope):
+            q_ref[b * (Q_BLOCK // nope) + i, 0:nope, :] = res[i * nope:(i + 1) * nope]
+        return 0
+
+    lax.fori_loop(0, n_uq // 2, plain, 0)
+    on_right.wait_recv()
+    on_left.wait_recv()
+    shares[6].start()
+    shares[7].start()
+    lax.fori_loop(n_uq // 2, n_uq, plain, 0)
+    for i in range(8):
+        shares[i].wait_recv()
+    out = pltpu.make_async_copy(lat, lat_hbm, lat_sem)
+    out.start()
+    for c in to_right + to_left + [on_right, on_left] + shares + cq_share + tab_share:
+        c.wait_send()
+    out.wait()
+
+
+def latents(tok_x, w_dkv, w_kr, w_dq, w_uq, w_qr, g_q, g_kv, tab, n_ctx):
+    rows, width = tok_x.shape
+    rank, rope, q_rank = w_dkv.shape[1], w_kr.shape[1], w_dq.shape[1]
+    heads = w_qr.shape[1] // rope // 2
+    nope = w_uq.shape[1] // heads // 2
+    bf16, f32 = jnp.bfloat16, jnp.float32
+    vmem = pl.BlockSpec(memory_space=pltpu.VMEM)
+    hbm = pl.BlockSpec(memory_space=pl.ANY)
+    dma = pltpu.SemaphoreType.DMA
+    n_uq, n_qr = heads * nope // Q_BLOCK, heads * rope // Q_BLOCK
+    lat_width = rank + 128
+    assert n_ctx == 8 and rope <= 128
+    lat, q_t = pl.pallas_call(
+        functools.partial(latent_kernel, n_ctx),
+        out_shape=[jax.ShapeDtypeStruct((2 * n_ctx, rows // 2, lat_width), bf16), jax.ShapeDtypeStruct((heads, nope + rope, 2 * rows), bf16)],
+        in_specs=[hbm] * 6 + [vmem] * 4,
+        out_specs=[hbm, vmem],
+        scratch_shapes=[
+            pltpu.VMEM((rows, width), bf16), pltpu.VMEM((width, rank), bf16), pltpu.VMEM((width, rope), bf16), pltpu.VMEM((Q_SLOTS, width, Q_BLOCK), bf16),
+            pltpu.VMEM((n_uq, q_rank, Q_BLOCK), bf16), pltpu.VMEM((n_qr, q_rank, Q_BLOCK), bf16),
+            pltpu.VMEM((rows, rank), f32), pltpu.VMEM((rows, rope), f32), pltpu.VMEM((rows, q_rank), f32),
+            pltpu.VMEM((4, rows // 2, q_rank), bf16), pltpu.VMEM((rope, 2 * rows), f32), pltpu.VMEM((2 * n_ctx, rows // 2, lat_width), bf16),
+            dma((K_CHUNKS,)), dma((K_CHUNKS,)), dma((K_CHUNKS,)), dma((Q_SLOTS,)), dma((n_uq,)), dma((n_qr,)),
+            dma((6,)), dma((6,)), dma((8,)), dma((8,)), dma((2,)), dma((2,)), dma((2,)), dma((2,)), dma,
+        ],
+        compiler_params=pltpu.CompilerParams(collective_id=2, has_side_effects=True, vmem_limit_bytes=62 * 1024 * 1024),
+        name='latents',
+    )(tok_x, w_dkv, w_kr, w_dq, w_uq, w_qr, g_q.astype(f32)[None], g_kv.astype(f32)[None], tab.T, tab)
+    return lat.reshape(n_ctx * rows, lat_width), q_t
+
+
 KEY_BLOCK = 256
 
 
-def attend_kernel(n_ctx, scale, q_ref, lat_ref, kpe_ref, wuk_hbm, wuv_hbm, o_ref, wuk, wuv, wuv_t, lat_t, kcat, v_t, s_buf, p_buf, w_sem):
+def attend_kernel(n_ctx, scale, q_ref, lat_ref, wuk_hbm, wuv_hbm, o_ref, wuk, wuv, wuv_t, lat_t, kcat, v_t, s_buf, p_buf, w_sem):
     me = lax.axis_index('ctx')
     col = me // 2
     part = lax.rem(me, 2)
     n_col = n_ctx // 2
     heads = q_ref.shape[0]
     n_pair = heads // 2
-    rank = lat_ref.shape[1]
+    rank = wuk.shape[1]
     v_dim = v_t.shape[0] // 2
     nope = wuk.shape[2] // 2
-    rope = kpe_ref.shape[1]
+    rope = q_ref.shape[1] - nope
     exp_scale = scale * 1.4426950408889634
 
     def w_copy(src, dst, which, hp):
@@ -202,9 +409,9 @@
         w_copy(wuk_hbm, wuk, 0, hp).start()
         w_copy(wuv_hbm, wuv, 1, hp).start()
     for blk in range(lat_ref.shape[0] // KEY_BLOCK):
-        lat_t[:, blk * KEY_BLOCK:(blk + 1) * KEY_BLOCK] = lat_ref[blk * KEY_BLOCK:(blk + 1) * KEY_BLOCK].T
+        lat_t[:, blk * KEY_BLOCK:(blk + 1) * KEY_BLOCK] = lat_ref[blk * KEY_BLOCK:(blk + 1) * KEY_BLOCK, 0:rank].T
         for g in range(2):
-            kcat[g, blk * KEY_BLOCK:(blk + 1) * KEY_BLOCK, nope:nope + rope] = kpe_ref[blk * KEY_BLOCK:(blk + 1) * KEY_BLOCK]
+            kcat[g, blk * KEY_BLOCK:(blk + 1) * KEY_BLOCK, nope:nope + rope] = lat_ref[blk * KEY_BLOCK:(blk + 1) * KEY_BLOCK, rank:rank + rope]
     for hp in range(n_pair):
         w_copy(wuk_hbm, wuk, 0, hp).wait()
         w_copy(wuv_hbm, wuv, 1, hp).wait()
@@ -219,7 +426,7 @@
         def pair_step(hp, _):
             for blk in range(n_blk):
                 rows = slice(blk * KEY_BLOCK, (blk + 1) * KEY_BLOCK)
-                k2 = jnp.dot(lat_ref[rows], wuk[hp], preferred_element_type=jnp.float32).astype(jnp.bfloat16)
+                k2 = jnp.dot(lat_ref[rows, 0:rank], wuk[hp], preferred_element_type=jnp.float32).astype(jnp.bfloat16)
                 kcat[0, rows, 0:nope] = k2[:, :nope]
                 kcat[1, rows, 0:nope] = k2[:, nope:]
                 v_t[:, rows] = jnp.dot(wuv_t[hp], lat_t[:, rows], preferred_element_type=jnp.float32).astype(jnp.bfloat16)
@@ -257,11 +464,11 @@
         pl.when(col == v)(functools.partial(phase, 1, 2 * n_col - v))
 
 
-def attend(q_t, lat, kpe, w_uk, w_uv, n_ctx, scale):
+def attend(q_t, lat, w_uk, w_uv, n_ctx, scale):
     heads, q_dim, q_count = q_t.shape
-    keys, rank = lat.shape
-    rope = kpe.shape[1]
-    nope = q_dim - rope
+    keys, rank = lat.shape[0], w_uk.shape[0]
+    nope = w_uk.shape[1] // (2 * heads)
+    rope = q_dim - nope
     v_dim = w_uv.shape[1] // (2 * heads)
     n_pair = heads // 2
     bf16, f32 = jnp.bfloat16, jnp.float32
@@ -271,7 +478,7 @@
     return pl.pallas_call(
         functools.partial(attend_kernel, n_ctx, scale),
         out_shape=jax.ShapeDtypeStruct((q_count, heads * v_dim), bf16),
-        in_specs=[vmem, vmem, vmem, hbm, hbm],
+        in_specs=[vmem, vmem, hbm, hbm],
         out_specs=vmem,
         scratch_shapes=[
             pltpu.VMEM((n_pair, rank, 2 * nope), bf16), pltpu.VMEM((n_pair, rank, 2 * v_dim), bf16), pltpu.VMEM((n_pair, 2 * v_dim, rank), bf16),
@@ -281,7 +488,7 @@
         ],
         compiler_params=pltpu.CompilerParams(vmem_limit_bytes=60 * 1024 * 1024),
         name='attend',
-    )(q_t, lat, kpe, w_uk, w_uv)
+    )(q_t, lat, w_uk, w_uv)
 
 
 def solution(mesh):
@@ -293,51 +500,15 @@
     row_spec = P('tp', None)
 
     def local_step(tok_x, tok_pos, w_dq, g_q, w_uq, w_qr, w_dkv, g_kv, w_kr, w_uk, w_uv, w_o):
-        my_index = lax.axis_index('ctx')
-        half_len = tok_x.shape[0] // 2
         rope_dim = w_kr.shape[1]
         heads_loc = w_qr.shape[1] // rope_dim
         nope_dim = w_uq.shape[1] // heads_loc
-        value_dim = w_uv.shape[1] // heads_loc
         score_scale = (nope_dim + rope_dim) ** -0.5
         n_ctx = mesh.shape['ctx']
-        heads_half = heads_loc // 2
-        part = my_index % 2
-        swap = [(i, i ^ 1) for i in range(n_ctx)]
-        cos_t, sin_t = rope_tables(tok_pos, rope_dim)
-        c_kv = rms_norm(jnp.dot(tok_x, w_dkv, preferred_element_type=jnp.float32), g_kv).astype(jnp.bfloat16)
-        k_pe = apply_rope(jnp.dot(tok_x, w_kr, preferred_element_type=jnp.float32), cos_t, sin_t).astype(jnp.bfloat16)
-        c_q = rms_norm(jnp.dot(tok_x, w_dq, preferred_element_type=jnp.float32), g_q).astype(jnp.bfloat16)
-
-        def in_order(rows):
-            rows = lax.all_gather(rows, 'ctx')
-            halves = rows.reshape((n_ctx, 2, half_len) + rows.shape[2:])
-            return jnp.concatenate([halves[:, 0], halves[::-1, 1]], axis=0).reshape((-1,) + rows.shape[2:])
-
-        def pair_rows(own):
-            other = lax.ppermute(own, 'ctx', swap)
-            even = jnp.where(part == 0, own, other)
-            odd = jnp.where(part == 0, other, own)
-            return jnp.concatenate([even[:half_len], odd[:half_len], odd[half_len:], even[half_len:]], axis=0)
-
-        lat_all = in_order(c_kv)
-        kpe_all = in_order(k_pe)
-        c_q2 = pair_rows(c_q)
-        cos_2, sin_2 = rope_tables(pair_rows(tok_pos[:, None])[:, 0], rope_dim)
-        w_uq_half = lax.dynamic_slice_in_dim(w_uq, part * heads_half * nope_dim, heads_half * nope_dim, axis=1)
-        w_qr_half = lax.dynamic_slice_in_dim(w_qr, part * heads_half * rope_dim, heads_half * rope_dim, axis=1)
-        q_nope = jnp.dot(c_q2, w_uq_half, preferred_element_type=jnp.float32).astype(jnp.bfloat16).reshape(-1, heads_half, nope_dim)
-        q_rot = jnp.dot(c_q2, w_qr_half, preferred_element_type=jnp.float32).reshape(-1, heads_half, rope_dim)
-        q_pe = apply_rope(q_rot, cos_2[:, None, :], sin_2[:, None, :]).astype(jnp.bfloat16)
-        q_t = jnp.transpose(jnp.concatenate([q_nope, q_pe], axis=-1), (1, 2, 0))
-        o_half = attend(q_t, lat_all, kpe_all, w_uk, w_uv, n_ctx, score_scale)
-        quarter = [o_half[i * half_len:(i + 1) * half_len] for i in range(4)]
-        o_even = jnp.concatenate([quarter[0], quarter[3]], axis=0)
-        o_odd = jnp.concatenate([quarter[1], quarter[2]], axis=0)
-        mine = jnp.where(part == 0, o_even, o_odd)
-        theirs = lax.ppermute(jnp.where(part == 0, o_odd, o_even), 'ctx', swap)
-        attn_out = jnp.concatenate([jnp.where(part == 0, mine, theirs), jnp.where(part == 0, theirs, mine)], axis=1)
-        return project_out(attn_out, w_o, mesh.shape['tp'])
+        tab = jnp.concatenate(rope_tables(tok_pos, rope_dim), axis=-1)
+        lat, q_t = latents(tok_x, w_dkv, w_kr, w_dq, w_uq, w_qr, g_q, g_kv, tab, n_ctx)
+        o_half = attend(q_t, lat, w_uk, w_uv, n_ctx, score_scale)
+        return project_out(o_half, w_o, mesh.shape['tp'])
 
     return jax.shard_map(local_step, mesh=mesh,
                          in_specs=(tok_spec, pos_spec, full_mat, full_vec, col_spec, col_spec, full_mat, full_vec, full_mat, col_spec, col_spec, row_spec),

time: 237 us -> 189 us (0.80)
  Pallas kernels: 139 us -> 176 us
  matrix products: 31.9 us -> 0 us
  blocking collectives: 22.2 us -> 0 us
  between operations: 13.7 us -> 0.04 us
  other arithmetic: 11.9 us -> 3.35 us
  local copies, waits for them, and re-layouts: 12.2 us -> 8.68 us
  waiting for transfers between devices: 2.69 us -> 0 us
    pallas_call x0 -> x1, Pallas kernels: none -> 35.5 us  [latents(): pl.pallas_call(functools.partial(latent_kernel, n_ctx), out_shape=[jax.Sh...]
    dot_general x5 -> x0, matrix products: 31.9 us -> none  [the longest x1 14.5 us: local_step(): jnp.dot(tok_x, w_dq, preferred_element_type=jnp.float32)]
    all_gather x1 -> x0, blocking collectives: 22.2 us -> none  [in_order(): rows = lax.all_gather(rows, 'ctx')]
    concatenate x5 -> x1, other arithmetic: 4.16 us -> 0.76 us  [local_step(): tab = jnp.concatenate(rope_tables(tok_pos, rope_dim), axis=-1)]
    convert_element_type x1 -> x0, local copies, waits for them, and re-layouts: 2.93 us -> none  [local_step(): jnp.dot(c_q2, w_uq_half, preferred_element_type=jnp.float32)]
    convert_element_type x4 -> x0, other arithmetic: 2.66 us -> none  [the longest x1 1.08 us: local_step(): rms_norm(jnp.dot(tok_x, w_dq, preferred_element_type=jnp.float32), g_q)]
    select_n x4 -> x0, other arithmetic: 2.64 us -> none  [the longest x1 1.62 us: local_step(): theirs = lax.ppermute(jnp.where(part == 0, o_odd, o_even), 'ctx', swap)]
    ppermute x3 -> x0, waiting for transfers between devices: 2.64 us -> none  [the longest x1 2.63 us: local_step(): theirs = lax.ppermute(jnp.where(part == 0, o_odd, o_even), 'ctx', swap)]
  transfers between devices with their start and end apart: 4 -> 0, of which waited for: 1 -> 0; matrix products, arithmetic and copies ran while one was open for 11% -> 0% of each run, Pallas kernels for 0% -> 0%
where the time goes in v3:
time: 189 us; the launch traced here: 188 us
  Pallas kernels  176 us (93%)
  local copies, waits for them, and re-layouts  8.68 us (5%)
  other arithmetic  3.35 us (2%)
    pallas_call x1, Pallas kernels, project_out(): pl.pallas_call(functools.partial(out_kernel, n_tp, n_blk), out_shape=jax....  105 us
    pallas_call x1, Pallas kernels, attend(): pl.pallas_call(functools.partial(attend_kernel, n_ctx, scale), out_shape=...  36.2 us
    pallas_call x1, Pallas kernels, latents(): pl.pallas_call(functools.partial(latent_kernel, n_ctx), out_shape=[jax.Sh...  35.5 us
    unnamed x2, local copies, waits for them, and re-layouts  6.69 us

profile of v3, /device:TPU:102, one launch (start us, length us, event | category | flops | bytes accessed | tf_op | source)
XLA Modules:
  0.0 188.3 jit_solution(16648776730371401135)
XLA Ops:
  0.0 0.7 convert_element_type.2
  0.7 1.3 broadcast_in_dim.17
  2.0 1.3 reshape.11.gq_ref
  3.2 0.5 multiply_cosine_fusion
  3.8 0.1 fusion
  3.9 0.8 pad_maximum_fusion.tabk_ref
  4.6 0.7 copy.17.tab_ref
  5.4 2.6 %copy.16.wkr_hbm = bf16[7168,64]{1,0:T(8,128)(2,1)} copy(bf16[7168,64]{0,1:T(8,128)(2,1)} %param.20) | data formatting | bytes 1835008 | tf_op args[8]
  7.9 35.5 %latents.1 = (bf16[16,128,640]{2,1,0:T(8,128)(2,1)}, bf16[16,192,512]{2,1,0:T(8,128)(2,1)}) custom-call(bf16[256,7168]{1,0:T(8,128)(2,1)} %x_hbm.1, bf16[7168,512]{1,0:T(8,128)(2,1)} %wdkv_hbm.1, bf16[7168,64]{1,0:T(8,128)(2,1)} %copy.16.wkr_hbm, bf16[7168,1536]{1,0:T(8,128)(2,1)} %wdq_hbm.1, bf16[1536,4096]{1,0:T(8,128)(2,1)} %wuq_hbm.1, ...), custom_call_target="tpu_custom_call" | custom-call | tf_op jit(solution)/shard_map/latents/pallas_call | solution.py:369
  43.4 36.2 %attend.1.o_ref = bf16[512,2048]{1,0:T(8,128)(2,1)} custom-call(bf16[16,192,512]{2,1,0:T(8,128)(2,1)} %get-tuple-element.7.q_ref, bf16[2048,640]{1,0:T(8,128)(2,1)} %bitcast.4, bf16[512,4096]{1,0:T(8,128)(2,1)} %wuk_hbm.1, bf16[512,4096]{1,0:T(8,128)(2,1)} %wuv_hbm.1), custom_call_target="tpu_custom_call" | custom-call | tf_op jit(solution)/shard_map/attend/pallas_call | solution.py:478
  79.6 104.6 %out_proj.1 = bf16[256,7168]{1,0:T(8,128)(2,1)} custom-call(bf16[512,2048]{1,0:T(8,128)(2,1)} %attend.1.o_ref, bf16[4096,7168]{1,0:T(8,128)(2,1)} %w_hbm.1), custom_call_target="tpu_custom_call" | custom-call | tf_op jit(solution)/shard_map/out_proj/pallas_call | solution.py:169
  184.2 4.1 %copy.19 = bf16[256,7168]{1,0:T(8,128)(2,1)} copy(bf16[256,7168]{1,0:T(8,128)(2,1)} %out_proj.1) | data formatting | bytes 7340032
  (1 shorter events, 0.0 us)

commit v4 on v3

v4 whole, which is shorter than its diff:
```python
import functools

import jax
import jax.numpy as jnp
from jax import lax
from jax.experimental import pallas as pl
from jax.experimental.pallas import tpu as pltpu
from jax.sharding import PartitionSpec as P

ROPE_BASE = 10000.0
NORM_EPS = 1e-6


def rope_tables(pos_vals, rope_dim):
    half_dim = rope_dim // 2
    inv_freq = ROPE_BASE ** (-jnp.arange(half_dim, dtype=jnp.float32) * 2.0 / rope_dim)
    angles = pos_vals.astype(jnp.float32)[..., None] * inv_freq
    return jnp.cos(angles), jnp.sin(angles)


MESH = pl.DeviceIdType.MESH
KEY_BLOCK = 256
OUT_BLOCK = 512
W_SLOTS = 3
LAG = 3


def mix_kernel(n_tp, n_ctx, n_blk, scale, q_ref, lat_ref, wuk_hbm, wuv_hbm, w_hbm, out_hbm,
               wuk, wuv, wuv_t, lat_t, kcat, v_t, s_buf, p_buf, o_buf, o_all, wbuf, part, recv, ybuf,
               up_sem, w_sem, o_send, o_recv, rs_send, rs_recv, ag_send, ag_recv, out_sem):
    f32, bf16 = jnp.float32, jnp.bfloat16
    ctx = lax.axis_index('ctx')
    col = ctx // 2
    core = lax.rem(ctx, 2)
    mate = ctx + 1 - 2 * core
    n_col = n_ctx // 2
    me = lax.axis_index('tp')
    right = lax.rem(me + 1, n_tp)
    left = lax.rem(me + n_tp - 1, n_tp)
    across = lax.rem(me + 2, n_tp)
    peer = (right, left)
    step_of = (n_tp - 1, 1)
    heads = q_ref.shape[0]
    n_hp = heads // 2
    rank = wuk.shape[1]
    v_dim = v_t.shape[0] // 2
    nope = wuk.shape[2] // 2
    rope = q_ref.shape[1] - nope
    exp_scale = scale * 1.4426950408889634
    blk = wbuf.shape[2]
    rows = part.shape[3]
    n_pair = n_blk // 2
    half = o_all.shape[2]

    def up_copy(src, dst, which, hp):
        cols = dst.shape[2]
        return pltpu.make_async_copy(src.at[:, pl.ds(pl.multiple_of((core * n_hp + hp) * cols, cols), cols)], dst.at[hp], up_sem.at[which, hp])

    def w_copy(i):
        b = lax.rem(i, n_blk)
        slot = lax.rem(i, W_SLOTS)
        return pltpu.make_async_copy(w_hbm.at[:, pl.ds(pl.multiple_of(b * blk, blk), blk)], wbuf.at[slot], w_sem.at[slot])

    def chunk_at(way, hop):
        return lax.rem(me + (hop + 1) * step_of[way], n_tp)

    def rs_first(sel, b, way):
        return pltpu.make_async_remote_copy(src_ref=part.at[sel, b, chunk_at(way, 0)], dst_ref=recv.at[sel, b, 0], send_sem=rs_send.at[sel, b, 0],
                                            recv_sem=rs_recv.at[sel, b, 0], device_id={'tp': peer[way]}, device_id_type=MESH)

    def rs_next(sel, b, way, hop):
        return pltpu.make_async_remote_copy(src_ref=recv.at[sel, b, hop - 1], dst_ref=recv.at[sel, b, hop], send_sem=rs_send.at[sel, b, hop],
                                            recv_sem=rs_recv.at[sel, b, hop], device_id={'tp': peer[way]}, device_id_type=MESH)

    def rs_arrived(sel, b, way, hop):
        pltpu.make_async_remote_copy(src_ref=recv.at[sel, b, hop], dst_ref=recv.at[sel, b, hop], send_sem=rs_send.at[sel, b, hop],
                                     recv_sem=rs_recv.at[sel, b, hop], device_id={'tp': peer[way]}, device_id_type=MESH).wait_recv()

    def ag_copy(sel, b, slot, way, chunk):
        return pltpu.make_async_remote_copy(src_ref=ybuf.at[sel, chunk, b], dst_ref=ybuf.at[sel, chunk, b], send_sem=ag_send.at[sel, b, slot],
                                            recv_sem=ag_recv.at[sel, b, slot], device_id={'tp': peer[way]}, device_id_type=MESH)

    def out_copy(sel, b, chunk):
        return pltpu.make_async_copy(ybuf.at[sel, chunk, b],
                                     out_hbm.at[pl.ds(pl.multiple_of(sel * half + chunk * rows, rows), rows), pl.ds(pl.multiple_of(b * blk, blk), blk)],
                                     out_sem.at[sel, chunk, b])

    own_at = (core, 3 - core)
    mate_at = (1 - core, 2 + core)

    def o_share(sel):
        return pltpu.make_async_remote_copy(src_ref=o_buf.at[pl.ds(pl.multiple_of(mate_at[sel] * half, half), half)], dst_ref=o_all.at[sel, core],
                                            send_sem=o_send.at[sel], recv_sem=o_recv.at[sel], device_id={'ctx': mate}, device_id_type=MESH)

    for hp in range(n_hp):
        up_copy(wuk_hbm, wuk, 0, hp).start()
        up_copy(wuv_hbm, wuv, 1, hp).start()
    for i in range(W_SLOTS):
        w_copy(i).start()
    barrier = pltpu.get_barrier_semaphore()
    for neighbour in peer:
        pl.semaphore_signal(barrier, inc=1, device_id={'tp': neighbour}, device_id_type=MESH)
    pl.semaphore_signal(barrier, inc=1, device_id={'ctx': mate}, device_id_type=MESH)
    for i in range(lat_ref.shape[0] // KEY_BLOCK):
        lat_t[:, i * KEY_BLOCK:(i + 1) * KEY_BLOCK] = lat_ref[i * KEY_BLOCK:(i + 1) * KEY_BLOCK, 0:rank].T
        for g in range(2):
            kcat[g, i * KEY_BLOCK:(i + 1) * KEY_BLOCK, nope:nope + rope] = lat_ref[i * KEY_BLOCK:(i + 1) * KEY_BLOCK, rank:rank + rope]
    for hp in range(n_hp):
        up_copy(wuk_hbm, wuk, 0, hp).wait()
        up_copy(wuv_hbm, wuv, 1, hp).wait()
        wuv_t[hp] = wuv[hp].T
    pl.semaphore_wait(barrier, 3)

    def attend(sel, n_key, serve):
        q_cols = slice(sel * KEY_BLOCK, (sel + 1) * KEY_BLOCK)
        key_i = lax.broadcasted_iota(jnp.int32, (KEY_BLOCK, KEY_BLOCK), 0)
        q_i = lax.broadcasted_iota(jnp.int32, (KEY_BLOCK, KEY_BLOCK), 1)
        visible = key_i <= q_i

        def pair_step(hp, _):
            for i in range(n_key):
                keys = slice(i * KEY_BLOCK, (i + 1) * KEY_BLOCK)
                k2 = jnp.dot(lat_ref[keys, 0:rank], wuk[hp], preferred_element_type=f32).astype(bf16)
                kcat[0, keys, 0:nope] = k2[:, :nope]
                kcat[1, keys, 0:nope] = k2[:, nope:]
                v_t[:, keys] = jnp.dot(wuv_t[hp], lat_t[:, keys], preferred_element_type=f32).astype(bf16)
            top = []
            for g in range(2):
                q_t = q_ref[2 * hp + g, :, q_cols]
                top8 = None
                for i in range(n_key):
                    keys = slice(i * KEY_BLOCK, (i + 1) * KEY_BLOCK)
                    s = jnp.dot(kcat[g, keys, 0:nope + rope], q_t, preferred_element_type=f32)
                    if i == n_key - 1:
                        s = jnp.where(visible, s, -1e30)
                    s_buf[g, keys] = s
                    blk8 = jnp.max(s.reshape(KEY_BLOCK // 8, 8, KEY_BLOCK), axis=0)
                    top8 = blk8 if top8 is None else jnp.maximum(top8, blk8)
                top.append(jnp.max(top8, axis=0, keepdims=True) * exp_scale)
            for g in range(2):
                sum8 = None
                for i in range(n_key):
                    keys = slice(i * KEY_BLOCK, (i + 1) * KEY_BLOCK)
                    p = jnp.exp2(s_buf[g, keys] * exp_scale - top[g])
                    blk8 = jnp.sum(p.reshape(KEY_BLOCK // 8, 8, KEY_BLOCK), axis=0)
                    sum8 = blk8 if sum8 is None else sum8 + blk8
                    p_buf[g, keys] = p.astype(bf16)
                total = jnp.sum(sum8, axis=0, keepdims=True)
                o_t = jnp.dot(v_t[g * v_dim:(g + 1) * v_dim, 0:n_key * KEY_BLOCK], p_buf[g, 0:n_key * KEY_BLOCK], preferred_element_type=f32)
                o_buf[q_cols, pl.ds(pl.multiple_of((2 * hp + g) * v_dim, v_dim), v_dim)] = (o_t / total).T.astype(bf16)
            if serve is not None:
                serve(hp)
            return 0

        lax.fori_loop(0, n_hp, pair_step, 0)

    def exchange(sel):
        o_share(sel).start()
        o_all[sel, core] = o_buf[pl.ds(pl.multiple_of(own_at[sel] * half, half), half), :]
        o_share(sel).wait()

    def product(sel, p):
        for way in range(2):
            b = 2 * p + way
            i = sel * n_blk + b
            slot = lax.rem(i, W_SLOTS)
            w_copy(i).wait()
            depth = o_all.shape[3]
            res = jnp.dot(o_all[sel, 0], wbuf[slot, 0:depth], preferred_element_type=f32) + jnp.dot(o_all[sel, 1], wbuf[slot, depth:], preferred_element_type=f32)
            part[sel, b] = res.reshape(n_tp, rows, blk)

            @pl.when(i + W_SLOTS < 2 * n_blk)
            def _():
                w_copy(i + W_SLOTS).start()

            rs_first(sel, b, way).start()

    def forward(sel, p, hop):
        for way in range(2):
            b = 2 * p + way
            rs_arrived(sel, b, way, hop - 1)
            recv[sel, b, hop - 1] = recv[sel, b, hop - 1] + part[sel, b, chunk_at(way, hop)]
        for way in range(2):
            rs_next(sel, 2 * p + way, way, hop).start()

    def finish(sel, p):
        for way in range(2):
            b = 2 * p + way
            rs_arrived(sel, b, way, n_tp - 2)
            ybuf[sel, me, b] = (recv[sel, b, n_tp - 2] + part[sel, b, me]).astype(ybuf.dtype)
        for way in range(2):
            b = 2 * p + way
            ag_copy(sel, b, 0, 0, me).start()
            ag_copy(sel, b, 1, 1, me).start()
            out_copy(sel, b, me).start()

    def relay(sel, p):
        ag_copy(sel, 2 * p, 0, 0, left).wait_recv()
        ag_copy(sel, 2 * p, 2, 0, left).start()
        ag_copy(sel, 2 * p + 1, 1, 1, right).wait_recv()
        ag_copy(sel, 2 * p + 1, 2, 1, right).start()
        out_copy(sel, 2 * p, left).start()
        out_copy(sel, 2 * p + 1, right).start()

    def drain(sel, p):
        ag_copy(sel, 2 * p, 1, 1, right).wait_recv()
        out_copy(sel, 2 * p, right).start()
        ag_copy(sel, 2 * p + 1, 0, 0, left).wait_recv()
        out_copy(sel, 2 * p + 1, left).start()
        for way in range(2):
            b = 2 * p + way
            ag_copy(sel, b, 2, way, across).wait_recv()
            out_copy(sel, b, across).start()

    def settle(sel, p):
        for way in range(2):
            b = 2 * p + way
            rs_first(sel, b, way).wait_send()
            for hop in range(1, n_tp - 1):
                rs_next(sel, b, way, hop).wait_send()
            ag_copy(sel, b, 0, 0, me).wait_send()
            ag_copy(sel, b, 1, 1, me).wait_send()
            ag_copy(sel, b, 2, way, left if way == 0 else right).wait_send()
            for chunk in range(n_tp):
                out_copy(sel, b, chunk).wait()

    def loop(start, stop, body):
        def step(p, _):
            body(p)
            return 0
        lax.fori_loop(start, stop, step, 0)

    for v in range(n_col):
        pl.when(col == v)(functools.partial(attend, 0, v + 1, None))
    exchange(0)

    def early(p):
        product(0, p)

        @pl.when(p >= LAG)
        def _():
            forward(0, p - LAG, 1)

    loop(0, n_pair, early)
    hop1_left = n_pair - LAG

    def serve(hp):
        for j in range(2):
            n = hop1_left + 2 * hp + j
            pl.when(n < n_pair)(lambda: forward(0, n, 1))
            pl.when((n >= n_pair) & (n < 2 * n_pair))(lambda: forward(0, n - n_pair, 2))
            pl.when((n >= 2 * n_pair) & (n < 3 * n_pair))(lambda: finish(0, n - 2 * n_pair))

    for v in range(n_col):
        pl.when(col == v)(functools.partial(attend, 1, 2 * n_col - v, serve))
    served = min(hop1_left + 2 * n_hp, 3 * n_pair) - 2 * n_pair
    exchange(1)

    def late(p):
        product(1, p)
        pl.when(p + served < n_pair)(lambda: finish(0, p + served))

        @pl.when(p >= LAG)
        def _():
            forward(1, p - LAG, 1)

        relay(0, p)

    loop(0, n_pair, late)
    loop(hop1_left, n_pair, lambda p: forward(1, p, 1))
    loop(0, n_pair, lambda p: forward(1, p, 2))

    def close(p):
        finish(1, p)
        pl.when(p > 0)(lambda: relay(1, p - 1))
        drain(0, p)

    loop(0, n_pair, close)
    relay(1, n_pair - 1)
    loop(0, n_pair, lambda p: drain(1, p))
    o_wait = n_pair
    loop(0, o_wait, lambda p: settle(0, p))
    loop(0, o_wait, lambda p: settle(1, p))


def mix(q_t, lat, w_uk, w_uv, w_o, n_tp, n_ctx, scale):
    heads, q_dim, q_count = q_t.shape
    keys, rank = lat.shape[0], w_uk.shape[0]
    nope = w_uk.shape[1] // (2 * heads)
    rope = q_dim - nope
    v_dim = w_uv.shape[1] // (2 * heads)
    n_hp = heads // 2
    depth, width = w_o.shape
    n_blk = width // OUT_BLOCK
    half = q_count // 4
    rows = half // n_tp
    assert n_tp == 4 and n_blk % 2 == 0 and width % OUT_BLOCK == 0
    assert q_count == 2 * KEY_BLOCK and keys == n_ctx * KEY_BLOCK
    bf16, f32 = jnp.bfloat16, jnp.float32
    vmem = pl.BlockSpec(memory_space=pltpu.VMEM)
    hbm = pl.BlockSpec(memory_space=pl.ANY)
    dma = pltpu.SemaphoreType.DMA
    return pl.pallas_call(
        functools.partial(mix_kernel, n_tp, n_ctx, n_blk, scale),
        out_shape=jax.ShapeDtypeStruct((2 * half, width), bf16),
        in_specs=[vmem, vmem, hbm, hbm, hbm],
        out_specs=hbm,
        scratch_shapes=[
            pltpu.VMEM((n_hp, rank, 2 * nope), bf16), pltpu.VMEM((n_hp, rank, 2 * v_dim), bf16), pltpu.VMEM((n_hp, 2 * v_dim, rank), bf16),
            pltpu.VMEM((rank, keys), bf16), pltpu.VMEM((2, keys, nope + rope), bf16), pltpu.VMEM((2 * v_dim, keys), bf16),
            pltpu.VMEM((2, keys, KEY_BLOCK), f32), pltpu.VMEM((2, keys, KEY_BLOCK), bf16),
            pltpu.VMEM((q_count, heads * v_dim), bf16), pltpu.VMEM((2, 2, half, depth // 2), bf16),
            pltpu.VMEM((W_SLOTS, depth, OUT_BLOCK), bf16),
            pltpu.VMEM((2, n_blk, n_tp, rows, OUT_BLOCK), f32),
            pltpu.VMEM((2, n_blk, n_tp - 1, rows, OUT_BLOCK), f32),
            pltpu.VMEM((2, n_tp, n_blk, rows, OUT_BLOCK), bf16),
            dma((2, n_hp)), dma((W_SLOTS,)), dma((2,)), dma((2,)), dma((2, n_blk, n_tp - 1)), dma((2, n_blk, n_tp - 1)),
            dma((2, n_blk, 3)), dma((2, n_blk, 3)), dma((2, n_tp, n_blk)),
        ],
        compiler_params=pltpu.CompilerParams(collective_id=1, has_side_effects=True, vmem_limit_bytes=63 * 1024 * 1024),
        name='mix',
    )(q_t, lat, w_uk, w_uv, w_o)


K_CHUNKS = 4
Q_BLOCK = 256
Q_SLOTS = 4


def latent_kernel(n_ctx, x_hbm, wdkv_hbm, wkr_hbm, wdq_hbm, wuq_hbm, wqr_hbm, gq_ref, gkv_ref, tab_ref, tabk_ref, lat_hbm, q_ref,
                  x_v, wdkv, wkr, wdq, wuq, wqr, kv_acc, kr_acc, cq_acc, cq_all, tab_all, lat,
                  x_sem, dkv_sem, kr_sem, dq_sem, uq_sem, qr_sem, ring_send, ring_recv, mate_send, mate_recv, cq_send, cq_recv, tab_send, tab_recv, lat_sem):
    me = lax.axis_index('ctx')
    part = lax.rem(me, 2)
    mate = me + 1 - 2 * part
    right = lax.rem(me + 2, n_ctx)
    left = lax.rem(me + n_ctx - 2, n_ctx)
    far = lax.rem(me + 4, n_ctx)
    f32 = jnp.float32
    rows, width = x_v.shape
    half = rows // 2
    rank = kv_acc.shape[1]
    rope = kr_acc.shape[1]
    rot = rope // 2
    kc = width // K_CHUNKS
    n_dq = cq_acc.shape[1] // Q_BLOCK
    n_uq, n_qr = wuq.shape[0], wqr.shape[0]
    nope = q_ref.shape[1] - rope

    def kcols(k):
        return pl.ds(k * kc, kc)

    x_copy = [pltpu.make_async_copy(x_hbm.at[:, kcols(k)], x_v.at[:, kcols(k)], x_sem.at[k]) for k in range(K_CHUNKS)]
    dkv_copy = [pltpu.make_async_copy(wdkv_hbm.at[kcols(k)], wdkv.at[kcols(k)], dkv_sem.at[k]) for k in range(K_CHUNKS)]
    kr_copy = [pltpu.make_async_copy(wkr_hbm.at[kcols(k)], wkr.at[kcols(k)], kr_sem.at[k]) for k in range(K_CHUNKS)]
    dq_copy = [pltpu.make_async_copy(wdq_hbm.at[:, pl.ds(b * Q_BLOCK, Q_BLOCK)], wdq.at[b % Q_SLOTS], dq_sem.at[b % Q_SLOTS]) for b in range(n_dq)]
    uq_copy = [pltpu.make_async_copy(wuq_hbm.at[:, pl.ds(pl.multiple_of((part * n_uq + b) * Q_BLOCK, Q_BLOCK), Q_BLOCK)], wuq.at[b], uq_sem.at[b]) for b in range(n_uq)]
    qr_copy = [pltpu.make_async_copy(wqr_hbm.at[:, pl.ds(pl.multiple_of((part * n_qr + b) * Q_BLOCK, Q_BLOCK), Q_BLOCK)], wqr.at[b], qr_sem.at[b]) for b in range(n_qr)]

    def piece(dev, sub):
        return dev if sub == 0 else 2 * n_ctx - 1 - dev

    def send(src, dst, send_sem, recv_sem, dev):
        return pltpu.make_async_remote_copy(src_ref=src, dst_ref=dst, send_sem=send_sem, recv_sem=recv_sem, device_id={'ctx': dev}, device_id_type=MESH)

    def ring(slot, src_dev, sub, dev):
        return send(lat.at[piece(src_dev, sub)], lat.at[piece(src_dev, sub)], ring_send.at[slot], ring_recv.at[slot], dev)

    def share(slot, src_dev, sub):
        return send(lat.at[piece(src_dev, sub)], lat.at[piece(src_dev, sub)], mate_send.at[slot], mate_recv.at[slot], mate)

    to_right = [ring(0, me, 0, right), ring(1, me, 1, right)]
    to_left = [ring(2, me, 0, left), ring(3, me, 1, left)]
    on_right = ring(4, left, 0, right)
    on_left = ring(5, right, 1, left)
    order = [(me, 0), (me, 1), (left, 0), (right, 1), (left, 1), (right, 0), (far, 0), (far, 1)]
    shares = [share(i, d, s) for i, (d, s) in enumerate(order)]
    slot_of = (part, 3 - part)
    cq_share = [send(cq_all.at[slot_of[s]], cq_all.at[slot_of[s]], cq_send.at[s], cq_recv.at[s], mate) for s in range(2)]

    def lanes(s):
        return pl.ds(pl.multiple_of(slot_of[s] * half, half), half)

    tab_share = [send(tab_all.at[:, lanes(s)], tab_all.at[:, lanes(s)], tab_send.at[s], tab_recv.at[s], mate) for s in range(2)]

    for k in range(K_CHUNKS):
        x_copy[k].start()
        dkv_copy[k].start()
        kr_copy[k].start()
    for b in range(Q_SLOTS):
        dq_copy[b].start()
    barrier = pltpu.get_barrier_semaphore()
    for dev in (mate, right, left):
        pl.semaphore_signal(barrier, inc=1, device_id={'ctx': dev}, device_id_type=MESH)
    for s in range(2):
        tab_all[:, lanes(s)] = tab_ref[:, s * half:(s + 1) * half]

    for k in range(K_CHUNKS):
        cols = slice(k * kc, (k + 1) * kc)
        x_copy[k].wait()
        dkv_copy[k].wait()
        kr_copy[k].wait()
        kv_new = jnp.dot(x_v[:, cols], wdkv[cols], preferred_element_type=f32)
        kr_new = jnp.dot(x_v[:, cols], wkr[cols], preferred_element_type=f32)
        if k == 0:
            kv_acc[...] = kv_new
            kr_acc[...] = kr_new
        else:
            kv_acc[...] += kv_new
            kr_acc[...] += kr_new
    kv = kv_acc[...]
    c_kv = (kv * lax.rsqrt(jnp.mean(kv * kv, axis=-1, keepdims=True) + NORM_EPS) * gkv_ref[...]).astype(jnp.bfloat16)
    kr = kr_acc[...]
    cos_k, sin_k = tabk_ref[:, :rot], tabk_ref[:, rot:]
    k_lo = (kr[:, :rot] * cos_k - kr[:, rot:] * sin_k).astype(jnp.bfloat16)
    k_hi = (kr[:, rot:] * cos_k + kr[:, :rot] * sin_k).astype(jnp.bfloat16)
    pad = jnp.zeros((half, lat.shape[2] - rank - rope), jnp.bfloat16)
    for s in range(2):
        own = slice(s * half, (s + 1) * half)
        lat[piece(me, s), :, 0:rank] = c_kv[own]
        lat[piece(me, s), :, rank:] = jnp.concatenate([k_lo[own], k_hi[own], pad], axis=1)

    pl.semaphore_wait(barrier, 3)
    for s in range(2):
        to_right[s].start()
        to_left[1 - s].start()
    for s in range(2):
        tab_share[s].start()
        shares[s].start()

    for b in range(n_dq):
        dq_copy[b].wait()
        cq_acc[:, b * Q_BLOCK:(b + 1) * Q_BLOCK] = jnp.dot(x_v[...], wdq[b % Q_SLOTS], preferred_element_type=f32)
        if b + Q_SLOTS < n_dq:
            dq_copy[b + Q_SLOTS].start()
        if b == 1:
            for c in qr_copy + uq_copy:
                c.start()
    for s in range(2):
        own = slice(s * half, (s + 1) * half)
        cq = cq_acc[own]
        cq_all[slot_of[s]] = (cq * lax.rsqrt(jnp.mean(cq * cq, axis=-1, keepdims=True) + NORM_EPS) * gq_ref[...]).astype(jnp.bfloat16)
        cq_share[s].start()

    to_right[0].wait_recv()
    on_right.start()
    to_left[1].wait_recv()
    on_left.start()
    shares[2].start()
    shares[3].start()
    for s in range(2):
        cq_share[s].wait_recv()
        tab_share[s].wait_recv()

    def rotary(b, _):
        pltpu.make_async_copy(wqr_hbm.at[:, pl.ds(0, Q_BLOCK)], wqr.at[b], qr_sem.at[b]).wait()
        res = jnp.dot(cq_all[...].reshape(2 * rows, cq_all.shape[2]), wqr[b], preferred_element_type=f32).T
        cos_q, sin_q = tab_all[0:rot], tab_all[rot:rope]
        for i in range(Q_BLOCK // rope):
            lo = res[i * rope:i * rope + rot]
            hi = res[i * rope + rot:(i + 1) * rope]
            h = b * (Q_BLOCK // rope) + i
            q_ref[h, nope:nope + rot, :] = (lo * cos_q - hi * sin_q).astype(jnp.bfloat16)
            q_ref[h, nope + rot:nope + rope, :] = (hi * cos_q + lo * sin_q).astype(jnp.bfloat16)
        return 0

    lax.fori_loop(0, n_qr, rotary, 0)
    to_right[1].wait_recv()
    to_left[0].wait_recv()
    shares[4].start()
    shares[5].start()

    def plain(b, _):
        pltpu.make_async_copy(wuq_hbm.at[:, pl.ds(0, Q_BLOCK)], wuq.at[b], uq_sem.at[b]).wait()
        res = jnp.dot(cq_all[...].reshape(2 * rows, cq_all.shape[2]), wuq[b], preferred_element_type=f32).astype(jnp.bfloat16).T
        for i in range(Q_BLOCK // nope):
            q_ref[b * (Q_BLOCK // nope) + i, 0:nope, :] = res[i * nope:(i + 1) * nope]
        return 0

    lax.fori_loop(0, n_uq // 2, plain, 0)
    on_right.wait_recv()
    on_left.wait_recv()
    shares[6].start()
    shares[7].start()
    lax.fori_loop(n_uq // 2, n_uq, plain, 0)
    for i in range(8):
        shares[i].wait_recv()
    out = pltpu.make_async_copy(lat, lat_hbm, lat_sem)
    out.start()
    for c in to_right + to_left + [on_right, on_left] + shares + cq_share + tab_share:
        c.wait_send()
    out.wait()


def latents(tok_x, w_dkv, w_kr, w_dq, w_uq, w_qr, g_q, g_kv, tab, n_ctx):
    rows, width = tok_x.shape
    rank, rope, q_rank = w_dkv.shape[1], w_kr.shape[1], w_dq.shape[1]
    heads = w_qr.shape[1] // rope // 2
    nope = w_uq.shape[1] // heads // 2
    bf16, f32 = jnp.bfloat16, jnp.float32
    vmem = pl.BlockSpec(memory_space=pltpu.VMEM)
    hbm = pl.BlockSpec(memory_space=pl.ANY)
    dma = pltpu.SemaphoreType.DMA
    n_uq, n_qr = heads * nope // Q_BLOCK, heads * rope // Q_BLOCK
    lat_width = rank + 128
    assert n_ctx == 8 and rope <= 128
    lat, q_t = pl.pallas_call(
        functools.partial(latent_kernel, n_ctx),
        out_shape=[jax.ShapeDtypeStruct((2 * n_ctx, rows // 2, lat_width), bf16), jax.ShapeDtypeStruct((heads, nope + rope, 2 * rows), bf16)],
        in_specs=[hbm] * 6 + [vmem] * 4,
        out_specs=[hbm, vmem],
        scratch_shapes=[
            pltpu.VMEM((rows, width), bf16), pltpu.VMEM((width, rank), bf16), pltpu.VMEM((width, rope), bf16), pltpu.VMEM((Q_SLOTS, width, Q_BLOCK), bf16),
            pltpu.VMEM((n_uq, q_rank, Q_BLOCK), bf16), pltpu.VMEM((n_qr, q_rank, Q_BLOCK), bf16),
            pltpu.VMEM((rows, rank), f32), pltpu.VMEM((rows, rope), f32), pltpu.VMEM((rows, q_rank), f32),
            pltpu.VMEM((4, rows // 2, q_rank), bf16), pltpu.VMEM((rope, 2 * rows), f32), pltpu.VMEM((2 * n_ctx, rows // 2, lat_width), bf16),
            dma((K_CHUNKS,)), dma((K_CHUNKS,)), dma((K_CHUNKS,)), dma((Q_SLOTS,)), dma((n_uq,)), dma((n_qr,)),
            dma((6,)), dma((6,)), dma((8,)), dma((8,)), dma((2,)), dma((2,)), dma((2,)), dma((2,)), dma,
        ],
        compiler_params=pltpu.CompilerParams(collective_id=2, has_side_effects=True, vmem_limit_bytes=62 * 1024 * 1024),
        name='latents',
    )(tok_x, w_dkv, w_kr, w_dq, w_uq, w_qr, g_q.astype(f32)[None], g_kv.astype(f32)[None], tab.T, tab)
    return lat.reshape(n_ctx * rows, lat_width), q_t


def solution(mesh):
    tok_spec = P(('dp', 'ctx'), None)
    pos_spec = P(('dp', 'ctx'))
    full_mat = P(None, None)
    full_vec = P(None)
    col_spec = P(None, 'tp')
    row_spec = P('tp', None)

    def local_step(tok_x, tok_pos, w_dq, g_q, w_uq, w_qr, w_dkv, g_kv, w_kr, w_uk, w_uv, w_o):
        rope_dim = w_kr.shape[1]
        heads_loc = w_qr.shape[1] // rope_dim
        nope_dim = w_uq.shape[1] // heads_loc
        score_scale = (nope_dim + rope_dim) ** -0.5
        n_ctx = mesh.shape['ctx']
        tab = jnp.concatenate(rope_tables(tok_pos, rope_dim), axis=-1)
        lat, q_t = latents(tok_x, w_dkv, w_kr, w_dq, w_uq, w_qr, g_q, g_kv, tab, n_ctx)
        return mix(q_t, lat, w_uk, w_uv, w_o, mesh.shape['tp'], n_ctx, score_scale)

    return jax.shard_map(local_step, mesh=mesh,
                         in_specs=(tok_spec, pos_spec, full_mat, full_vec, col_spec, col_spec, full_mat, full_vec, full_mat, col_spec, col_spec, row_spec),
                         out_specs=tok_spec, check_vma=False)
```

time: 189 us -> 176 us (0.931)
  Pallas kernels: 176 us -> 164 us
    pallas_call x2 -> x1, Pallas kernels: 141 us -> 128 us  [mix(): pl.pallas_call(functools.partial(mix_kernel, n_tp, n_ctx, n_blk, scale),...]
where the time goes in v4:
time: 176 us
  Pallas kernels  164 us (93%)
  local copies, waits for them, and re-layouts  8.67 us (5%)
  other arithmetic  3.32 us (2%)
    pallas_call x1, Pallas kernels, mix(): pl.pallas_call(functools.partial(mix_kernel, n_tp, n_ctx, n_blk, scale),...  128 us
    pallas_call x1, Pallas kernels, latents(): pl.pallas_call(functools.partial(latent_kernel, n_ctx), out_shape=[jax.Sh...  35.5 us
    unnamed x2, local copies, waits for them, and re-layouts  6.69 us

profile of v4, /device:TPU:102, one launch (start us, length us, event | category | flops | bytes accessed | tf_op | source)
XLA Modules:
  0.0 175.8 jit_solution(4397668768872457922)
XLA Ops:
  0.0 0.7 convert_element_type.2
  0.7 1.3 broadcast_in_dim.17
  2.0 1.3 reshape.11.gq_ref
  3.2 0.5 multiply_cosine_fusion
  3.8 0.1 fusion
  3.9 0.7 pad_maximum_fusion.tabk_ref
  4.6 0.7 copy.17.tab_ref
  5.3 2.6 %copy.16.wkr_hbm = bf16[7168,64]{1,0:T(8,128)(2,1)} copy(bf16[7168,64]{0,1:T(8,128)(2,1)} %param.20) | data formatting | bytes 1835008 | tf_op args[8]
  7.9 35.5 %latents.1 = (bf16[16,128,640]{2,1,0:T(8,128)(2,1)}, bf16[16,192,512]{2,1,0:T(8,128)(2,1)}) custom-call(bf16[256,7168]{1,0:T(8,128)(2,1)} %x_hbm.1, bf16[7168,512]{1,0:T(8,128)(2,1)} %wdkv_hbm.1, bf16[7168,64]{1,0:T(8,128)(2,1)} %copy.16.wkr_hbm, bf16[7168,1536]{1,0:T(8,128)(2,1)} %wdq_hbm.1, bf16[1536,4096]{1,0:T(8,128)(2,1)} %wuq_hbm.1, ...), custom_call_target="tpu_custom_call" | custom-call | tf_op jit(solution)/shard_map/latents/pallas_call | solution.py:507
  43.4 128.3 %mix.1 = bf16[256,7168]{1,0:T(8,128)(2,1)} custom-call(bf16[16,192,512]{2,1,0:T(8,128)(2,1)} %get-tuple-element.7.q_ref, bf16[2048,640]{1,0:T(8,128)(2,1)} %bitcast.4, bf16[512,4096]{1,0:T(8,128)(2,1)} %wuk_hbm.1, bf16[512,4096]{1,0:T(8,128)(2,1)} %wuv_hbm.1, bf16[4096,7168]{1,0:T(8,128)(2,1)} %w_hbm.1), custom_call_target="tpu_custom_call" | custom-call | tf_op jit(solution)/shard_map/mix/pallas_call | solution.py:303
  171.7 4.1 %copy.19 = bf16[256,7168]{1,0:T(8,128)(2,1)} copy(bf16[256,7168]{1,0:T(8,128)(2,1)} %mix.1) | data formatting | bytes 7340032
  (1 shorter events, 0.0 us)

commit v5 on v4

--- a/solution.py
+++ b/solution.py
@@ -11,11 +11,12 @@
 NORM_EPS = 1e-6
 
 
-def rope_tables(pos_vals, rope_dim):
+def rope_table(pos_vals, rope_dim):
     half_dim = rope_dim // 2
-    inv_freq = ROPE_BASE ** (-jnp.arange(half_dim, dtype=jnp.float32) * 2.0 / rope_dim)
-    angles = pos_vals.astype(jnp.float32)[..., None] * inv_freq
-    return jnp.cos(angles), jnp.sin(angles)
+    lane = lax.broadcasted_iota(jnp.int32, (1, 128), 1)
+    inv_freq = ROPE_BASE ** (-(lane % half_dim).astype(jnp.float32) * 2.0 / rope_dim)
+    angles = pos_vals.astype(jnp.float32)[:, None] * inv_freq
+    return jnp.where(lane % rope_dim < half_dim, jnp.cos(angles), jnp.sin(angles))
 
 
 MESH = pl.DeviceIdType.MESH
@@ -118,36 +119,38 @@
         visible = key_i <= q_i
 
         def pair_step(hp, _):
-            for i in range(n_key):
-                keys = slice(i * KEY_BLOCK, (i + 1) * KEY_BLOCK)
-                k2 = jnp.dot(lat_ref[keys, 0:rank], wuk[hp], preferred_element_type=f32).astype(bf16)
-                kcat[0, keys, 0:nope] = k2[:, :nope]
-                kcat[1, keys, 0:nope] = k2[:, nope:]
-                v_t[:, keys] = jnp.dot(wuv_t[hp], lat_t[:, keys], preferred_element_type=f32).astype(bf16)
-            top = []
+            span = n_key * KEY_BLOCK
+            k2 = jnp.dot(lat_ref[0:span, 0:rank], wuk[hp], preferred_element_type=f32).astype(bf16)
+            kcat[0, 0:span, 0:nope] = k2[:, :nope]
+            kcat[1, 0:span, 0:nope] = k2[:, nope:]
+            v_t[:, 0:span] = jnp.dot(wuv_t[hp], lat_t[:, 0:span], preferred_element_type=f32).astype(bf16)
             for g in range(2):
-                q_t = q_ref[2 * hp + g, :, q_cols]
+                s_buf[g, 0:span] = jnp.dot(kcat[g, 0:span, 0:nope + rope], q_ref[2 * hp + g, :, q_cols], preferred_element_type=f32)
+            total = []
+            for g in range(2):
                 top8 = None
                 for i in range(n_key):
-                    keys = slice(i * KEY_BLOCK, (i + 1) * KEY_BLOCK)
-                    s = jnp.dot(kcat[g, keys, 0:nope + rope], q_t, preferred_element_type=f32)
+                    s = s_buf[g, i * KEY_BLOCK:(i + 1) * KEY_BLOCK]
                     if i == n_key - 1:
                         s = jnp.where(visible, s, -1e30)
-                    s_buf[g, keys] = s
                     blk8 = jnp.max(s.reshape(KEY_BLOCK // 8, 8, KEY_BLOCK), axis=0)
                     top8 = blk8 if top8 is None else jnp.maximum(top8, blk8)
-                top.append(jnp.max(top8, axis=0, keepdims=True) * exp_scale)
-            for g in range(2):
+                top = jnp.max(top8, axis=0, keepdims=True) * exp_scale
                 sum8 = None
                 for i in range(n_key):
                     keys = slice(i * KEY_BLOCK, (i + 1) * KEY_BLOCK)
-                    p = jnp.exp2(s_buf[g, keys] * exp_scale - top[g])
+                    s = s_buf[g, keys]
+                    if i == n_key - 1:
+                        s = jnp.where(visible, s, -1e30)
+                    p = jnp.exp2(s * exp_scale - top)
                     blk8 = jnp.sum(p.reshape(KEY_BLOCK // 8, 8, KEY_BLOCK), axis=0)
                     sum8 = blk8 if sum8 is None else sum8 + blk8
-                    p_buf[g, keys] = p.astype(bf16)
-                total = jnp.sum(sum8, axis=0, keepdims=True)
-                o_t = jnp.dot(v_t[g * v_dim:(g + 1) * v_dim, 0:n_key * KEY_BLOCK], p_buf[g, 0:n_key * KEY_BLOCK], preferred_element_type=f32)
-                o_buf[q_cols, pl.ds(pl.multiple_of((2 * hp + g) * v_dim, v_dim), v_dim)] = (o_t / total).T.astype(bf16)
+                    p_buf[keys, g * KEY_BLOCK:(g + 1) * KEY_BLOCK] = p.astype(bf16)
+                total.append(jnp.sum(sum8, axis=0, keepdims=True))
+            o_t = jnp.dot(v_t[:, 0:span], p_buf[0:span], preferred_element_type=f32)
+            for g in range(2):
+                o_g = o_t[g * v_dim:(g + 1) * v_dim, g * KEY_BLOCK:(g + 1) * KEY_BLOCK] / total[g]
+                o_buf[q_cols, pl.ds(pl.multiple_of((2 * hp + g) * v_dim, v_dim), v_dim)] = o_g.T.astype(bf16)
             if serve is not None:
                 serve(hp)
             return 0
@@ -308,7 +311,7 @@
         scratch_shapes=[
             pltpu.VMEM((n_hp, rank, 2 * nope), bf16), pltpu.VMEM((n_hp, rank, 2 * v_dim), bf16), pltpu.VMEM((n_hp, 2 * v_dim, rank), bf16),
             pltpu.VMEM((rank, keys), bf16), pltpu.VMEM((2, keys, nope + rope), bf16), pltpu.VMEM((2 * v_dim, keys), bf16),
-            pltpu.VMEM((2, keys, KEY_BLOCK), f32), pltpu.VMEM((2, keys, KEY_BLOCK), bf16),
+            pltpu.VMEM((2, keys, KEY_BLOCK), f32), pltpu.VMEM((keys, 2 * KEY_BLOCK), bf16),
             pltpu.VMEM((q_count, heads * v_dim), bf16), pltpu.VMEM((2, 2, half, depth // 2), bf16),
             pltpu.VMEM((W_SLOTS, depth, OUT_BLOCK), bf16),
             pltpu.VMEM((2, n_blk, n_tp, rows, OUT_BLOCK), f32),
@@ -324,10 +327,9 @@
 
 K_CHUNKS = 4
 Q_BLOCK = 256
-Q_SLOTS = 4
-
-
-def latent_kernel(n_ctx, x_hbm, wdkv_hbm, wkr_hbm, wdq_hbm, wuq_hbm, wqr_hbm, gq_ref, gkv_ref, tab_ref, tabk_ref, lat_hbm, q_ref,
+
+
+def latent_kernel(n_ctx, x_hbm, wdkv_hbm, wkr_hbm, wdq_hbm, wuq_hbm, wqr_hbm, gain_ref, tab_ref, lat_hbm, q_ref,
                   x_v, wdkv, wkr, wdq, wuq, wqr, kv_acc, kr_acc, cq_acc, cq_all, tab_all, lat,
                   x_sem, dkv_sem, kr_sem, dq_sem, uq_sem, qr_sem, ring_send, ring_recv, mate_send, mate_recv, cq_send, cq_recv, tab_send, tab_recv, lat_sem):
     me = lax.axis_index('ctx')
@@ -343,7 +345,6 @@
     rope = kr_acc.shape[1]
     rot = rope // 2
     kc = width // K_CHUNKS
-    n_dq = cq_acc.shape[1] // Q_BLOCK
     n_uq, n_qr = wuq.shape[0], wqr.shape[0]
     nope = q_ref.shape[1] - rope
 
@@ -352,8 +353,8 @@
 
     x_copy = [pltpu.make_async_copy(x_hbm.at[:, kcols(k)], x_v.at[:, kcols(k)], x_sem.at[k]) for k in range(K_CHUNKS)]
     dkv_copy = [pltpu.make_async_copy(wdkv_hbm.at[kcols(k)], wdkv.at[kcols(k)], dkv_sem.at[k]) for k in range(K_CHUNKS)]
-    kr_copy = [pltpu.make_async_copy(wkr_hbm.at[kcols(k)], wkr.at[kcols(k)], kr_sem.at[k]) for k in range(K_CHUNKS)]
-    dq_copy = [pltpu.make_async_copy(wdq_hbm.at[:, pl.ds(b * Q_BLOCK, Q_BLOCK)], wdq.at[b % Q_SLOTS], dq_sem.at[b % Q_SLOTS]) for b in range(n_dq)]
+    kr_copy = [pltpu.make_async_copy(wkr_hbm.at[:, kcols(k)], wkr.at[:, kcols(k)], kr_sem.at[k]) for k in range(K_CHUNKS)]
+    dq_copy = [pltpu.make_async_copy(wdq_hbm.at[kcols(k)], wdq.at[kcols(k)], dq_sem.at[k]) for k in range(K_CHUNKS)]
     uq_copy = [pltpu.make_async_copy(wuq_hbm.at[:, pl.ds(pl.multiple_of((part * n_uq + b) * Q_BLOCK, Q_BLOCK), Q_BLOCK)], wuq.at[b], uq_sem.at[b]) for b in range(n_uq)]
     qr_copy = [pltpu.make_async_copy(wqr_hbm.at[:, pl.ds(pl.multiple_of((part * n_qr + b) * Q_BLOCK, Q_BLOCK), Q_BLOCK)], wqr.at[b], qr_sem.at[b]) for b in range(n_qr)]
 
@@ -387,13 +388,13 @@
         x_copy[k].start()
         dkv_copy[k].start()
         kr_copy[k].start()
-    for b in range(Q_SLOTS):
-        dq_copy[b].start()
+    for k in range(K_CHUNKS):
+        dq_copy[k].start()
     barrier = pltpu.get_barrier_semaphore()
     for dev in (mate, right, left):
         pl.semaphore_signal(barrier, inc=1, device_id={'ctx': dev}, device_id_type=MESH)
     for s in range(2):
-        tab_all[:, lanes(s)] = tab_ref[:, s * half:(s + 1) * half]
+        tab_all[:, lanes(s)] = tab_ref[s * half:(s + 1) * half].T[0:rope]
 
     for k in range(K_CHUNKS):
         cols = slice(k * kc, (k + 1) * kc)
@@ -401,7 +402,7 @@
         dkv_copy[k].wait()
         kr_copy[k].wait()
         kv_new = jnp.dot(x_v[:, cols], wdkv[cols], preferred_element_type=f32)
-        kr_new = jnp.dot(x_v[:, cols], wkr[cols], preferred_element_type=f32)
+        kr_new = lax.dot_general(x_v[:, cols], wkr[:, cols], (((1,), (1,)), ((), ())), preferred_element_type=f32)
         if k == 0:
             kv_acc[...] = kv_new
             kr_acc[...] = kr_new
@@ -409,9 +410,9 @@
             kv_acc[...] += kv_new
             kr_acc[...] += kr_new
     kv = kv_acc[...]
-    c_kv = (kv * lax.rsqrt(jnp.mean(kv * kv, axis=-1, keepdims=True) + NORM_EPS) * gkv_ref[...]).astype(jnp.bfloat16)
+    c_kv = (kv * lax.rsqrt(jnp.mean(kv * kv, axis=-1, keepdims=True) + NORM_EPS) * gain_ref[0:1, 0:rank]).astype(jnp.bfloat16)
     kr = kr_acc[...]
-    cos_k, sin_k = tabk_ref[:, :rot], tabk_ref[:, rot:]
+    cos_k, sin_k = tab_ref[:, :rot], tab_ref[:, rot:rope]
     k_lo = (kr[:, :rot] * cos_k - kr[:, rot:] * sin_k).astype(jnp.bfloat16)
     k_hi = (kr[:, rot:] * cos_k + kr[:, :rot] * sin_k).astype(jnp.bfloat16)
     pad = jnp.zeros((half, lat.shape[2] - rank - rope), jnp.bfloat16)
@@ -428,18 +429,20 @@
         tab_share[s].start()
         shares[s].start()
 
-    for b in range(n_dq):
-        dq_copy[b].wait()
-        cq_acc[:, b * Q_BLOCK:(b + 1) * Q_BLOCK] = jnp.dot(x_v[...], wdq[b % Q_SLOTS], preferred_element_type=f32)
-        if b + Q_SLOTS < n_dq:
-            dq_copy[b + Q_SLOTS].start()
-        if b == 1:
+    for k in range(K_CHUNKS):
+        cols = slice(k * kc, (k + 1) * kc)
+        dq_copy[k].wait()
+        cq_new = jnp.dot(x_v[:, cols], wdq[cols], preferred_element_type=f32)
+        if k == 0:
+            cq_acc[...] = cq_new
             for c in qr_copy + uq_copy:
                 c.start()
+        else:
+            cq_acc[...] += cq_new
     for s in range(2):
         own = slice(s * half, (s + 1) * half)
         cq = cq_acc[own]
-        cq_all[slot_of[s]] = (cq * lax.rsqrt(jnp.mean(cq * cq, axis=-1, keepdims=True) + NORM_EPS) * gq_ref[...]).astype(jnp.bfloat16)
+        cq_all[slot_of[s]] = (cq * lax.rsqrt(jnp.mean(cq * cq, axis=-1, keepdims=True) + NORM_EPS) * gain_ref[0:1, rank:]).astype(jnp.bfloat16)
         cq_share[s].start()
 
     to_right[0].wait_recv()
@@ -504,22 +507,23 @@
     n_uq, n_qr = heads * nope // Q_BLOCK, heads * rope // Q_BLOCK
     lat_width = rank + 128
     assert n_ctx == 8 and rope <= 128
+    gain = jnp.broadcast_to(jnp.concatenate([g_kv, g_q]).astype(f32)[None], (8, rank + q_rank))
     lat, q_t = pl.pallas_call(
         functools.partial(latent_kernel, n_ctx),
         out_shape=[jax.ShapeDtypeStruct((2 * n_ctx, rows // 2, lat_width), bf16), jax.ShapeDtypeStruct((heads, nope + rope, 2 * rows), bf16)],
-        in_specs=[hbm] * 6 + [vmem] * 4,
+        in_specs=[hbm] * 6 + [vmem] * 2,
         out_specs=[hbm, vmem],
         scratch_shapes=[
-            pltpu.VMEM((rows, width), bf16), pltpu.VMEM((width, rank), bf16), pltpu.VMEM((width, rope), bf16), pltpu.VMEM((Q_SLOTS, width, Q_BLOCK), bf16),
+            pltpu.VMEM((rows, width), bf16), pltpu.VMEM((width, rank), bf16), pltpu.VMEM((rope, width), bf16), pltpu.VMEM((width, q_rank), bf16),
             pltpu.VMEM((n_uq, q_rank, Q_BLOCK), bf16), pltpu.VMEM((n_qr, q_rank, Q_BLOCK), bf16),
             pltpu.VMEM((rows, rank), f32), pltpu.VMEM((rows, rope), f32), pltpu.VMEM((rows, q_rank), f32),
             pltpu.VMEM((4, rows // 2, q_rank), bf16), pltpu.VMEM((rope, 2 * rows), f32), pltpu.VMEM((2 * n_ctx, rows // 2, lat_width), bf16),
-            dma((K_CHUNKS,)), dma((K_CHUNKS,)), dma((K_CHUNKS,)), dma((Q_SLOTS,)), dma((n_uq,)), dma((n_qr,)),
+            dma((K_CHUNKS,)), dma((K_CHUNKS,)), dma((K_CHUNKS,)), dma((K_CHUNKS,)), dma((n_uq,)), dma((n_qr,)),
             dma((6,)), dma((6,)), dma((8,)), dma((8,)), dma((2,)), dma((2,)), dma((2,)), dma((2,)), dma,
         ],
         compiler_params=pltpu.CompilerParams(collective_id=2, has_side_effects=True, vmem_limit_bytes=62 * 1024 * 1024),
         name='latents',
-    )(tok_x, w_dkv, w_kr, w_dq, w_uq, w_qr, g_q.astype(f32)[None], g_kv.astype(f32)[None], tab.T, tab)
+    )(tok_x, w_dkv, w_kr.T, w_dq, w_uq, w_qr, gain, tab)
     return lat.reshape(n_ctx * rows, lat_width), q_t
 
 
@@ -537,7 +541,7 @@
         nope_dim = w_uq.shape[1] // heads_loc
         score_scale = (nope_dim + rope_dim) ** -0.5
         n_ctx = mesh.shape['ctx']
-        tab = jnp.concatenate(rope_tables(tok_pos, rope_dim), axis=-1)
+        tab = rope_table(tok_pos, rope_dim)
         lat, q_t = latents(tok_x, w_dkv, w_kr, w_dq, w_uq, w_qr, g_q, g_kv, tab, n_ctx)
         return mix(q_t, lat, w_uk, w_uv, w_o, mesh.shape['tp'], n_ctx, score_scale)
 

time: 176 us -> 167 us (0.949)
  Pallas kernels: 164 us -> 160 us
  local copies, waits for them, and re-layouts: 8.67 us -> 4.73 us
    pallas_call x1, Pallas kernels: 35.5 us -> 30.4 us  [latents(): pl.pallas_call(functools.partial(latent_kernel, n_ctx), out_shape=[jax.Sh...]
    unnamed x2 -> x1, local copies, waits for them, and re-layouts: 6.69 us -> 4.11 us
where the time goes in v5:
time: 167 us
  Pallas kernels  160 us (96%)
  local copies, waits for them, and re-layouts  4.73 us (3%)
  other arithmetic  2.59 us (2%)
    pallas_call x1, Pallas kernels, mix(): pl.pallas_call(functools.partial(mix_kernel, n_tp, n_ctx, n_blk, scale),...  129 us
    pallas_call x1, Pallas kernels, latents(): pl.pallas_call(functools.partial(latent_kernel, n_ctx), out_shape=[jax.Sh...  30.4 us
    unnamed x1, local copies, waits for them, and re-layouts  4.11 us

profile of v5, /device:TPU:102, one launch (start us, length us, event | category | flops | bytes accessed | tf_op | source)
XLA Modules:
  0.0 167.0 jit_solution(11282674860587254891)
XLA Ops:
  0.0 0.7 convert_element_type.19
  0.7 0.7 maximum_convert_fusion
  1.4 0.6 broadcast_in_dim.10.gain_ref
  2.0 1.2 fusion.tab_ref
  3.2 30.4 %latents.1 = (bf16[16,128,640]{2,1,0:T(8,128)(2,1)}, bf16[16,192,512]{2,1,0:T(8,128)(2,1)}) custom-call(bf16[256,7168]{1,0:T(8,128)(2,1)} %x_hbm.1, bf16[7168,512]{1,0:T(8,128)(2,1)} %wdkv_hbm.1, bf16[64,7168]{1,0:T(8,128)(2,1)} %bitcast.3, bf16[7168,1536]{1,0:T(8,128)(2,1)} %wdq_hbm.1, bf16[1536,4096]{1,0:T(8,128)(2,1)} %wuq_hbm.1, ...), custom_call_target="tpu_custom_call" | custom-call | tf_op jit(solution)/shard_map/latents/pallas_call | solution.py:511
  33.6 129.3 %mix.1 = bf16[256,7168]{1,0:T(8,128)(2,1)} custom-call(bf16[16,192,512]{2,1,0:T(8,128)(2,1)} %get-tuple-element.7.q_ref, bf16[2048,640]{1,0:T(8,128)(2,1)} %bitcast.2, bf16[512,4096]{1,0:T(8,128)(2,1)} %wuk_hbm.1, bf16[512,4096]{1,0:T(8,128)(2,1)} %wuv_hbm.1, bf16[4096,7168]{1,0:T(8,128)(2,1)} %w_hbm.1), custom_call_target="tpu_custom_call" | custom-call | tf_op jit(solution)/shard_map/mix/pallas_call | solution.py:306
  162.9 4.1 %copy.14 = bf16[256,7168]{1,0:T(8,128)(2,1)} copy(bf16[256,7168]{1,0:T(8,128)(2,1)} %mix.1) | data formatting | bytes 7340032
  (2 shorter events, 0.0 us)

commit v6 on v5

--- a/solution.py
+++ b/solution.py
@@ -27,7 +27,7 @@
 
 
 def mix_kernel(n_tp, n_ctx, n_blk, scale, q_ref, lat_ref, wuk_hbm, wuv_hbm, w_hbm, out_hbm,
-               wuk, wuv, wuv_t, lat_t, kcat, v_t, s_buf, p_buf, o_buf, o_all, wbuf, part, recv, ybuf,
+               wuk, wuv, wuv_t, lat_t, kcat, v_t, s_buf, top_buf, p_buf, o_buf, o_all, wbuf, part, recv, ybuf,
                up_sem, w_sem, o_send, o_recv, rs_send, rs_recv, ag_send, ag_recv, out_sem):
     f32, bf16 = jnp.float32, jnp.bfloat16
     ctx = lax.axis_index('ctx')
@@ -44,7 +44,7 @@
     heads = q_ref.shape[0]
     n_hp = heads // 2
     rank = wuk.shape[1]
-    v_dim = v_t.shape[0] // 2
+    v_dim = v_t.shape[1] // 2
     nope = wuk.shape[2] // 2
     rope = q_ref.shape[1] - nope
     exp_scale = scale * 1.4426950408889634
@@ -118,39 +118,43 @@
         q_i = lax.broadcasted_iota(jnp.int32, (KEY_BLOCK, KEY_BLOCK), 1)
         visible = key_i <= q_i
 
+        span = n_key * KEY_BLOCK
+
+        def overlap(nxt, now):
+            top8 = [None, None]
+            sum8 = [None, None]
+            top = None if now is None else [top_buf[g] for g in range(2)]
+            for i in range(n_key):
+                keys = slice(i * KEY_BLOCK, (i + 1) * KEY_BLOCK)
+                if now is not None:
+                    for g in range(2):
+                        p = jnp.exp2(s_buf[g, keys] * exp_scale - top[g])
+                        blk8 = jnp.sum(p.reshape(KEY_BLOCK // 8, 8, KEY_BLOCK), axis=0)
+                        sum8[g] = blk8 if sum8[g] is None else sum8[g] + blk8
+                        p_buf[keys, g * KEY_BLOCK:(g + 1) * KEY_BLOCK] = p.astype(bf16)
+                k2 = jnp.dot(lat_ref[keys, 0:rank], wuk[nxt], preferred_element_type=f32).astype(bf16)
+                kcat[0, keys, 0:nope] = k2[:, :nope]
+                kcat[1, keys, 0:nope] = k2[:, nope:]
+                v_t[lax.rem(nxt, 2), :, keys] = jnp.dot(wuv_t[nxt], lat_t[:, keys], preferred_element_type=f32).astype(bf16)
+                for g in range(2):
+                    sc = jnp.dot(kcat[g, keys, 0:nope + rope], q_ref[2 * nxt + g, :, q_cols], preferred_element_type=f32)
+                    if i == n_key - 1:
+                        sc = jnp.where(visible, sc, -1e30)
+                    s_buf[g, keys] = sc
+                    blk8 = jnp.max(sc.reshape(KEY_BLOCK // 8, 8, KEY_BLOCK), axis=0)
+                    top8[g] = blk8 if top8[g] is None else jnp.maximum(top8[g], blk8)
+            for g in range(2):
+                top_buf[g] = jnp.max(top8[g], axis=0, keepdims=True) * exp_scale
+            if now is not None:
+                o_t = jnp.dot(v_t[lax.rem(now, 2), :, 0:span], p_buf[0:span], preferred_element_type=f32)
+                for g in range(2):
+                    o_g = o_t[g * v_dim:(g + 1) * v_dim, g * KEY_BLOCK:(g + 1) * KEY_BLOCK] / jnp.sum(sum8[g], axis=0, keepdims=True)
+                    o_buf[q_cols, pl.ds(pl.multiple_of((2 * now + g) * v_dim, v_dim), v_dim)] = o_g.T.astype(bf16)
+
+        overlap(0, None)
+
         def pair_step(hp, _):
-            span = n_key * KEY_BLOCK
-            k2 = jnp.dot(lat_ref[0:span, 0:rank], wuk[hp], preferred_element_type=f32).astype(bf16)
-            kcat[0, 0:span, 0:nope] = k2[:, :nope]
-            kcat[1, 0:span, 0:nope] = k2[:, nope:]
-            v_t[:, 0:span] = jnp.dot(wuv_t[hp], lat_t[:, 0:span], preferred_element_type=f32).astype(bf16)
-            for g in range(2):
-                s_buf[g, 0:span] = jnp.dot(kcat[g, 0:span, 0:nope + rope], q_ref[2 * hp + g, :, q_cols], preferred_element_type=f32)
-            total = []
-            for g in range(2):
-                top8 = None
-                for i in range(n_key):
-                    s = s_buf[g, i * KEY_BLOCK:(i + 1) * KEY_BLOCK]
-                    if i == n_key - 1:
-                        s = jnp.where(visible, s, -1e30)
-                    blk8 = jnp.max(s.reshape(KEY_BLOCK // 8, 8, KEY_BLOCK), axis=0)
-                    top8 = blk8 if top8 is None else jnp.maximum(top8, blk8)
-                top = jnp.max(top8, axis=0, keepdims=True) * exp_scale
-                sum8 = None
-                for i in range(n_key):
-                    keys = slice(i * KEY_BLOCK, (i + 1) * KEY_BLOCK)
-                    s = s_buf[g, keys]
-                    if i == n_key - 1:
-                        s = jnp.where(visible, s, -1e30)
-                    p = jnp.exp2(s * exp_scale - top)
-                    blk8 = jnp.sum(p.reshape(KEY_BLOCK // 8, 8, KEY_BLOCK), axis=0)
-                    sum8 = blk8 if sum8 is None else sum8 + blk8
-                    p_buf[keys, g * KEY_BLOCK:(g + 1) * KEY_BLOCK] = p.astype(bf16)
-                total.append(jnp.sum(sum8, axis=0, keepdims=True))
-            o_t = jnp.dot(v_t[:, 0:span], p_buf[0:span], preferred_element_type=f32)
-            for g in range(2):
-                o_g = o_t[g * v_dim:(g + 1) * v_dim, g * KEY_BLOCK:(g + 1) * KEY_BLOCK] / total[g]
-                o_buf[q_cols, pl.ds(pl.multiple_of((2 * hp + g) * v_dim, v_dim), v_dim)] = o_g.T.astype(bf16)
+            overlap(jnp.where(hp + 1 < n_hp, hp + 1, n_hp - 2), hp)
             if serve is not None:
                 serve(hp)
             return 0
@@ -310,8 +314,8 @@
         out_specs=hbm,
         scratch_shapes=[
             pltpu.VMEM((n_hp, rank, 2 * nope), bf16), pltpu.VMEM((n_hp, rank, 2 * v_dim), bf16), pltpu.VMEM((n_hp, 2 * v_dim, rank), bf16),
-            pltpu.VMEM((rank, keys), bf16), pltpu.VMEM((2, keys, nope + rope), bf16), pltpu.VMEM((2 * v_dim, keys), bf16),
-            pltpu.VMEM((2, keys, KEY_BLOCK), f32), pltpu.VMEM((keys, 2 * KEY_BLOCK), bf16),
+            pltpu.VMEM((rank, keys), bf16), pltpu.VMEM((2, keys, nope + rope), bf16), pltpu.VMEM((2, 2 * v_dim, keys), bf16),
+            pltpu.VMEM((2, keys, KEY_BLOCK), f32), pltpu.VMEM((2, 1, KEY_BLOCK), f32), pltpu.VMEM((keys, 2 * KEY_BLOCK), bf16),
             pltpu.VMEM((q_count, heads * v_dim), bf16), pltpu.VMEM((2, 2, half, depth // 2), bf16),
             pltpu.VMEM((W_SLOTS, depth, OUT_BLOCK), bf16),
             pltpu.VMEM((2, n_blk, n_tp, rows, OUT_BLOCK), f32),
@@ -429,16 +433,17 @@
         tab_share[s].start()
         shares[s].start()
 
-    for k in range(K_CHUNKS):
-        cols = slice(k * kc, (k + 1) * kc)
-        dq_copy[k].wait()
-        cq_new = jnp.dot(x_v[:, cols], wdq[cols], preferred_element_type=f32)
-        if k == 0:
-            cq_acc[...] = cq_new
-            for c in qr_copy + uq_copy:
-                c.start()
-        else:
-            cq_acc[...] += cq_new
+    for c in qr_copy + uq_copy:
+        c.start()
+    cq_acc[...] = jnp.zeros_like(cq_acc)
+
+    def contract(k, _):
+        cols = pl.ds(pl.multiple_of(k * kc, kc), kc)
+        pltpu.make_async_copy(wdq_hbm.at[cols], wdq.at[cols], dq_sem.at[k]).wait()
+        cq_acc[...] += jnp.dot(x_v[:, cols], wdq[cols], preferred_element_type=f32)
+        return 0
+
+    lax.fori_loop(0, K_CHUNKS, contract, 0)
     for s in range(2):
         own = slice(s * half, (s + 1) * half)
         cq = cq_acc[own]

time: 167 us -> 169 us (1.012)
  no operation moved by 1% of the time
where the time goes in v6:
time: 169 us
  Pallas kernels  161 us (95%)
  local copies, waits for them, and re-layouts  4.73 us (3%)
  other arithmetic  2.59 us (2%)
    pallas_call x1, Pallas kernels, mix(): pl.pallas_call(functools.partial(mix_kernel, n_tp, n_ctx, n_blk, scale),...  130 us
    pallas_call x1, Pallas kernels, latents(): pl.pallas_call(functools.partial(latent_kernel, n_ctx), out_shape=[jax.Sh...  30.9 us
    unnamed x1, local copies, waits for them, and re-layouts  4.11 us

profile of v6, /device:TPU:102, one launch (start us, length us, event | category | flops | bytes accessed | tf_op | source)
XLA Modules:
  0.0 168.6 jit_solution(7503486377591901022)
XLA Ops:
  0.0 0.7 convert_element_type.19
  0.7 0.7 maximum_convert_fusion
  1.4 0.6 broadcast_in_dim.10.gain_ref
  2.0 1.2 fusion.tab_ref
  3.2 30.9 %latents.1 = (bf16[16,128,640]{2,1,0:T(8,128)(2,1)}, bf16[16,192,512]{2,1,0:T(8,128)(2,1)}) custom-call(bf16[256,7168]{1,0:T(8,128)(2,1)} %x_hbm.1, bf16[7168,512]{1,0:T(8,128)(2,1)} %wdkv_hbm.1, bf16[64,7168]{1,0:T(8,128)(2,1)} %bitcast.3, bf16[7168,1536]{1,0:T(8,128)(2,1)} %wdq_hbm.1, bf16[1536,4096]{1,0:T(8,128)(2,1)} %wuq_hbm.1, ...), custom_call_target="tpu_custom_call" | custom-call | tf_op jit(solution)/shard_map/latents/pallas_call | solution.py:516
  34.2 130.3 %mix.1 = bf16[256,7168]{1,0:T(8,128)(2,1)} custom-call(bf16[16,192,512]{2,1,0:T(8,128)(2,1)} %get-tuple-element.7.q_ref, bf16[2048,640]{1,0:T(8,128)(2,1)} %bitcast.2, bf16[512,4096]{1,0:T(8,128)(2,1)} %wuk_hbm.1, bf16[512,4096]{1,0:T(8,128)(2,1)} %wuv_hbm.1, bf16[4096,7168]{1,0:T(8,128)(2,1)} %w_hbm.1), custom_call_target="tpu_custom_call" | custom-call | tf_op jit(solution)/shard_map/mix/pallas_call | solution.py:310
  164.5 4.1 %copy.14 = bf16[256,7168]{1,0:T(8,128)(2,1)} copy(bf16[256,7168]{1,0:T(8,128)(2,1)} %mix.1) | data formatting | bytes 7340032
  (2 shorter events, 0.0 us)

commit v7 on v5

--- a/solution.py
+++ b/solution.py
@@ -96,8 +96,6 @@
     for hp in range(n_hp):
         up_copy(wuk_hbm, wuk, 0, hp).start()
         up_copy(wuv_hbm, wuv, 1, hp).start()
-    for i in range(W_SLOTS):
-        w_copy(i).start()
     barrier = pltpu.get_barrier_semaphore()
     for neighbour in peer:
         pl.semaphore_signal(barrier, inc=1, device_id={'tp': neighbour}, device_id_type=MESH)
@@ -110,6 +108,8 @@
         up_copy(wuk_hbm, wuk, 0, hp).wait()
         up_copy(wuv_hbm, wuv, 1, hp).wait()
         wuv_t[hp] = wuv[hp].T
+    for i in range(W_SLOTS):
+        w_copy(i).start()
     pl.semaphore_wait(barrier, 3)
 
     def attend(sel, n_key, serve):
@@ -384,12 +384,18 @@
 
     tab_share = [send(tab_all.at[:, lanes(s)], tab_all.at[:, lanes(s)], tab_send.at[s], tab_recv.at[s], mate) for s in range(2)]
 
-    for k in range(K_CHUNKS):
-        x_copy[k].start()
-        dkv_copy[k].start()
-        kr_copy[k].start()
-    for k in range(K_CHUNKS):
-        dq_copy[k].start()
+    def fetch(k):
+        if k < K_CHUNKS:
+            group = [x_copy[k], dkv_copy[k], kr_copy[k]]
+        elif k < 2 * K_CHUNKS:
+            group = [dq_copy[k - K_CHUNKS]]
+        else:
+            group = qr_copy if k == 2 * K_CHUNKS else uq_copy
+        for c in group:
+            c.start()
+
+    fetch(0)
+    fetch(1)
     barrier = pltpu.get_barrier_semaphore()
     for dev in (mate, right, left):
         pl.semaphore_signal(barrier, inc=1, device_id={'ctx': dev}, device_id_type=MESH)
@@ -401,6 +407,7 @@
         x_copy[k].wait()
         dkv_copy[k].wait()
         kr_copy[k].wait()
+        fetch(k + 2)
         kv_new = jnp.dot(x_v[:, cols], wdkv[cols], preferred_element_type=f32)
         kr_new = lax.dot_general(x_v[:, cols], wkr[:, cols], (((1,), (1,)), ((), ())), preferred_element_type=f32)
         if k == 0:
@@ -432,11 +439,10 @@
     for k in range(K_CHUNKS):
         cols = slice(k * kc, (k + 1) * kc)
         dq_copy[k].wait()
+        fetch(K_CHUNKS + k + 2)
         cq_new = jnp.dot(x_v[:, cols], wdq[cols], preferred_element_type=f32)
         if k == 0:
             cq_acc[...] = cq_new
-            for c in qr_copy + uq_copy:
-                c.start()
         else:
             cq_acc[...] += cq_new
     for s in range(2):

time: 167 us -> 162 us (0.970)
  Pallas kernels: 160 us -> 154 us
    pallas_call x1, Pallas kernels: 30.4 us -> 27.2 us  [latents(): pl.pallas_call(functools.partial(latent_kernel, n_ctx), out_shape=[jax.Sh...]
    pallas_call x1, Pallas kernels: 129 us -> 127 us  [mix(): pl.pallas_call(functools.partial(mix_kernel, n_tp, n_ctx, n_blk, scale),...]
where the time goes in v7:
time: 162 us; the launch traced here: 161 us
  Pallas kernels  154 us (95%)
  local copies, waits for them, and re-layouts  4.73 us (3%)
  other arithmetic  2.59 us (2%)
    pallas_call x1, Pallas kernels, mix(): pl.pallas_call(functools.partial(mix_kernel, n_tp, n_ctx, n_blk, scale),...  127 us
    pallas_call x1, Pallas kernels, latents(): pl.pallas_call(functools.partial(latent_kernel, n_ctx), out_shape=[jax.Sh...  27.2 us
    unnamed x1, local copies, waits for them, and re-layouts  4.11 us

profile of v7, /device:TPU:102, one launch (start us, length us, event | category | flops | bytes accessed | tf_op | source)
XLA Modules:
  0.0 161.3 jit_solution(11873595231766675857)
XLA Ops:
  0.0 0.7 convert_element_type.19
  0.7 0.7 maximum_convert_fusion
  1.4 0.6 broadcast_in_dim.10.gain_ref
  2.0 1.2 fusion.tab_ref
  3.2 27.2 %latents.1 = (bf16[16,128,640]{2,1,0:T(8,128)(2,1)}, bf16[16,192,512]{2,1,0:T(8,128)(2,1)}) custom-call(bf16[256,7168]{1,0:T(8,128)(2,1)} %x_hbm.1, bf16[7168,512]{1,0:T(8,128)(2,1)} %wdkv_hbm.1, bf16[64,7168]{1,0:T(8,128)(2,1)} %bitcast.3, bf16[7168,1536]{1,0:T(8,128)(2,1)} %wdq_hbm.1, bf16[1536,4096]{1,0:T(8,128)(2,1)} %wuq_hbm.1, ...), custom_call_target="tpu_custom_call" | custom-call | tf_op jit(solution)/shard_map/latents/pallas_call | solution.py:517
  30.5 126.7 %mix.1 = bf16[256,7168]{1,0:T(8,128)(2,1)} custom-call(bf16[16,192,512]{2,1,0:T(8,128)(2,1)} %get-tuple-element.7.q_ref, bf16[2048,640]{1,0:T(8,128)(2,1)} %bitcast.2, bf16[512,4096]{1,0:T(8,128)(2,1)} %wuk_hbm.1, bf16[512,4096]{1,0:T(8,128)(2,1)} %wuv_hbm.1, bf16[4096,7168]{1,0:T(8,128)(2,1)} %w_hbm.1), custom_call_target="tpu_custom_call" | custom-call | tf_op jit(solution)/shard_map/mix/pallas_call | solution.py:306
  157.2 4.1 %copy.14 = bf16[256,7168]{1,0:T(8,128)(2,1)} copy(bf16[256,7168]{1,0:T(8,128)(2,1)} %mix.1) | data formatting | bytes 7340032
  (2 shorter events, 0.0 us)

commit v8 on v7

--- a/solution.py
+++ b/solution.py
@@ -26,8 +26,8 @@
 LAG = 3
 
 
-def mix_kernel(n_tp, n_ctx, n_blk, scale, q_ref, lat_ref, wuk_hbm, wuv_hbm, w_hbm, out_hbm,
-               wuk, wuv, wuv_t, lat_t, kcat, v_t, s_buf, p_buf, o_buf, o_all, wbuf, part, recv, ybuf,
+def mix_kernel(n_tp, n_ctx, n_blk, scale, q_hbm, lat_hbm, wuk_hbm, wuv_hbm, w_hbm, out_hbm,
+               q_ref, lat_ref, in_sem, wuk, wuv, wuv_t, lat_t, kcat, v_t, s_buf, p_buf, o_buf, o_all, wbuf, part, recv, ybuf,
                up_sem, w_sem, o_send, o_recv, rs_send, rs_recv, ag_send, ag_recv, out_sem):
     f32, bf16 = jnp.float32, jnp.bfloat16
     ctx = lax.axis_index('ctx')
@@ -93,13 +93,18 @@
         return pltpu.make_async_remote_copy(src_ref=o_buf.at[pl.ds(pl.multiple_of(mate_at[sel] * half, half), half)], dst_ref=o_all.at[sel, core],
                                             send_sem=o_send.at[sel], recv_sem=o_recv.at[sel], device_id={'ctx': mate}, device_id_type=MESH)
 
+    lat_in = pltpu.make_async_copy(lat_hbm, lat_ref, in_sem.at[0])
+    q_in = pltpu.make_async_copy(q_hbm, q_ref, in_sem.at[1])
+    lat_in.start()
     for hp in range(n_hp):
         up_copy(wuk_hbm, wuk, 0, hp).start()
         up_copy(wuv_hbm, wuv, 1, hp).start()
+    q_in.start()
     barrier = pltpu.get_barrier_semaphore()
     for neighbour in peer:
         pl.semaphore_signal(barrier, inc=1, device_id={'tp': neighbour}, device_id_type=MESH)
     pl.semaphore_signal(barrier, inc=1, device_id={'ctx': mate}, device_id_type=MESH)
+    lat_in.wait()
     for i in range(lat_ref.shape[0] // KEY_BLOCK):
         lat_t[:, i * KEY_BLOCK:(i + 1) * KEY_BLOCK] = lat_ref[i * KEY_BLOCK:(i + 1) * KEY_BLOCK, 0:rank].T
         for g in range(2):
@@ -108,6 +113,7 @@
         up_copy(wuk_hbm, wuk, 0, hp).wait()
         up_copy(wuv_hbm, wuv, 1, hp).wait()
         wuv_t[hp] = wuv[hp].T
+    q_in.wait()
     for i in range(W_SLOTS):
         w_copy(i).start()
     pl.semaphore_wait(barrier, 3)
@@ -300,15 +306,15 @@
     assert n_tp == 4 and n_blk % 2 == 0 and width % OUT_BLOCK == 0
     assert q_count == 2 * KEY_BLOCK and keys == n_ctx * KEY_BLOCK
     bf16, f32 = jnp.bfloat16, jnp.float32
-    vmem = pl.BlockSpec(memory_space=pltpu.VMEM)
     hbm = pl.BlockSpec(memory_space=pl.ANY)
     dma = pltpu.SemaphoreType.DMA
     return pl.pallas_call(
         functools.partial(mix_kernel, n_tp, n_ctx, n_blk, scale),
         out_shape=jax.ShapeDtypeStruct((2 * half, width), bf16),
-        in_specs=[vmem, vmem, hbm, hbm, hbm],
+        in_specs=[hbm] * 5,
         out_specs=hbm,
         scratch_shapes=[
+            pltpu.VMEM(q_t.shape, bf16), pltpu.VMEM(lat.shape, bf16), dma((2,)),
             pltpu.VMEM((n_hp, rank, 2 * nope), bf16), pltpu.VMEM((n_hp, rank, 2 * v_dim), bf16), pltpu.VMEM((n_hp, 2 * v_dim, rank), bf16),
             pltpu.VMEM((rank, keys), bf16), pltpu.VMEM((2, keys, nope + rope), bf16), pltpu.VMEM((2 * v_dim, keys), bf16),
             pltpu.VMEM((2, keys, KEY_BLOCK), f32), pltpu.VMEM((keys, 2 * KEY_BLOCK), bf16),

time: 162 us -> 161 us (level)
  no operation moved by 1% of the time
where the time goes in v8:
time: 161 us
  Pallas kernels  154 us (96%)
  local copies, waits for them, and re-layouts  4.73 us (3%)
  other arithmetic  2.59 us (2%)
    pallas_call x1, Pallas kernels, mix(): pl.pallas_call(functools.partial(mix_kernel, n_tp, n_ctx, n_blk, scale),...  126 us
    pallas_call x1, Pallas kernels, latents(): pl.pallas_call(functools.partial(latent_kernel, n_ctx), out_shape=[jax.Sh...  27.2 us
    unnamed x1, local copies, waits for them, and re-layouts  4.11 us

profile of v8, /device:TPU:102, one launch (start us, length us, event | category | flops | bytes accessed | tf_op | source)
XLA Modules:
  0.0 161.0 jit_solution(9276857807624578321)
XLA Ops:
  0.0 0.7 convert_element_type.19
  0.7 0.7 maximum_convert_fusion
  1.4 0.6 broadcast_in_dim.10.gain_ref
  2.0 1.2 fusion.tab_ref
  3.2 27.2 %latents.1 = (bf16[16,128,640]{2,1,0:T(8,128)(2,1)}, bf16[16,192,512]{2,1,0:T(8,128)(2,1)}) custom-call(bf16[256,7168]{1,0:T(8,128)(2,1)} %x_hbm.1, bf16[7168,512]{1,0:T(8,128)(2,1)} %wdkv_hbm.1, bf16[64,7168]{1,0:T(8,128)(2,1)} %bitcast.3, bf16[7168,1536]{1,0:T(8,128)(2,1)} %wdq_hbm.1, bf16[1536,4096]{1,0:T(8,128)(2,1)} %wuq_hbm.1, ...), custom_call_target="tpu_custom_call" | custom-call | tf_op jit(solution)/shard_map/latents/pallas_call | solution.py:523
  30.5 126.4 %mix.1 = bf16[256,7168]{1,0:T(8,128)(2,1)} custom-call(bf16[16,192,512]{2,1,0:T(8,128)(2,1)} %get-tuple-element.7.q_hbm, bf16[2048,640]{1,0:T(8,128)(2,1)} %bitcast.2, bf16[512,4096]{1,0:T(8,128)(2,1)} %wuk_hbm.1, bf16[512,4096]{1,0:T(8,128)(2,1)} %wuv_hbm.1, bf16[4096,7168]{1,0:T(8,128)(2,1)} %w_hbm.1), custom_call_target="tpu_custom_call" | custom-call | tf_op jit(solution)/shard_map/mix/pallas_call | solution.py:311
  156.9 4.1 %copy.14 = bf16[256,7168]{1,0:T(8,128)(2,1)} copy(bf16[256,7168]{1,0:T(8,128)(2,1)} %mix.1) | data formatting | bytes 7340032
  (2 shorter events, 0.0 us)
